TPU v7x, 128 devices: a whole 4x4x4 slice. The times are simulated.
128 devices in a mesh: row: 16 (over x_hi, y, core), col: 4 (over z), dp: 2 (over x_lo).
Axes of the slice: x: 4 (x_hi: 2, x_lo: 2; x = x_hi * 2 + x_lo), y: 4, z: 4, core: 2. Of those that a mesh axis runs over, the one named last changes fastest.
Arguments:
- slides: bfloat16 [2, 256, 128, 512], P('dp', 'row', 'col'), may hold values from -6 to 6
- cotangent: bfloat16 [2, 256, 128, 512], P('dp', 'row', 'col'), may hold values from -6 to 6
- kernel: float32 [2, 7, 7, 512], replicated, may hold values from -0.875 to 0.875
- kernel_bias: float32 [2, 512], replicated, may hold values from -3 to 3
- norm_gain: float32 [2, 512], replicated, may hold values from 0.1 to 1.9
- norm_bias: float32 [2, 512], replicated, may hold values from -3 to 3
- weight_in: bfloat16 [2, 512, 2048], P(None, 'dp'), may hold values from -0.25 to 0.25
- bias_in: float32 [2, 2048], replicated, may hold values from -3 to 3
- weight_out: bfloat16 [2, 2048, 512], P(None, None, 'dp'), may hold values from -0.125 to 0.125
- bias_out: float32 [2, 512], replicated, may hold values from -3 to 3
- layer_scale: float32 [2, 512], replicated, may hold values from 0.3 to 1.5
Outputs:
- output: bfloat16 [2, 256, 128, 512], P('dp', 'row', 'col')
- grad_slides: bfloat16 [2, 256, 128, 512], P('dp', 'row', 'col')
- grad_weight_in: float32 [2, 512, 2048], P(None, 'dp')
- grad_weight_out: float32 [2, 2048, 512], P(None, None, 'dp')
- grad_kernel: float32 [2, 7, 7, 512], replicated
- grad_channel: float32 [2, 5, 512], replicated
- grad_bias_in: float32 [2, 2048], replicated
All inputs are finite; a program needn't handle non-finite values.
Results may differ from a plain program's by a relative error of at most 0.01.
Values may be sent and summed in bfloat16 or wider, within the bound.
No kernel may reach another device: no remote copies, remote signals or barrier semaphores. Data moves between devices by JAX's collectives and lax.ppermute only.
A program may use at most 128 MiB of HBM per device.

v0:
```python
import functools

import jax
import jax.numpy as jnp
from jax import lax
from jax.experimental import pallas as pl
from jax.experimental.pallas import tpu as pltpu
from jax.sharding import PartitionSpec as P

COEF = 0.7978845608028654
CUBIC = 0.044715
EPSILON = 1e-06

PIX = 512
CH = 512
FF = 2048
HALF = 1024
WIRE = FF + 128
ROWS, COLS = 16, 32
WIDE = 40
DEEP = 14
SLAB = DEEP * WIDE * 8
SPACE = ("xh", "y", "z")
F32, BF16 = jnp.float32, jnp.bfloat16

VM = pl.BlockSpec(memory_space=pltpu.VMEM)
SM = pl.BlockSpec(memory_space=pltpu.SMEM)


FAR = pl.BlockSpec(memory_space=pltpu.HBM)
DMA = pltpu.SemaphoreType.DMA


def call(body, outs, count, flops, scratch=(), scalars=0, grant=5, far=(), far_out=()):
    shapes = [
        pltpu.HBM(s, d) if n in far_out else jax.ShapeDtypeStruct(s, d)
        for n, (s, d) in enumerate(outs)
    ]
    made = pl.pallas_call(
        body,
        out_shape=shapes,
        in_specs=[
            SM if n < scalars else FAR if n in far else VM for n in range(count)
        ],
        out_specs=[FAR if n in far_out else VM for n in range(len(outs))],
        scratch_shapes=list(scratch),
        compiler_params=pltpu.CompilerParams(vmem_limit_bytes=grant * 1024 * 1024),
        cost_estimate=pl.CostEstimate(
            flops=flops, bytes_accessed=4_000_000, transcendentals=0
        ),
    )

    def run(*args):
        return made(
            *(
                pltpu.with_memory_space_constraint(arg, pltpu.HBM) if n in far else arg
                for n, arg in enumerate(args)
            )
        )

    return run


def started(source, target, sem):
    copy = pltpu.make_async_copy(source, target, sem)
    copy.start()
    return copy


def at(row, col):
    return (row * WIDE + col) * 8


def homes(row):
    found = []
    if row < DEEP:
        found.append((0, row))
    if row >= 8:
        found.append((1, row - 8))
    return found


def put_row(slab, row, line):
    for block, inner in homes(row):
        for group in range(4):
            slab[pl.ds(at(inner, 3) + block * 4 + group, COLS, stride=8), :] = line[
                :, group * 128 : (group + 1) * 128
            ]


def either(odd, a, b):
    return jnp.where(odd == 1, a, b)


def put_edges(slab, odd, near, far):
    for n in range(3):
        a = near[n * COLS : (n + 1) * COLS, :].astype(F32)
        b = far[n * COLS : (n + 1) * COLS, :].astype(F32)
        put_row(slab, n, either(odd, a, b))
        put_row(slab, 19 + n, either(odd, b, a))


def put_columns(slab, odd, near, far):
    for row in range(DEEP):
        a = near[row * 24 : (row + 1) * 24, :].astype(F32)
        b = far[row * 24 : (row + 1) * 24, :].astype(F32)
        slab[pl.ds(at(row, 0), 24), :] = either(odd, a, b)
        slab[pl.ds(at(row, 35), 24), :] = either(odd, b, a)


def give_columns(row, odd, low, high, near, far):
    near[row * 24 : (row + 1) * 24, :] = either(odd, low, high).astype(BF16)
    far[row * 24 : (row + 1) * 24, :] = either(odd, high, low).astype(BF16)


def spread(kernel, k, taps):
    for tap in range(49):
        line = kernel[tap // 7, tap % 7, k : k + 1, :]
        for part in range(8):
            group = part % 4
            taps[tap * 8 + part : tap * 8 + part + 1, :] = line[
                :, group * 128 : (group + 1) * 128
            ]


def filtered(slab, taps, store, turned):
    def step(n, carry):
        row = n // 4
        col = (n % 4) * 8
        sums = [None] * 8
        for p in range(7):
            base = pl.multiple_of(((row + p) * WIDE + col) * 8, 8)
            seen = [slab[pl.ds(base + 8 * k, 8), :] for k in range(14)]
            for q in range(7):
                tap = 48 - p * 7 - q if turned else p * 7 + q
                weight = taps[tap * 8 : tap * 8 + 8, :]
                for m in range(8):
                    term = seen[m + q] * weight
                    sums[m] = term if sums[m] is None else sums[m] + term
        base = pl.multiple_of((row * COLS + col) * 8, 8)
        for m in range(8):
            store[pl.ds(base + 8 * m, 8), :] = sums[m]
        return carry

    lax.fori_loop(0, 32, step, 0)


def line_of(store, row):
    block, inner = row // 8, row % 8
    return jnp.concatenate(
        [
            store[pl.ds(inner * COLS * 8 + block * 4 + group, COLS, stride=8), :]
            for group in range(4)
        ],
        axis=1,
    )


def strips_body(place, x, near, far):
    odd = place[0]
    near[...] = x[pl.ds(pl.multiple_of((1 - odd) * 416, 32), 96), :]
    far[...] = x[pl.ds(pl.multiple_of(odd * 416, 32), 96), :]


def pack_body(place, x, edge_near, edge_far, slab, near, far):
    for row in range(ROWS):
        put_row(slab, row + 3, x[row * COLS : (row + 1) * COLS, :].astype(F32))
    put_edges(slab, place[0], edge_near, edge_far)
    for row in range(DEEP):
        give_columns(
            row, place[3], slab[pl.ds(at(row, 3), 24), :], slab[pl.ds(at(row, 32), 24), :],
            near, far,
        )


def edge_body(place, slab, edge_near, edge_far, near, far, rim):
    put_edges(rim, place[0], edge_near, edge_far)
    upper = lax.broadcasted_iota(jnp.int32, (24, 128), 0) % 8 < 4
    for row in range(DEEP):
        found = []
        for col in (3, 32):
            value = slab[pl.ds(at(row, col), 24), :]
            if row < 3:
                value = jnp.where(upper, rim[pl.ds(at(row, col), 24), :], value)
            if row >= 11:
                value = jnp.where(upper, value, rim[pl.ds(at(row, col), 24), :])
            found.append(value)
        give_columns(row, place[3], *found, near, far)


def norm_body(
    k, place, old, near, far, kernel, bias, gain, shift, slab, normal, normed, rstd, store, taps
):
    one = slice(k, k + 1)
    spread(kernel, k, taps)
    slab[...] = old[...]
    put_columns(slab, place[3], near, far)
    filtered(slab, taps, store, False)
    for row in range(ROWS):
        a, b = row * COLS, (row + 1) * COLS
        mixed = line_of(store, row) + bias[one, :]
        center = mixed - jnp.mean(mixed, -1, keepdims=True)
        scale = lax.rsqrt(jnp.mean(center * center, -1, keepdims=True) + EPSILON)
        value = center * scale
        normed[a:b, :] = value
        rstd[a:b, :] = jnp.broadcast_to(scale, (COLS, 128))
        normal[a:b, :] = (value * gain[one, :] + shift[one, :]).astype(BF16)


def mlp_body(k, far, *refs):
    (
        place, a, normal, own_in, got_in, mate_in, own_out, got_out, mate_out,
        bias_in, bias_out, scale, out, edge_near, edge_far,
    ) = refs[:15]
    kept = refs[15:20]
    act, slope, branch, full_in, full_out = refs[20:25] if far else kept
    sems = refs[-1]
    copies = []

    def leave(which, span=slice(None)):
        if far:
            source = refs[20 + which].at[:, span] if span != slice(None) else refs[20 + which]
            target = kept[which].at[:, span] if span != slice(None) else kept[which]
            copies.append(started(source, target, sems.at[len(copies)]))

    one = slice(k, k + 1)
    core, part = place[0], place[1]
    mine = pl.multiple_of(part * 256, 256)
    theirs = pl.multiple_of((1 - part) * 256, 256)
    full_in[pl.ds(mine, 256), :] = own_in[k]
    full_in[pl.ds(pl.multiple_of(theirs + core * 128, 128), 128), :] = got_in[0]
    full_in[pl.ds(pl.multiple_of(theirs + (1 - core) * 128, 128), 128), :] = mate_in[0]
    leave(3)
    full_out[:, pl.ds(mine, 256)] = own_out[k]
    full_out[pl.ds(pl.multiple_of(core * HALF, HALF), HALF), pl.ds(theirs, 256)] = got_out[0]
    full_out[pl.ds(pl.multiple_of((1 - core) * HALF, HALF), HALF), pl.ds(theirs, 256)] = mate_out[0]
    leave(4)
    for c in range(8):
        cols = slice(c * 256, (c + 1) * 256)
        hidden = jnp.dot(normal[...], full_in[:, cols], preferred_element_type=F32)
        v = hidden + bias_in[one, cols]
        square = v * v
        tangent = jnp.tanh(v * (COEF + (COEF * CUBIC) * square))
        half = 0.5 * v
        act[:, cols] = (half + half * tangent).astype(BF16)
        slope[:, cols] = (
            0.5
            + 0.5 * tangent
            + half * (1.0 - tangent * tangent) * (COEF + (3.0 * COEF * CUBIC) * square)
        ).astype(BF16)
        if c % 2:
            leave(0, slice(c * 256 - 256, c * 256 + 256))
            leave(1, slice(c * 256 - 256, c * 256 + 256))
    for c in range(2):
        cols = slice(c * 256, (c + 1) * 256)
        value = jnp.dot(act[...], full_out[:, cols], preferred_element_type=F32)
        value = value + bias_out[one, cols]
        branch[:, cols] = value
        leave(2, cols)
        result = (a[:, cols].astype(F32) + scale[one, cols] * value).astype(BF16)
        out[:, cols] = result
        edge_near[:, cols] = either(core, result[:96, :], result[416:, :])
        edge_far[:, cols] = either(core, result[416:, :], result[:96, :])
    for copy in copies:
        copy.wait()


def back_body(
    k, place, u, branch, slope, normed, rstd, full_in, full_out, gain, scale,
    low, gh, slab, edge_near, edge_far, channel, bias, gn, rim,
):
    one = slice(k, k + 1)
    cols_last = (((1,), (1,)), ((), ()))
    up = u[...].astype(F32)
    channel[4:5, :] = jnp.sum(up * branch[...], 0, keepdims=True)
    gb = up * scale[one, :]
    channel[3:4, :] = jnp.sum(gb, 0, keepdims=True)
    low[...] = gb.astype(BF16)
    for c in range(8):
        cols = slice(c * 256, (c + 1) * 256)
        ga = lax.dot_general(
            low[...], full_out[cols, :], cols_last, preferred_element_type=F32
        )
        value = ga * slope[:, cols].astype(F32)
        bias[:, cols] = jnp.sum(value, 0, keepdims=True)
        gh[:, cols] = value.astype(BF16)
    for c in range(2):
        cols = slice(c * 256, (c + 1) * 256)
        gn[:, cols] = lax.dot_general(
            gh[...], full_in[cols, :], cols_last, preferred_element_type=F32
        )
    sums = [jnp.zeros((8, CH), F32) for _ in range(3)]

    def folded(value):
        return value[0:8] + value[8:16] + value[16:24] + value[24:32]

    for row in range(ROWS):
        a, b = row * COLS, (row + 1) * COLS
        grad = gn[a:b, :]
        value = normed[a:b, :]
        sums[1] += folded(grad * value)
        sums[2] += folded(grad)
        gs = grad * gain[one, :]
        gm = rstd[a:b, 0:1] * (
            gs
            - jnp.mean(gs, -1, keepdims=True)
            - value * jnp.mean(gs * value, -1, keepdims=True)
        )
        sums[0] += folded(gm)
        put_row(slab, row + 3, gm)
        if row < 3:
            rim[1 - place[0], a:b, :] = gm.astype(BF16)
        if row >= 13:
            rim[place[0], a - 416 : b - 416, :] = gm.astype(BF16)
    edge_near[...] = rim[0]
    edge_far[...] = rim[1]
    for n in range(3):
        channel[n : n + 1, :] = jnp.sum(sums[n], 0, keepdims=True)


def grads_body(place, normal, low, act, gh, keep, give):
    core = place[0]
    rows_first = (((0,), (0,)), ((), ()))
    for side, ref in ((1 - core, give), (core, keep)):
        for c in range(4):
            cols = pl.ds(pl.multiple_of(side * HALF + c * 256, 256), 256)
            ref[:, c * 256 : (c + 1) * 256] = lax.dot_general(
                normal[...], gh[:, cols], rows_first, preferred_element_type=F32
            ).astype(BF16)
            ref[:, HALF + c * 256 : HALF + (c + 1) * 256] = lax.dot_general(
                low[...], act[:, cols], rows_first, preferred_element_type=F32
            ).astype(BF16)


def taps_body(seen, grads, out):
    for p in range(7):

        def step(n, sums, p=p):
            row = n // 4
            col = (n % 4) * 8
            base = pl.multiple_of(((row + p) * WIDE + col) * 8, 8)
            home = pl.multiple_of(((row + 3) * WIDE + col + 3) * 8, 8)
            near = [seen[pl.ds(base + 8 * k, 8), :] for k in range(14)]
            sums = list(sums)
            for m in range(8):
                grad = grads[pl.ds(home + 8 * m, 8), :]
                for q in range(7):
                    sums[q] = sums[q] + near[m + q] * grad
            return tuple(sums)

        sums = lax.fori_loop(0, 32, step, tuple(jnp.zeros((8, 128), F32) for _ in range(7)))
        for q in range(7):
            out[(p * 7 + q) * 4 : (p * 7 + q + 1) * 4, :] = sums[q][0:4] + sums[q][4:8]


def up_body(
    k, count, place, old, edge_near, edge_far, near, far, kernel, u, *refs
):
    later, out, brought = refs[:count], refs[count], refs[count + 1 : 2 * count + 1]
    slab, store, taps, strips, edges, base, sems = refs[2 * count + 1 :]
    whole = started(old, slab, sems.at[0])
    copies = [
        started(edge_near, edges.at[0], sems.at[1]),
        started(edge_far, edges.at[1], sems.at[2]),
        started(near, strips.at[0], sems.at[3]),
        started(far, strips.at[1], sems.at[4]),
    ]
    last = started(u, base, sems.at[5])
    coming = [started(later[n], brought[n], sems.at[6 + n]) for n in range(count)]
    spread(kernel, k, taps)
    whole.wait()
    for copy in copies:
        copy.wait()
    put_edges(slab, place[0], edges.at[0], edges.at[1])
    put_columns(slab, place[3], strips.at[0], strips.at[1])
    filtered(slab, taps, store, True)
    last.wait()
    for row in range(ROWS):
        a, b = row * COLS, (row + 1) * COLS
        out[a:b, :] = (base[a:b, :].astype(F32) + line_of(store, row)).astype(out.dtype)
    for copy in coming:
        copy.wait()


def pair_body(keep, got, taps, channel, bias, far, out, lines, sems):
    lines[0:196, :] = taps[...]
    spot = 196
    for kind in range(5):
        for group in range(4):
            lines[spot : spot + 1, :] = channel[
                kind : kind + 1, group * 128 : (group + 1) * 128
            ]
            spot += 1
    for group in range(16):
        lines[spot : spot + 1, :] = bias[:, group * 128 : (group + 1) * 128]
        spot += 1
    lines[spot:256, :] = jnp.zeros((256 - spot, 128), F32)

    def step(n, carry):
        rows = pl.ds(pl.multiple_of(n * 32, 32), 32)
        total = keep[rows, :].astype(F32) + got[rows, :].astype(F32)
        out[pl.ds(n * 4, 4), :, :FF] = total.reshape(4, 8, FF).astype(BF16)
        rows = pl.ds(pl.multiple_of((n % 8) * 32, 32), 32)
        out[pl.ds(n * 4, 4), :, FF:] = lines[rows, :].reshape(4, 8, 128).astype(BF16)
        return carry

    copies = []
    for part in range(4):
        lax.fori_loop(part * 4, part * 4 + 4, step, 0)
        span = pl.ds(part * 16, 16)
        copies.append(started(out.at[span], far.at[span], sems.at[part]))
    for copy in copies:
        copy.wait()


def total_body(pieces, out):
    for a, b in ((0, 512), (512, 1024), (1024, 1536), (1536, WIRE)):

        def step(n, total, a=a, b=b):
            for m in range(4):
                total = total + pieces[n * 4 + m, :, a:b].astype(F32)
            return total

        total = lax.fori_loop(0, 16, step, jnp.zeros((8, b - a), F32))
        out[:, a:b] = total.astype(BF16)


def merge_body(other, pieces, far, out, sums, sems):
    total_body(pieces, sums)
    copies = []
    for part in range(4):
        for n in range(part * 8, part * 8 + 8):
            out[n, :, :WIRE] = sums[...]
            out[n, :, WIRE:] = other[...]
        span = pl.ds(part * 8, 8)
        copies.append(started(out.at[span], far.at[span], sems.at[part]))
    for copy in copies:
        copy.wait()


def small_body(whole0, whole1, mate0, mate1, taps, channel, bias, lines):
    for k, whole, mate in ((0, whole0, mate0), (1, whole1, mate1)):
        lines[0:256, :] = (whole[...].astype(F32) + mate[...].astype(F32)).reshape(256, 128)
        for group in range(4):
            cols = slice(group * 128, (group + 1) * 128)
            for tap in range(49):
                line = tap * 4 + group
                taps[tap // 7, tap % 7, k : k + 1, cols] = lines[line : line + 1, :]
            for kind in range(5):
                line = 196 + kind * 4 + group
                channel[kind, k : k + 1, cols] = lines[line : line + 1, :]
        for group in range(16):
            bias[k : k + 1, group * 128 : (group + 1) * 128] = lines[216 + group : 217 + group, :]


def finish_body(place, ref, *refs):
    grad_in, grad_out = refs[-2:]
    value = ref[:, :, :FF].astype(F32).reshape(128, FF)
    grad_in[0] = value[:, :HALF]
    grad_out[0] = value[:, HALF:].T


STORE = pltpu.VMEM((ROWS * COLS * 4 + 16, 128), F32)
TAPS = pltpu.VMEM((400, 128), F32)
STRIP = ((DEEP * 24, 128), BF16)
EDGE = ((96, CH), BF16)


def edge_strips(place, x):
    return call(strips_body, [EDGE, EDGE], 2, 1_000_000, scalars=1)(place, x)


def pack(place, x, near, far):
    outs = [((SLAB, 128), F32), STRIP, STRIP]
    return call(pack_body, outs, 4, 10_000_000, scalars=1)(place, x, near, far)


def pack_edges(place, slab, near, far):
    scratch = [pltpu.VMEM((SLAB, 128), F32)]
    return call(edge_body, [STRIP, STRIP], 4, 10_000_000, scratch, scalars=1)(
        place, slab, near, far
    )


def normalise(k, place, slab, near, far, kernel, bias, gain, shift):
    outs = [((SLAB, 128), F32), ((PIX, CH), BF16), ((PIX, CH), F32), ((PIX, 128), F32)]
    return call(
        functools.partial(norm_body, k), outs, 8, 40_000_000, [STORE, TAPS], scalars=1
    )(place, slab, near, far, kernel, bias, gain, shift)


def mlp(k, place, a, normal, weights, bias_in, bias_out, scale):
    kept = [
        ((PIX, FF), BF16), ((PIX, FF), BF16), ((PIX, CH), F32), ((CH, FF), BF16), ((FF, CH), BF16),
    ]
    outs = [((PIX, CH), BF16), EDGE, EDGE, *kept]
    far = k == 0
    scratch = [*(pltpu.VMEM(s, d) for s, d in kept), DMA((12,))] if far else [DMA((1,))]
    return call(
        functools.partial(mlp_body, k, far), outs, 12, 60_000_000, scratch, scalars=1,
        grant=14 if far else 5, far_out=range(3, 8) if far else (),
    )(place, a, normal, *weights, bias_in, bias_out, scale)


def backward(k, place, u, saved, gain, scale):
    outs = [
        ((PIX, CH), BF16), ((PIX, FF), BF16), ((SLAB, 128), F32), EDGE, EDGE,
        ((8, CH), F32), ((1, FF), F32),
    ]
    scratch = [pltpu.VMEM((PIX, CH), F32), pltpu.VMEM((2, *EDGE[0]), BF16)]
    return call(
        functools.partial(back_body, k), outs, 10, 60_000_000, scratch, scalars=1
    )(place, u, *saved, gain, scale)


def weight_grads(place, normal, low, act, gh):
    outs = [((CH, FF), BF16), ((CH, FF), BF16)]
    return call(grads_body, outs, 5, 50_000_000, scalars=1)(place, normal, low, act, gh)


def tap_grads(seen, grads):
    return call(taps_body, [((49 * 4, 128), F32)], 2, 40_000_000)(seen, grads)[0]


def upstream(k, place, slab, edge_near, edge_far, near, far, kernel, u, dtype, later=()):
    scratch = [
        pltpu.VMEM((SLAB, 128), F32), STORE, TAPS,
        pltpu.VMEM((2, *STRIP[0]), BF16), pltpu.VMEM((2, *EDGE[0]), BF16),
        pltpu.VMEM((PIX, CH), u.dtype), DMA((6 + len(later),)),
    ]
    outs = [((PIX, CH), dtype), *((x.shape, x.dtype) for x in later)]
    return call(
        functools.partial(up_body, k, len(later)), outs, 8 + len(later), 40_000_000, scratch,
        grant=8, far=(1, 2, 3, 4, 5, 7, *range(8, 8 + len(later))), scalars=1,
    )(place, slab, edge_near, edge_far, near, far, kernel, u, *later)


def finish(place, side, value, buffers):
    held = [pl.BlockSpec(memory_space=pl.ANY)] * len(buffers)
    return pl.pallas_call(
        finish_body,
        grid_spec=pltpu.PrefetchScalarGridSpec(
            num_scalar_prefetch=1,
            grid=(2, 2),
            in_specs=[pl.BlockSpec((16, 8, WIRE), lambda layer, i, s: (i, 0, layer)), *held],
            out_specs=[
                pl.BlockSpec((1, 128, HALF), lambda layer, i, s: (layer, i, s[side])),
                pl.BlockSpec((1, HALF, 128), lambda layer, i, s: (layer, s[side], i)),
            ],
        ),
        out_shape=[
            jax.ShapeDtypeStruct((2, 256, FF), F32),
            jax.ShapeDtypeStruct((2, FF, 256), F32),
        ],
        input_output_aliases={2: 0, 3: 1} if buffers else {},
        compiler_params=pltpu.CompilerParams(vmem_limit_bytes=10 * 1024 * 1024),
        cost_estimate=pl.CostEstimate(
            flops=5_000_000, bytes_accessed=6_000_000, transcendentals=0
        ),
    )(place, value, *buffers)


def finish_small(whole, mate):
    first = pl.BlockSpec((32, 8, 128), lambda i: (0, 0, FF // 128))
    second = pl.BlockSpec((32, 8, 128), lambda i: (0, 0, (WIRE + FF) // 128))
    shapes = [(7, 7, 2, CH), (5, 2, CH), (2, FF)]
    return pl.pallas_call(
        small_body,
        grid=(1,),
        out_shape=[jax.ShapeDtypeStruct(s, F32) for s in shapes],
        in_specs=[first, second, first, second],
        out_specs=[
            pl.BlockSpec((7, 7, 2, CH), lambda i: (0, 0, 0, 0)),
            pl.BlockSpec((5, 2, CH), lambda i: (0, 0, 0)),
            pl.BlockSpec((2, FF), lambda i: (0, 0)),
        ],
        scratch_shapes=[pltpu.VMEM((256 + 8, 128), F32)],
        compiler_params=pltpu.CompilerParams(vmem_limit_bytes=4 * 1024 * 1024),
        cost_estimate=pl.CostEstimate(
            flops=1_000_000, bytes_accessed=1_000_000, transcendentals=0
        ),
    )(whole, whole, mate, mate)


RANKS = ("xh", "y", "core")


def pairs(first, count):
    found = [(i, i + 1) for i in range(first, count - 1, 2)]
    return found + [(b, a) for a, b in found]


def from_rows(near, far):
    near = lax.ppermute(near, RANKS, pairs(0, 16))
    far = lax.ppermute(far, RANKS, pairs(1, 16))
    return near, far


def from_columns(near, far):
    near = lax.ppermute(near, "z", pairs(0, 4))
    far = lax.ppermute(far, "z", pairs(1, 4))
    return near, far


def swapped(value, axis):
    return lax.ppermute(value, axis, [(0, 1), (1, 0)])


def around_x(value, step):
    return lax.ppermute(value, ("xh", "dp"), [(i, (i + step) % 4) for i in range(4)])


def fetch_weights(core, weight_in, weight_out, k):
    half_in = lax.dynamic_slice(weight_in, (k, core * 128, 0), (1, 128, FF))
    half_out = lax.dynamic_slice(weight_out, (k, core * HALF, 0), (1, HALF, 256))
    got_in = around_x(half_in, 1)
    got_out = around_x(half_out, -1)
    mate_in = swapped(got_in, "core")
    mate_out = swapped(got_out, "core")
    return weight_in, got_in, mate_in, weight_out, got_out, mate_out


def send_grads(keep, got, taps, channel, bias):
    scratch = [pltpu.VMEM((64, 8, WIRE), BF16), pltpu.VMEM((256, 128), F32), DMA((4,))]
    pair = call(
        pair_body, [((64, 8, WIRE), BF16)], 5, 2_000_000, scratch, far_out=(0,)
    )(keep, got, taps, channel, bias)[0]
    return lax.all_to_all(pair, ("dp", *SPACE), 0, 0, tiled=True)


def per_device(
    slides,
    cotangent,
    kernel,
    kernel_bias,
    norm_gain,
    norm_bias,
    weight_in,
    bias_in,
    weight_out,
    bias_out,
    layer_scale,
):
    core, part = lax.axis_index("core"), lax.axis_index("dp")
    place = jnp.stack([core, part, 1 - core, lax.axis_index("z") % 2]).astype(jnp.int32)
    slides, place = lax.optimization_barrier((slides, place))
    kernel = jnp.transpose(kernel, (1, 2, 0, 3))
    current = slides.reshape(PIX, CH)
    edges = edge_strips(place, current)
    saved = []
    weights = [fetch_weights(core, weight_in, weight_out, k) for k in range(2)]
    for k in range(2):
        edges = from_rows(*edges)
        slab, *sides = pack(place, current, *edges)
        sides = from_columns(*sides)
        slab, normal, normed, rstd = normalise(
            k, place, slab, *sides, kernel, kernel_bias, norm_gain, norm_bias
        )
        current, *edges, act, slope, branch, full_in, full_out = mlp(
            k, place, current, normal, weights[k], bias_in, bias_out, layer_scale
        )
        saved.append((slab, act, normal, (branch, slope, normed, rstd, full_in, full_out)))
    up = cotangent.reshape(PIX, CH)
    pieces = [None] * 2
    for k in (1, 0):
        seen, act, normal, rest = saved[k]
        low, gh, grads, *edges, channel, bias = backward(k, place, up, rest, norm_gain, layer_scale)
        edges = from_rows(*edges)
        keep, give = weight_grads(place, normal, low, act, gh)
        got = swapped(give, "core")
        taps = tap_grads(seen, grads)
        pieces[k] = send_grads(keep, got, taps, channel, bias)
        sides = pack_edges(place, grads, *edges)
        sides = from_columns(*sides)
        later = saved[0][3] if k else ()
        up, *brought = upstream(
            k, place, grads, *edges, *sides, kernel, up, F32 if k else BF16, later
        )
        if k:
            saved[0] = (*saved[0][:3], brought)
    other = call(total_body, [((8, WIRE), BF16)], 1, 5_000_000)(pieces[1])[0]
    scratch = [
        pltpu.VMEM((32, 8, 2 * WIRE), BF16), pltpu.VMEM((8, WIRE), BF16), DMA((4,)),
    ]
    copies = call(
        merge_body, [((32, 8, 2 * WIRE), BF16)], 2, 5_000_000, scratch, grant=8, far_out=(0,)
    )(other, pieces[0])[0]
    whole = lax.all_to_all(copies, SPACE, 0, 0, tiled=True)
    mate = swapped(whole, "core")
    buffers = finish(place, 0, whole, ())
    grad_in, grad_out = finish(place, 2, mate, buffers)
    grad_taps, grad_channel, grad_bias = finish_small(whole, mate)
    return (
        current.reshape(slides.shape),
        up.reshape(slides.shape),
        grad_in,
        grad_out,
        jnp.transpose(grad_taps, (2, 0, 1, 3)),
        jnp.transpose(grad_channel, (1, 0, 2)),
        grad_bias,
    )


def solution(mesh):
    fine = jax.sharding.Mesh(
        mesh.devices.reshape(2, 4, 2, 4, 2), ("xh", "y", "core", "z", "dp")
    )
    maps = P("dp", RANKS, "z", None)
    split_in, split_out = P(None, "dp", None), P(None, None, "dp")
    whole = P()
    return jax.shard_map(
        per_device,
        mesh=fine,
        in_specs=(
            maps, maps, whole, whole, whole, whole, split_in, whole, split_out, whole, whole,
        ),
        out_specs=(maps, maps, split_in, split_out, whole, whole, whole),
        check_vma=False,
    )
```

profile of v0, /device:TPU:1, one launch (start us, length us, event | category | flops | bytes accessed | tf_op | source)
XLA Modules:
  0.0 273.9 jit_solution(9373745451670782112)
XLA Ops:
  0.7 2.4 constant_dynamic-slice_fusion.1
  3.1 2.0 collective-permute-start.4
  7.5 2.5 collective-permute-start.14
  10.0 7.9 %collective-permute-done.4.refs_4_ = bf16[1,128,2048]{2,1,0:T(8,128)(2,1)S(1)} collective-permute-done((bf16[1,128,2048]{2,1,0:T(8,128)(2,1)}, bf16[1,128,2048]{2,1,0:T(8,128)(2,1)S(1)}, u32[]{:S(2)}, u32[]{:S(2)}) %collective-permute-start.4) | collective-permute-done | bytes 524320 | tf_op jit(solution)/shard_map/ppermute | solution.py:610
  17.9 2.8 %collective-permute-start.5 = (bf16[1,128,2048]{2,1,0:T(8,128)(2,1)S(1)}, bf16[1,128,2048]{2,1,0:T(8,128)(2,1)}, u32[]{:S(2)}, u32[]{:S(2)}) collective-permute-start(bf16[1,128,2048]{2,1,0:T(8,128)(2,1)S(1)} %collective-permute-done.4.refs_4_), channel_id=1, source_target_pairs={{0,8},{8,0},{1,9},{9,1},{2,10},{10,2},{3,11},{11,3},{4,12},{12,4},... | collective-permute-start | bytes 1572872 | tf_op jit(solution)/shard_map/ppermute | solution.py:606
  22.6 6.6 %collective-permute-done.12.refs_4_ = bf16[1,128,2048]{2,1,0:T(8,128)(2,1)} collective-permute-done((bf16[1,128,2048]{2,1,0:T(8,128)(2,1)}, bf16[1,128,2048]{2,1,0:T(8,128)(2,1)}, u32[]{:S(2)}, u32[]{:S(2)}) %collective-permute-start.12) | collective-permute-done | bytes 524320 | tf_op jit(solution)/shard_map/ppermute | solution.py:610
  29.2 1.6 collective-permute-start.13
  31.7 3.1 %collective-permute-start.1 = (bf16[96,512]{1,0:T(8,128)(2,1)S(1)}, bf16[96,512]{1,0:T(8,128)(2,1)S(1)}, u32[]{:S(2)}, u32[]{:S(2)}) collective-permute-start(bf16[96,512]{1,0:T(8,128)(2,1)S(1)} %get-tuple-element.78), channel_id=1, source_target_pairs={{8,16},{24,32},{40,48},{56,64},{72,80},{88,96},{104,112},{16,8},{3... | collective-permute-start | bytes 294920 | tf_op jit(solution)/shard_map/ppermute | solution.py:595
  34.8 2.8 %collective-permute-done.1.edge_far = bf16[96,512]{1,0:T(8,128)(2,1)S(1)} collective-permute-done((bf16[96,512]{1,0:T(8,128)(2,1)S(1)}, bf16[96,512]{1,0:T(8,128)(2,1)S(1)}, u32[]{:S(2)}, u32[]{:S(2)}) %collective-permute-start.1) | collective-permute-done | bytes 98336 | tf_op jit(solution)/shard_map/ppermute | solution.py:595
  38.4 1.7 collective-permute-start.2
  40.1 1.9 collective-permute-done.2.near
  44.1 6.2 %shard_map.164 = (f32[4480,128]{1,0:T(8,128)S(1)}, bf16[512,512]{1,0:T(8,128)(2,1)S(1)}, f32[512,512]{1,0:T(8,128)S(1)}, f32[512,128]{1,0:T(8,128)S(1)}) custom-call(s32[4]{0:T(128)S(1)} %pad_add_fusion.place.refs_0_, f32[4480,128]{1,0:T(8,128)S(1)} %get-tuple-element.79.old, bf16[336,128]{1,0:T(8,128)(2,1)S(1)} %collective-permute-done.2.near, ...), custom_call_target="tpu_custom_call" | custom-call | flops 40000000 | bytes 4000000 | tf_op jit(solution)/shard_map/pallas_call | solution.py:54
  50.4 1.4 copy-done.9
  53.5 1.6 copy-done.4
  57.5 7.3 %shard_map.165 = (bf16[512,512]{1,0:T(8,128)(2,1)S(1)}, bf16[96,512]{1,0:T(8,128)(2,1)S(1)}, bf16[96,512]{1,0:T(8,128)(2,1)S(1)}, bf16[512,2048]{1,0:T(8,128)(2,...) custom-call(s32[4]{0:T(128)S(1)} %pad_add_fusion.place.refs_0_, ...), custom_call_target="tpu_custom_call" | custom-call | flops 60000000 | bytes 4000000 | tf_op jit(solution)/shard_map/pallas_call | solution.py:54
  65.6 4.8 %collective-permute-start.9 = (bf16[96,512]{1,0:T(8,128)(2,1)S(1)}, bf16[96,512]{1,0:T(8,128)(2,1)S(1)}, u32[]{:S(2)}, u32[]{:S(2)}) collective-permute-start(bf16[96,512]{1,0:T(8,128)(2,1)S(1)} %get-tuple-element.85), channel_id=1, source_target_pairs={{8,16},{24,32},{40,48},{56,64},{72,80},{88,96},{104,112},{16,8},{3... | collective-permute-start | bytes 294920 | tf_op jit(solution)/shard_map/ppermute | solution.py:595
  70.4 2.3 collective-permute-done.9.edge_far
  73.5 7.5 %collective-permute-start.10 = (bf16[336,128]{1,0:T(8,128)(2,1)S(1)}, bf16[336,128]{1,0:T(8,128)(2,1)S(1)}, u32[]{:S(2)}, u32[]{:S(2)}) collective-permute-start(bf16[336,128]{1,0:T(8,128)(2,1)S(1)} %get-tuple-element.87), channel_id=1, source_target_pairs={{0,2},{4,6},{2,0},{6,4},{1,3},{5,7},{3,1},{7,5},{8,10},{12,14},{10... | collective-permute-start | bytes 258056 | tf_op jit(solution)/shard_map/ppermute | solution.py:600
  82.9 5.6 %shard_map.167 = (f32[4480,128]{1,0:T(8,128)S(1)}, bf16[512,512]{1,0:T(8,128)(2,1)S(1)}, f32[512,512]{1,0:T(8,128)S(1)}, f32[512,128]{1,0:T(8,128)S(1)}) custom-call(s32[4]{0:T(128)S(1)} %pad_add_fusion.place.refs_0_, f32[4480,128]{1,0:T(8,128)S(1)} %get-tuple-element.86.old, bf16[336,128]{1,0:T(8,128)(2,1)S(1)} %collective-permute-done.10.near, ...), custom_call_target="tpu_custom_call" | custom-call | flops 40000000 | bytes 4000000 | tf_op jit(solution)/shard_map/pallas_call | solution.py:54
  88.6 6.9 %shard_map.168 = (bf16[512,512]{1,0:T(8,128)(2,1)}, bf16[96,512]{1,0:T(8,128)(2,1)}, bf16[96,512]{1,0:T(8,128)(2,1)}, bf16[512,2048]{1,0:T(8,128)(2,1)S(1)}, bf1...) custom-call(s32[4]{0:T(128)S(1)} %pad_add_fusion.place.refs_0_, ...), custom_call_target="tpu_custom_call" | custom-call | flops 60000000 | bytes 4000000 | tf_op jit(solution)/shard_map/pallas_call | solution.py:54
  95.5 3.5 %shard_map.169 = (bf16[512,512]{1,0:T(8,128)(2,1)S(1)}, bf16[512,2048]{1,0:T(8,128)(2,1)S(1)}, f32[4480,128]{1,0:T(8,128)S(1)}, bf16[96,512]{1,0:T(8,128)(2,1)S(...) custom-call(s32[4]{0:T(128)S(1)} %pad_add_fusion.place.refs_0_, ...), custom_call_target="tpu_custom_call" | custom-call | flops 60000000 | bytes 4000000 | tf_op jit(solution)/shard_map/pallas_call | solution.py:54
  99.0 3.1 %shard_map.175 = (bf16[512,2048]{1,0:T(8,128)(2,1)S(1)}, bf16[512,2048]{1,0:T(8,128)(2,1)S(1)}) custom-call(s32[4]{0:T(128)S(1)} %pad_add_fusion.place.refs_0_, bf16[512,512]{1,0:T(8,128)(2,1)S(1)} %get-tuple-element.89.refs_2_.normal, bf16[512,512]{1,0:T(8,128)(2,1)S(1)} %get-tuple-element.120.low, bf16[512,2048]{1,0:T(8,128)(2,1)S(1)} %get-tuple-element.121.act, ...), custom_call_target="tpu_custom_call" | custom-call | flops 50000000 | bytes 4000000 | tf_op jit(solution)/shard_map/pallas_call | solution.py:54
  102.7 4.8 %collective-permute-start.17 = (bf16[96,512]{1,0:T(8,128)(2,1)S(1)}, bf16[96,512]{1,0:T(8,128)(2,1)S(1)}, u32[]{:S(2)}, u32[]{:S(2)}) collective-permute-start(bf16[96,512]{1,0:T(8,128)(2,1)S(1)} %get-tuple-element.99), channel_id=1, source_target_pairs={{8,16},{24,32},{40,48},{56,64},{72,80},{88,96},{104,112},{16,8},{3... | collective-permute-start | bytes 294920 | tf_op jit(solution)/shard_map/ppermute | solution.py:595
  107.5 2.3 collective-permute-done.17.edge_far
  110.4 3.6 %collective-permute-start.18 = (bf16[336,128]{1,0:T(8,128)(2,1)S(1)}, bf16[336,128]{1,0:T(8,128)(2,1)S(1)}, u32[]{:S(2)}, u32[]{:S(2)}) collective-permute-start(bf16[336,128]{1,0:T(8,128)(2,1)S(1)} %get-tuple-element.100), channel_id=1, source_target_pairs={{0,2},{4,6},{2,0},{6,4},{1,3},{5,7},{3,1},{7,5},{8,10},{12,14},{10... | collective-permute-start | bytes 258056 | tf_op jit(solution)/shard_map/ppermute | solution.py:600
  114.7 6.0 %shard_map.176.taps = f32[196,128]{1,0:T(8,128)S(1)} custom-call(f32[4480,128]{1,0:T(8,128)S(1)} %get-tuple-element.125.seen, f32[4480,128]{1,0:T(8,128)S(1)} %get-tuple-element.97.slab.old.grads), custom_call_target="tpu_custom_call" | custom-call | flops 40000000 | bytes 4000000 | tf_op jit(solution)/shard_map/pallas_call | solution.py:54
  120.8 1.6 shard_map.177
  122.3 16.1 %all-to-all-start = ((bf16[64,8,2176]{2,1,0:T(8,128)(2,1)}), bf16[64,8,2176]{2,1,0:T(8,128)(2,1)}, u32[]{:S(2)}, u32[]{:S(2)}) async-start(bf16[64,8,2176]{2,1,0:T(8,128)(2,1)} %shard_map.177), calls=%async_computation | async-start | bytes 4456448 | tf_op jit(solution)/shard_map/all_to_all | solution.py:628
  139.2 7.0 %shard_map.171 = (f32[512,512]{1,0:T(8,128)S(1)}, f32[512,512]{1,0:T(8,128)S(1)}, bf16[512,2048]{1,0:T(8,128)(2,1)S(1)}, f32[512,512]{1,0:T(8,128)S(1)}, f32[512...) custom-call(s32[4]{0:T(128)S(1)} %pad_add_fusion.place.refs_0_, ...), custom_call_target="tpu_custom_call" | custom-call | flops 40000000 | bytes 4000000 | tf_op jit(solution)/shard_map/pallas_call | solution.py:54
  146.3 3.4 %shard_map.172 = (bf16[512,512]{1,0:T(8,128)(2,1)S(1)}, bf16[512,2048]{1,0:T(8,128)(2,1)S(1)}, f32[4480,128]{1,0:T(8,128)S(1)}, bf16[96,512]{1,0:T(8,128)(2,1)S(...) custom-call(s32[4]{0:T(128)S(1)} %pad_add_fusion.place.refs_0_, ...), custom_call_target="tpu_custom_call" | custom-call | flops 60000000 | bytes 4000000 | tf_op jit(solution)/shard_map/pallas_call | solution.py:54
  149.7 3.1 %shard_map.179 = (bf16[512,2048]{1,0:T(8,128)(2,1)S(1)}, bf16[512,2048]{1,0:T(8,128)(2,1)S(1)}) custom-call(s32[4]{0:T(128)S(1)} %pad_add_fusion.place.refs_0_, bf16[512,512]{1,0:T(8,128)(2,1)S(1)} %copy-done.13, bf16[512,512]{1,0:T(8,128)(2,1)S(1)} %get-tuple-element.128.low, bf16[512,2048]{1,0:T(8,128)(2,1)S(1)} %copy-done.11, ...), custom_call_target="tpu_custom_call" | custom-call | flops 50000000 | bytes 4000000 | tf_op jit(solution)/shard_map/pallas_call | solution.py:54
  152.8 2.9 %collective-permute-start.25 = (bf16[512,2048]{1,0:T(8,128)(2,1)S(1)}, bf16[512,2048]{1,0:T(8,128)(2,1)S(1)}, u32[]{:S(2)}, u32[]{:S(2)}) collective-permute-start(bf16[512,2048]{1,0:T(8,128)(2,1)S(1)} %get-tuple-element.132), channel_id=1, source_target_pairs={{0,8},{8,0},{1,9},{9,1},{2,10},{10,2},{3,11},{11,3},{4,12},{12,4},... | collective-permute-start | bytes 6291464 | tf_op jit(solution)/shard_map/ppermute | solution.py:606
  155.8 6.0 %shard_map.180.taps = f32[196,128]{1,0:T(8,128)S(1)} custom-call(f32[4480,128]{1,0:T(8,128)S(1)} %copy-done.10, f32[4480,128]{1,0:T(8,128)S(1)} %get-tuple-element.115.slab.old.grads), custom_call_target="tpu_custom_call" | custom-call | flops 40000000 | bytes 4000000 | tf_op jit(solution)/shard_map/pallas_call | solution.py:54
  161.8 1.5 shard_map.181
  163.4 1.7 all-to-all-done.pieces
  165.1 10.5 %all-to-all-start.1 = ((bf16[64,8,2176]{2,1,0:T(8,128)(2,1)}), bf16[64,8,2176]{2,1,0:T(8,128)(2,1)}, u32[]{:S(2)}, u32[]{:S(2)}) async-start(bf16[64,8,2176]{2,1,0:T(8,128)(2,1)} %shard_map.181), calls=%async_computation.1 | async-start | bytes 4456448 | tf_op jit(solution)/shard_map/all_to_all | solution.py:628
  175.6 2.2 shard_map.178.other
  177.8 26.4 %all-to-all-done.1.pieces = bf16[64,8,2176]{2,1,0:T(8,128)(2,1)} async-done(((bf16[64,8,2176]{2,1,0:T(8,128)(2,1)}), bf16[64,8,2176]{2,1,0:T(8,128)(2,1)}, u32[]{:S(2)}, u32[]{:S(2)}) %all-to-all-start.1) | async-done | bytes 2228256 | tf_op jit(solution)/shard_map/all_to_all | solution.py:628
  204.2 3.6 %shard_map.182 = bf16[32,8,4352]{2,1,0:T(8,128)(2,1)} custom-call(bf16[8,2176]{1,0:T(8,128)(2,1)S(1)} %shard_map.178.other, bf16[64,8,2176]{2,1,0:T(8,128)(2,1)} %all-to-all-done.1.pieces), custom_call_target="tpu_custom_call" | custom-call | flops 5000000 | bytes 4000000 | tf_op jit(solution)/shard_map/pallas_call | solution.py:54
  207.8 37.1 %all_to_all.15.ref.whole0.whole1 = bf16[32,8,4352]{2,1,0:T(8,128)(2,1)S(1)} all-to-all(bf16[32,8,4352]{2,1,0:T(8,128)(2,1)} %shard_map.182), channel_id=1, replica_groups=mesh['xh'=2,'y'=4,'core'=2,'z'=4,'dp'=2] {'xh','y','z'}, dimensions={0} | all-to-all | bytes 4456448 | tf_op jit(solution)/shard_map/all_to_all | solution.py:688
  244.9 2.6 collective-permute-start.26
  247.5 2.6 collective-permute-start.21
  250.1 1.5 collective-permute-done.20.edge_near
  251.6 1.8 collective-permute-done.21.edge_far
  255.0 2.5 collective-permute-done.22.near
  258.8 7.8 %shard_map.174 = bf16[512,512]{1,0:T(8,128)(2,1)} custom-call(s32[4]{0:T(128)S(1)} %pad_add_fusion.place.refs_0_, f32[4480,128]{1,0:T(8,128)} %copy-done.1, bf16[96,512]{1,0:T(8,128)(2,1)} %copy-done.20, bf16[96,512]{1,0:T(8,128)(2,1)} %copy-done.21, bf16[336,128]{1,0:T(8,128)(2,1)} %copy-done.39, bf16[336,128]{1,0:T(8,128)(2,1)} %copy-done.40, ...), custom_call_target="tpu_custom_call" | custom-call | flops 40000000 | bytes 4000000 | tf_op jit(solution)/shard_map/pallas_call | solution.py:54
  266.5 3.2 %shard_map.183 = (f32[2,256,2048]{2,1,0:T(8,128)}, f32[2,2048,256]{2,1,0:T(8,128)}) custom-call(s32[4]{0:T(128)S(1)} %pad_add_fusion.place.refs_0_, bf16[32,8,4352]{2,1,0:T(8,128)(2,1)S(1)} %all_to_all.15.ref.whole0.whole1), custom_call_target="tpu_custom_call" | custom-call | flops 5000000 | bytes 6000000 | tf_op jit(solution)/shard_map/pallas_call | solution.py:540
  270.6 3.2 %shard_map.184 = (f32[2,256,2048]{2,1,0:T(8,128)}, f32[2,2048,256]{2,1,0:T(8,128)}) custom-call(s32[4]{0:T(128)S(1)} %pad_add_fusion.place.refs_0_, bf16[32,8,4352]{2,1,0:T(8,128)(2,1)S(1)} %collective-permute-done.26.ref.mate0.mate1, f32[2,256,2048]{2,1,0:T(8,128)} %get-tuple-element.136.refs_0_, ...), custom_call_target="tpu_custom_call", output_to_operand_aliasing={{0}: (2, {}), {1}: (3, {})} | custom-call | flops 5000000 | bytes 6000000 | tf_op jit(solution)/shard_map/pallas_call | solution.py:540
  (120 shorter events, 21.8 us)
Async XLA Ops:
  0.6 21.3 %copy-start.6 = (bf16[1,16,32,512]{3,2,1,0:T(8,128)(2,1)S(1)}, bf16[1,16,32,512]{3,2,1,0:T(8,128)(2,1)}, u32[]{:S(2)}) copy-start(bf16[1,16,32,512]{3,2,1,0:T(8,128)(2,1)} %param.11) | copy-start | bytes 1572868
  3.1 39.6 %copy-start.8 = (f32[2,7,7,512]{3,0,2,1:T(2,128)S(1)}, f32[2,7,7,512]{3,0,2,1:T(2,128)}, u32[]{:S(2)}) copy-start(f32[2,7,7,512]{3,0,2,1:T(2,128)} %param.13) | copy-start | bytes 602116
  3.1 39.6 %copy-start.25 = (f32[2,512]{1,0:T(2,128)S(1)}, f32[2,512]{1,0:T(2,128)}, u32[]{:S(2)}) copy-start(f32[2,512]{1,0:T(2,128)} %gain.7) | copy-start | bytes 12292
  3.1 14.8 %collective-permute-start.4 = (bf16[1,128,2048]{2,1,0:T(8,128)(2,1)}, bf16[1,128,2048]{2,1,0:T(8,128)(2,1)S(1)}, u32[]{:S(2)}, u32[]{:S(2)}) collective-permute-start(bf16[1,128,2048]{2,1,0:T(8,128)(2,1)} %get-tuple-element.146), channel_id=1, source_target_pairs={{0,1},{1,64},{64,65},{65,0},{2,3},{3,66},{66,67},{67,2},{4,5},{5,6... | collective-permute-start | bytes 1572872 | tf_op jit(solution)/shard_map/ppermute | solution.py:610
  6.0 47.4 %copy-start.2 = (bf16[2,256,2048]{2,1,0:T(8,128)(2,1)S(1)}, bf16[2,256,2048]{2,1,0:T(8,128)(2,1)}, u32[]{:S(2)}) copy-start(bf16[2,256,2048]{2,1,0:T(8,128)(2,1)} %refs_3_.3) | copy-start | bytes 6291460
  6.0 47.5 %copy-start.26 = (f32[2,512]{1,0:T(2,128)S(1)}, f32[2,512]{1,0:T(2,128)}, u32[]{:S(2)}) copy-start(f32[2,512]{1,0:T(2,128)} %scale.3) | copy-start | bytes 12292
  6.0 14.7 %collective-permute-start.6 = (bf16[1,1024,256]{2,1,0:T(8,128)(2,1)S(1)}, bf16[1,1024,256]{2,1,0:T(8,128)(2,1)}, u32[]{:S(2)}, u32[]{:S(2)}) collective-permute-start(bf16[1,1024,256]{2,1,0:T(8,128)(2,1)S(1)} %get-tuple-element.144), channel_id=1, source_target_pairs={{0,65},{1,0},{64,1},{65,64},{2,67},{3,2},{66,3},{67,66},{4,69},{5,... | collective-permute-start | bytes 1572872 | tf_op jit(solution)/shard_map/ppermute | solution.py:610
  7.3 21.9 %collective-permute-start.12 = (bf16[1,128,2048]{2,1,0:T(8,128)(2,1)}, bf16[1,128,2048]{2,1,0:T(8,128)(2,1)}, u32[]{:S(2)}, u32[]{:S(2)}) collective-permute-start(bf16[1,128,2048]{2,1,0:T(8,128)(2,1)} %get-tuple-element.145), channel_id=1, source_target_pairs={{0,1},{1,64},{64,65},{65,0},{2,3},{3,66},{66,67},{67,2},{4,5},{5,6... | collective-permute-start | bytes 1572872 | tf_op jit(solution)/shard_map/ppermute | solution.py:610
  7.5 23.4 %collective-permute-start.14 = (bf16[1,1024,256]{2,1,0:T(8,128)(2,1)}, bf16[1,1024,256]{2,1,0:T(8,128)(2,1)}, u32[]{:S(2)}, u32[]{:S(2)}) collective-permute-start(bf16[1,1024,256]{2,1,0:T(8,128)(2,1)} %get-tuple-element.143), channel_id=1, source_target_pairs={{0,65},{1,0},{64,1},{65,64},{2,67},{3,2},{66,3},{67,66},{4,69},{5,... | collective-permute-start | bytes 1572872 | tf_op jit(solution)/shard_map/ppermute | solution.py:610
  17.9 35.6 %copy-start.16 = (bf16[1,128,2048]{2,1,0:T(8,128)(2,1)}, bf16[1,128,2048]{2,1,0:T(8,128)(2,1)S(1)}, u32[]{:S(2)}) copy-start(bf16[1,128,2048]{2,1,0:T(8,128)(2,1)S(1)} %collective-permute-done.4.refs_4_) | copy-start | bytes 1572868
  17.9 35.6 %collective-permute-start.5 = (bf16[1,128,2048]{2,1,0:T(8,128)(2,1)S(1)}, bf16[1,128,2048]{2,1,0:T(8,128)(2,1)}, u32[]{:S(2)}, u32[]{:S(2)}) collective-permute-start(bf16[1,128,2048]{2,1,0:T(8,128)(2,1)S(1)} %collective-permute-done.4.refs_4_), channel_id=1, source_target_pairs={{0,8},{8,0},{1,9},{9,1},{2,10},{10,2},{3,11},{11,3},{4,12},{12,4},... | collective-permute-start | bytes 1572872 | tf_op jit(solution)/shard_map/ppermute | solution.py:606
  20.7 32.7 %collective-permute-start.7 = (bf16[1,1024,256]{2,1,0:T(8,128)(2,1)}, bf16[1,1024,256]{2,1,0:T(8,128)(2,1)}, u32[]{:S(2)}, u32[]{:S(2)}) collective-permute-start(bf16[1,1024,256]{2,1,0:T(8,128)(2,1)} %collective-permute-done.6.refs_7_), channel_id=1, source_target_pairs={{0,8},{8,0},{1,9},{9,1},{2,10},{10,2},{3,11},{11,3},{4,12},{12,4},... | collective-permute-start | bytes 1572872 | tf_op jit(solution)/shard_map/ppermute | solution.py:606
  22.5 9.2 %collective-permute-start = (bf16[96,512]{1,0:T(8,128)(2,1)S(1)}, bf16[96,512]{1,0:T(8,128)(2,1)S(1)}, u32[]{:S(2)}, u32[]{:S(2)}) collective-permute-start(bf16[96,512]{1,0:T(8,128)(2,1)S(1)} %get-tuple-element.77), channel_id=1, source_target_pairs={{0,8},{16,24},{32,40},{48,56},{64,72},{80,88},{96,104},{112,120},{... | collective-permute-start | bytes 294920 | tf_op jit(solution)/shard_map/ppermute | solution.py:594
  29.2 59.4 %collective-permute-start.13 = (bf16[1,128,2048]{2,1,0:T(8,128)(2,1)}, bf16[1,128,2048]{2,1,0:T(8,128)(2,1)S(1)}, u32[]{:S(2)}, u32[]{:S(2)}) collective-permute-start(bf16[1,128,2048]{2,1,0:T(8,128)(2,1)} %collective-permute-done.12.refs_4_), channel_id=1, source_target_pairs={{0,8},{8,0},{1,9},{9,1},{2,10},{10,2},{3,11},{11,3},{4,12},{12,4},... | collective-permute-start | bytes 1572872 | tf_op jit(solution)/shard_map/ppermute | solution.py:606
  30.8 57.8 %collective-permute-start.15 = (bf16[1,1024,256]{2,1,0:T(8,128)(2,1)}, bf16[1,1024,256]{2,1,0:T(8,128)(2,1)S(1)}, u32[]{:S(2)}, u32[]{:S(2)}) collective-permute-start(bf16[1,1024,256]{2,1,0:T(8,128)(2,1)} %collective-permute-done.14.refs_7_), channel_id=1, source_target_pairs={{0,8},{8,0},{1,9},{9,1},{2,10},{10,2},{3,11},{11,3},{4,12},{12,4},... | collective-permute-start | bytes 1572872 | tf_op jit(solution)/shard_map/ppermute | solution.py:606
  31.7 5.9 %collective-permute-start.1 = (bf16[96,512]{1,0:T(8,128)(2,1)S(1)}, bf16[96,512]{1,0:T(8,128)(2,1)S(1)}, u32[]{:S(2)}, u32[]{:S(2)}) collective-permute-start(bf16[96,512]{1,0:T(8,128)(2,1)S(1)} %get-tuple-element.78), channel_id=1, source_target_pairs={{8,16},{24,32},{40,48},{56,64},{72,80},{88,96},{104,112},{16,8},{3... | collective-permute-start | bytes 294920 | tf_op jit(solution)/shard_map/ppermute | solution.py:595
  38.4 3.6 %collective-permute-start.2 = (bf16[336,128]{1,0:T(8,128)(2,1)S(1)}, bf16[336,128]{1,0:T(8,128)(2,1)S(1)}, u32[]{:S(2)}, u32[]{:S(2)}) collective-permute-start(bf16[336,128]{1,0:T(8,128)(2,1)S(1)} %get-tuple-element.80), channel_id=1, source_target_pairs={{0,2},{4,6},{2,0},{6,4},{1,3},{5,7},{3,1},{7,5},{8,10},{12,14},{10... | collective-permute-start | bytes 258056 | tf_op jit(solution)/shard_map/ppermute | solution.py:600
  42.0 0.7 collective-permute-start.3
  57.5 25.4 %copy-start.28 = (f32[2,512]{1,0:T(2,128)S(1)}, f32[2,512]{1,0:T(2,128)}, u32[]{:S(2)}) copy-start(f32[2,512]{1,0:T(2,128)} %bias.3) | copy-start | bytes 12292
  57.5 25.4 %copy-start.30 = (f32[2,512]{1,0:T(2,128)S(1)}, f32[2,512]{1,0:T(2,128)}, u32[]{:S(2)}) copy-start(f32[2,512]{1,0:T(2,128)} %shift.3) | copy-start | bytes 12292
  65.6 23.0 %copy-start.5 = (bf16[2,2048,256]{2,1,0:T(8,128)(2,1)S(1)}, bf16[2,2048,256]{2,1,0:T(8,128)(2,1)}, u32[]{:S(2)}) copy-start(bf16[2,2048,256]{2,1,0:T(8,128)(2,1)} %refs_6_.3) | copy-start | bytes 6291460
  65.6 23.0 %copy-start.24 = (f32[2,2048]{1,0:T(2,128)S(1)}, f32[2,2048]{1,0:T(2,128)}, u32[]{:S(2)}) copy-start(f32[2,2048]{1,0:T(2,128)} %refs_9_.3) | copy-start | bytes 49156
  65.6 23.0 %copy-start.32 = (f32[2,512]{1,0:T(2,128)S(1)}, f32[2,512]{1,0:T(2,128)}, u32[]{:S(2)}) copy-start(f32[2,512]{1,0:T(2,128)} %refs_10_.3) | copy-start | bytes 12292
  65.6 4.9 %collective-permute-start.8 = (bf16[96,512]{1,0:T(8,128)(2,1)S(1)}, bf16[96,512]{1,0:T(8,128)(2,1)S(1)}, u32[]{:S(2)}, u32[]{:S(2)}) collective-permute-start(bf16[96,512]{1,0:T(8,128)(2,1)S(1)} %get-tuple-element.84), channel_id=1, source_target_pairs={{0,8},{16,24},{32,40},{48,56},{64,72},{80,88},{96,104},{112,120},{... | collective-permute-start | bytes 294920 | tf_op jit(solution)/shard_map/ppermute | solution.py:594
  65.6 7.1 %collective-permute-start.9 = (bf16[96,512]{1,0:T(8,128)(2,1)S(1)}, bf16[96,512]{1,0:T(8,128)(2,1)S(1)}, u32[]{:S(2)}, u32[]{:S(2)}) collective-permute-start(bf16[96,512]{1,0:T(8,128)(2,1)S(1)} %get-tuple-element.85), channel_id=1, source_target_pairs={{8,16},{24,32},{40,48},{56,64},{72,80},{88,96},{104,112},{16,8},{3... | collective-permute-start | bytes 294920 | tf_op jit(solution)/shard_map/ppermute | solution.py:595
  73.5 9.4 %collective-permute-start.10 = (bf16[336,128]{1,0:T(8,128)(2,1)S(1)}, bf16[336,128]{1,0:T(8,128)(2,1)S(1)}, u32[]{:S(2)}, u32[]{:S(2)}) collective-permute-start(bf16[336,128]{1,0:T(8,128)(2,1)S(1)} %get-tuple-element.87), channel_id=1, source_target_pairs={{0,2},{4,6},{2,0},{6,4},{1,3},{5,7},{3,1},{7,5},{8,10},{12,14},{10... | collective-permute-start | bytes 258056 | tf_op jit(solution)/shard_map/ppermute | solution.py:600
  81.0 1.9 collective-permute-start.11
  88.6 6.9 %copy-start.14 = (bf16[1,16,32,512]{3,2,1,0:T(8,128)(2,1)S(1)}, bf16[1,16,32,512]{3,2,1,0:T(8,128)(2,1)}, u32[]{:S(2)}) copy-start(bf16[1,16,32,512]{3,2,1,0:T(8,128)(2,1)} %param.12) | copy-start | bytes 1572868
  99.0 15.7 %copy-start = (f32[4480,128]{1,0:T(8,128)}, f32[4480,128]{1,0:T(8,128)S(1)}, u32[]{:S(2)}) copy-start(f32[4480,128]{1,0:T(8,128)S(1)} %get-tuple-element.97.slab.old.grads) | copy-start | bytes 6881284
  102.1 18.7 %collective-permute-start.24 = (bf16[512,2048]{1,0:T(8,128)(2,1)S(1)}, bf16[512,2048]{1,0:T(8,128)(2,1)S(1)}, u32[]{:S(2)}, u32[]{:S(2)}) collective-permute-start(bf16[512,2048]{1,0:T(8,128)(2,1)S(1)} %get-tuple-element.124), channel_id=1, source_target_pairs={{0,8},{8,0},{1,9},{9,1},{2,10},{10,2},{3,11},{11,3},{4,12},{12,4},... | collective-permute-start | bytes 6291464 | tf_op jit(solution)/shard_map/ppermute | solution.py:606
  102.2 5.3 %collective-permute-start.16 = (bf16[96,512]{1,0:T(8,128)(2,1)S(1)}, bf16[96,512]{1,0:T(8,128)(2,1)S(1)}, u32[]{:S(2)}, u32[]{:S(2)}) collective-permute-start(bf16[96,512]{1,0:T(8,128)(2,1)S(1)} %get-tuple-element.98), channel_id=1, source_target_pairs={{0,8},{16,24},{32,40},{48,56},{64,72},{80,88},{96,104},{112,120},{... | collective-permute-start | bytes 294920 | tf_op jit(solution)/shard_map/ppermute | solution.py:594
  102.7 7.1 %collective-permute-start.17 = (bf16[96,512]{1,0:T(8,128)(2,1)S(1)}, bf16[96,512]{1,0:T(8,128)(2,1)S(1)}, u32[]{:S(2)}, u32[]{:S(2)}) collective-permute-start(bf16[96,512]{1,0:T(8,128)(2,1)S(1)} %get-tuple-element.99), channel_id=1, source_target_pairs={{8,16},{24,32},{40,48},{56,64},{72,80},{88,96},{104,112},{16,8},{3... | collective-permute-start | bytes 294920 | tf_op jit(solution)/shard_map/ppermute | solution.py:595
  107.5 13.2 %copy-start.18 = (bf16[96,512]{1,0:T(8,128)(2,1)}, bf16[96,512]{1,0:T(8,128)(2,1)S(1)}, u32[]{:S(2)}) copy-start(bf16[96,512]{1,0:T(8,128)(2,1)S(1)} %collective-permute-done.16.edge_near) | copy-start | bytes 294916
  109.8 10.9 %copy-start.19 = (bf16[96,512]{1,0:T(8,128)(2,1)}, bf16[96,512]{1,0:T(8,128)(2,1)S(1)}, u32[]{:S(2)}) copy-start(bf16[96,512]{1,0:T(8,128)(2,1)S(1)} %collective-permute-done.17.edge_far) | copy-start | bytes 294916
  110.4 28.1 %collective-permute-start.18 = (bf16[336,128]{1,0:T(8,128)(2,1)S(1)}, bf16[336,128]{1,0:T(8,128)(2,1)S(1)}, u32[]{:S(2)}, u32[]{:S(2)}) collective-permute-start(bf16[336,128]{1,0:T(8,128)(2,1)S(1)} %get-tuple-element.100), channel_id=1, source_target_pairs={{0,2},{4,6},{2,0},{6,4},{1,3},{5,7},{3,1},{7,5},{8,10},{12,14},{10... | collective-permute-start | bytes 258056 | tf_op jit(solution)/shard_map/ppermute | solution.py:600
  114.0 24.5 %collective-permute-start.19 = (bf16[336,128]{1,0:T(8,128)(2,1)S(1)}, bf16[336,128]{1,0:T(8,128)(2,1)S(1)}, u32[]{:S(2)}, u32[]{:S(2)}) collective-permute-start(bf16[336,128]{1,0:T(8,128)(2,1)S(1)} %get-tuple-element.101), channel_id=1, source_target_pairs={{2,4},{4,2},{3,5},{5,3},{10,12},{12,10},{11,13},{13,11},{18,20},{2... | collective-permute-start | bytes 258056 | tf_op jit(solution)/shard_map/ppermute | solution.py:601
  122.3 42.8 %all-to-all-start = ((bf16[64,8,2176]{2,1,0:T(8,128)(2,1)}), bf16[64,8,2176]{2,1,0:T(8,128)(2,1)}, u32[]{:S(2)}, u32[]{:S(2)}) async-start(bf16[64,8,2176]{2,1,0:T(8,128)(2,1)} %shard_map.177), calls=%async_computation | async-start | bytes 4456448 | tf_op jit(solution)/shard_map/all_to_all | solution.py:628
  149.7 103.8 %copy-start.1 = (f32[4480,128]{1,0:T(8,128)}, f32[4480,128]{1,0:T(8,128)S(1)}, u32[]{:S(2)}) copy-start(f32[4480,128]{1,0:T(8,128)S(1)} %get-tuple-element.115.slab.old.grads) | copy-start | bytes 6881284
  149.7 6.0 %copy-start.10 = (f32[4480,128]{1,0:T(8,128)S(1)}, f32[4480,128]{1,0:T(8,128)}, u32[]{:S(2)}) copy-start(f32[4480,128]{1,0:T(8,128)} %copy-done.9) | copy-start | bytes 6881284
  152.8 9.0 %collective-permute-start.25 = (bf16[512,2048]{1,0:T(8,128)(2,1)S(1)}, bf16[512,2048]{1,0:T(8,128)(2,1)S(1)}, u32[]{:S(2)}, u32[]{:S(2)}) collective-permute-start(bf16[512,2048]{1,0:T(8,128)(2,1)S(1)} %get-tuple-element.132), channel_id=1, source_target_pairs={{0,8},{8,0},{1,9},{9,1},{2,10},{10,2},{3,11},{11,3},{4,12},{12,4},... | collective-permute-start | bytes 6291464 | tf_op jit(solution)/shard_map/ppermute | solution.py:606
  165.1 39.1 %all-to-all-start.1 = ((bf16[64,8,2176]{2,1,0:T(8,128)(2,1)}), bf16[64,8,2176]{2,1,0:T(8,128)(2,1)}, u32[]{:S(2)}, u32[]{:S(2)}) async-start(bf16[64,8,2176]{2,1,0:T(8,128)(2,1)} %shard_map.181), calls=%async_computation.1 | async-start | bytes 4456448 | tf_op jit(solution)/shard_map/all_to_all | solution.py:628
  207.8 39.8 %copy-start.36 = (bf16[96,512]{1,0:T(8,128)(2,1)S(1)}, bf16[96,512]{1,0:T(8,128)(2,1)}, u32[]{:S(2)}) copy-start(bf16[96,512]{1,0:T(8,128)(2,1)} %copy-done.35) | copy-start | bytes 294916
  207.8 39.8 %copy-start.34 = (bf16[96,512]{1,0:T(8,128)(2,1)S(1)}, bf16[96,512]{1,0:T(8,128)(2,1)}, u32[]{:S(2)}) copy-start(bf16[96,512]{1,0:T(8,128)(2,1)} %copy-done.33) | copy-start | bytes 294916
  244.9 24.8 %collective-permute-start.26 = (bf16[32,8,4352]{2,1,0:T(8,128)(2,1)S(1)}, bf16[32,8,4352]{2,1,0:T(8,128)(2,1)S(1)}, u32[]{:S(2)}, u32[]{:S(2)}) collective-permute-start(bf16[32,8,4352]{2,1,0:T(8,128)(2,1)S(1)} %all_to_all.15.ref.whole0.whole1), channel_id=1, source_target_pairs={{0,8},{8,0},{1,9},{9,1},{2,10},{10,2},{3,11},{11,3},{4,12},{12,4},... | collective-permute-start | bytes 6684680 | tf_op jit(solution)/shard_map/ppermute | solution.py:606
  247.5 4.1 %collective-permute-start.20 = (bf16[96,512]{1,0:T(8,128)(2,1)S(1)}, bf16[96,512]{1,0:T(8,128)(2,1)S(1)}, u32[]{:S(2)}, u32[]{:S(2)}) collective-permute-start(bf16[96,512]{1,0:T(8,128)(2,1)S(1)} %copy-done.36), channel_id=1, source_target_pairs={{0,8},{16,24},{32,40},{48,56},{64,72},{80,88},{96,104},{112,120},{... | collective-permute-start | bytes 294920 | tf_op jit(solution)/shard_map/ppermute | solution.py:594
  247.5 5.9 %collective-permute-start.21 = (bf16[96,512]{1,0:T(8,128)(2,1)S(1)}, bf16[96,512]{1,0:T(8,128)(2,1)S(1)}, u32[]{:S(2)}, u32[]{:S(2)}) collective-permute-start(bf16[96,512]{1,0:T(8,128)(2,1)S(1)} %copy-done.34), channel_id=1, source_target_pairs={{8,16},{24,32},{40,48},{56,64},{72,80},{88,96},{104,112},{16,8},{3... | collective-permute-start | bytes 294920 | tf_op jit(solution)/shard_map/ppermute | solution.py:595
  254.1 3.4 %collective-permute-start.22 = (bf16[336,128]{1,0:T(8,128)(2,1)S(1)}, bf16[336,128]{1,0:T(8,128)(2,1)S(1)}, u32[]{:S(2)}, u32[]{:S(2)}) collective-permute-start(bf16[336,128]{1,0:T(8,128)(2,1)S(1)} %get-tuple-element.118), channel_id=1, source_target_pairs={{0,2},{4,6},{2,0},{6,4},{1,3},{5,7},{3,1},{7,5},{8,10},{12,14},{10... | collective-permute-start | bytes 258056 | tf_op jit(solution)/shard_map/ppermute | solution.py:600
  254.3 3.2 %collective-permute-start.23 = (bf16[336,128]{1,0:T(8,128)(2,1)S(1)}, bf16[336,128]{1,0:T(8,128)(2,1)S(1)}, u32[]{:S(2)}, u32[]{:S(2)}) collective-permute-start(bf16[336,128]{1,0:T(8,128)(2,1)S(1)} %get-tuple-element.119), channel_id=1, source_target_pairs={{2,4},{4,2},{3,5},{5,3},{10,12},{12,10},{11,13},{13,11},{18,20},{2... | collective-permute-start | bytes 258056 | tf_op jit(solution)/shard_map/ppermute | solution.py:601
  (22 other events, 42.9 us)
where the time goes:
time: 278 us; the launch traced here: 274 us
  Pallas kernels  85.5 us (31%)
  starting transfers between devices  76.5 us (28%)
  waiting for transfers between devices  58.8 us (21%)
  blocking collectives  37.1 us (13%)
  local copies, waits for them, and re-layouts  14.6 us (5%)
    pallas_call x21, Pallas kernels, run(): made(*(pltpu.with_memory_space_constraint(arg, pltpu.HBM) if n in far els...  78.2 us
    all_to_all x1, blocking collectives, per_device(): whole = lax.all_to_all(copies, SPACE, 0, 0, tiled=True)  37.1 us
    all_to_all x2, waiting for transfers between devices, send_grads(): return lax.all_to_all(pair, ('dp', *SPACE), 0, 0, tiled=True)  28.1 us
    all_to_all x2, starting transfers between devices, send_grads(): return lax.all_to_all(pair, ('dp', *SPACE), 0, 0, tiled=True)  26.6 us
    ppermute x4, starting transfers between devices, from_rows(): far = lax.ppermute(far, RANKS, pairs(1, 16))  15.3 us
    ppermute x4, waiting for transfers between devices, around_x(): lax.ppermute(value, ('xh', 'dp'), [(i, (i + step) % 4) for i in range(4)])  14.5 us
    ppermute x4, starting transfers between devices, from_columns(): near = lax.ppermute(near, 'z', pairs(0, 4))  13.1 us
    ppermute x7, starting transfers between devices, swapped(): return lax.ppermute(value, axis, [(0, 1), (1, 0)])  12.1 us
  transfers between devices with their start and end apart: 29, of which 12 were waited for; matrix products, arithmetic and copies ran while one was open for 0% of the time, Pallas kernels for 24%

commit v1 on v0

--- a/solution.py
+++ b/solution.py
@@ -15,7 +15,7 @@
 CH = 512
 FF = 2048
 HALF = 1024
-WIRE = FF + 128
+WIRE = FF + 256
 ROWS, COLS = 16, 32
 WIDE = 40
 DEEP = 14
@@ -189,12 +189,17 @@
 
 
 def norm_body(
-    k, place, old, near, far, kernel, bias, gain, shift, slab, normal, normed, rstd, store, taps
+    k, far, place, old, near, far_side, kernel, bias, gain, shift, slab, normal, normed, rstd,
+    store, taps, *held,
 ):
+    kept = slab, normed, rstd
+    if far:
+        slab, normed, rstd, sems = held
     one = slice(k, k + 1)
     spread(kernel, k, taps)
     slab[...] = old[...]
-    put_columns(slab, place[3], near, far)
+    put_columns(slab, place[3], near, far_side)
+    copies = [started(slab, kept[0], sems.at[0])] if far else []
     filtered(slab, taps, store, False)
     for row in range(ROWS):
         a, b = row * COLS, (row + 1) * COLS
@@ -205,6 +210,13 @@
         normed[a:b, :] = value
         rstd[a:b, :] = jnp.broadcast_to(scale, (COLS, 128))
         normal[a:b, :] = (value * gain[one, :] + shift[one, :]).astype(BF16)
+        if far and row in (7, 15):
+            span = pl.ds((row - 7) * COLS, 8 * COLS)
+            half = row // 8
+            copies.append(started(normed.at[span], kept[1].at[span], sems.at[1 + half]))
+            copies.append(started(rstd.at[span], kept[2].at[span], sems.at[3 + half]))
+    for copy in copies:
+        copy.wait()
 
 
 def mlp_body(k, far, *refs):
@@ -382,26 +394,33 @@
         copy.wait()
 
 
-def pair_body(keep, got, taps, channel, bias, far, out, lines, sems):
-    lines[0:196, :] = taps[...]
-    spot = 196
-    for kind in range(5):
-        for group in range(4):
-            lines[spot : spot + 1, :] = channel[
-                kind : kind + 1, group * 128 : (group + 1) * 128
-            ]
+def pair_body(count, keep, got, *refs):
+    parts, (far, out, *lines), sems = refs[: 3 * count], refs[3 * count : -1], refs[-1]
+    for n in range(count):
+        taps, channel, bias = parts[3 * n : 3 * n + 3]
+        ref = lines[n]
+        ref[0:196, :] = taps[...]
+        spot = 196
+        for kind in range(5):
+            for group in range(4):
+                ref[spot : spot + 1, :] = channel[
+                    kind : kind + 1, group * 128 : (group + 1) * 128
+                ]
+                spot += 1
+        for group in range(16):
+            ref[spot : spot + 1, :] = bias[:, group * 128 : (group + 1) * 128]
             spot += 1
-    for group in range(16):
-        lines[spot : spot + 1, :] = bias[:, group * 128 : (group + 1) * 128]
-        spot += 1
-    lines[spot:256, :] = jnp.zeros((256 - spot, 128), F32)
+        ref[spot:256, :] = jnp.zeros((256 - spot, 128), F32)
 
     def step(n, carry):
         rows = pl.ds(pl.multiple_of(n * 32, 32), 32)
         total = keep[rows, :].astype(F32) + got[rows, :].astype(F32)
         out[pl.ds(n * 4, 4), :, :FF] = total.reshape(4, 8, FF).astype(BF16)
         rows = pl.ds(pl.multiple_of((n % 8) * 32, 32), 32)
-        out[pl.ds(n * 4, 4), :, FF:] = lines[rows, :].reshape(4, 8, 128).astype(BF16)
+        for m in range(count):
+            out[pl.ds(n * 4, 4), :, FF + m * 128 : FF + (m + 1) * 128] = (
+                lines[m][rows, :].reshape(4, 8, 128).astype(BF16)
+            )
         return carry
 
     copies = []
@@ -414,7 +433,9 @@
 
 
 def total_body(pieces, out):
-    for a, b in ((0, 512), (512, 1024), (1024, 1536), (1536, WIRE)):
+    width = pieces.shape[2]
+    for a in range(0, width, 512):
+        b = min(a + 512, width)
 
         def step(n, total, a=a, b=b):
             for m in range(4):
@@ -426,14 +447,19 @@
 
 
 def merge_body(other, pieces, far, out, sums, sems):
+    for n in range(32):
+        out[n, :, FF : 2 * FF] = other[...]
+    copies = [started(out.at[:, :, FF : 2 * FF], far.at[:, :, FF : 2 * FF], sems.at[0])]
     total_body(pieces, sums)
-    copies = []
-    for part in range(4):
-        for n in range(part * 8, part * 8 + 8):
-            out[n, :, :WIRE] = sums[...]
-            out[n, :, WIRE:] = other[...]
-        span = pl.ds(part * 8, 8)
-        copies.append(started(out.at[span], far.at[span], sems.at[part]))
+    for part in range(2):
+        for n in range(part * 16, part * 16 + 16):
+            out[n, :, :FF] = sums[:, :FF]
+            out[n, :, 2 * FF :] = sums[:, FF:]
+        span = pl.ds(part * 16, 16)
+        for m, cols in enumerate((slice(0, FF), slice(2 * FF, 2 * FF + 256))):
+            copies.append(
+                started(out.at[span, :, cols], far.at[span, :, cols], sems.at[1 + part * 2 + m])
+            )
     for copy in copies:
         copy.wait()
 
@@ -455,7 +481,7 @@
 
 def finish_body(place, ref, *refs):
     grad_in, grad_out = refs[-2:]
-    value = ref[:, :, :FF].astype(F32).reshape(128, FF)
+    value = ref[...].astype(F32).reshape(128, FF)
     grad_in[0] = value[:, :HALF]
     grad_out[0] = value[:, HALF:].T
 
@@ -482,11 +508,16 @@
     )
 
 
-def normalise(k, place, slab, near, far, kernel, bias, gain, shift):
+def normalise(k, place, slab, near, far_side, kernel, bias, gain, shift):
     outs = [((SLAB, 128), F32), ((PIX, CH), BF16), ((PIX, CH), F32), ((PIX, 128), F32)]
+    far = k == 0
+    scratch = [STORE, TAPS]
+    if far:
+        scratch += [pltpu.VMEM(*outs[n]) for n in (0, 2, 3)] + [DMA((5,))]
     return call(
-        functools.partial(norm_body, k), outs, 8, 40_000_000, [STORE, TAPS], scalars=1
-    )(place, slab, near, far, kernel, bias, gain, shift)
+        functools.partial(norm_body, k, far), outs, 8, 40_000_000, scratch, scalars=1,
+        grant=8 if far else 5, far_out=(0, 2, 3) if far else (),
+    )(place, slab, near, far_side, kernel, bias, gain, shift)
 
 
 def mlp(k, place, a, normal, weights, bias_in, bias_out, scale):
@@ -542,7 +573,7 @@
         grid_spec=pltpu.PrefetchScalarGridSpec(
             num_scalar_prefetch=1,
             grid=(2, 2),
-            in_specs=[pl.BlockSpec((16, 8, WIRE), lambda layer, i, s: (i, 0, layer)), *held],
+            in_specs=[pl.BlockSpec((16, 8, FF), lambda layer, i, s: (i, 0, layer)), *held],
             out_specs=[
                 pl.BlockSpec((1, 128, HALF), lambda layer, i, s: (layer, i, s[side])),
                 pl.BlockSpec((1, HALF, 128), lambda layer, i, s: (layer, s[side], i)),
@@ -561,8 +592,8 @@
 
 
 def finish_small(whole, mate):
-    first = pl.BlockSpec((32, 8, 128), lambda i: (0, 0, FF // 128))
-    second = pl.BlockSpec((32, 8, 128), lambda i: (0, 0, (WIRE + FF) // 128))
+    first = pl.BlockSpec((32, 8, 128), lambda i: (0, 0, 2 * FF // 128))
+    second = pl.BlockSpec((32, 8, 128), lambda i: (0, 0, 2 * FF // 128 + 1))
     shapes = [(7, 7, 2, CH), (5, 2, CH), (2, FF)]
     return pl.pallas_call(
         small_body,
@@ -620,11 +651,16 @@
     return weight_in, got_in, mate_in, weight_out, got_out, mate_out
 
 
-def send_grads(keep, got, taps, channel, bias):
-    scratch = [pltpu.VMEM((64, 8, WIRE), BF16), pltpu.VMEM((256, 128), F32), DMA((4,))]
+def send_grads(keep, got, small):
+    count = len(small) // 3
+    shape = (64, 8, FF + 128 * count)
+    scratch = [
+        pltpu.VMEM(shape, BF16), *[pltpu.VMEM((256, 128), F32)] * count, DMA((4,)),
+    ]
     pair = call(
-        pair_body, [((64, 8, WIRE), BF16)], 5, 2_000_000, scratch, far_out=(0,)
-    )(keep, got, taps, channel, bias)[0]
+        functools.partial(pair_body, count), [(shape, BF16)], 2 + len(small), 2_000_000,
+        scratch, far_out=(0,),
+    )(keep, got, *small)[0]
     return lax.all_to_all(pair, ("dp", *SPACE), 0, 0, tiled=True)
 
 
@@ -662,6 +698,7 @@
         saved.append((slab, act, normal, (branch, slope, normed, rstd, full_in, full_out)))
     up = cotangent.reshape(PIX, CH)
     pieces = [None] * 2
+    small = []
     for k in (1, 0):
         seen, act, normal, rest = saved[k]
         low, gh, grads, *edges, channel, bias = backward(k, place, up, rest, norm_gain, layer_scale)
@@ -669,7 +706,8 @@
         keep, give = weight_grads(place, normal, low, act, gh)
         got = swapped(give, "core")
         taps = tap_grads(seen, grads)
-        pieces[k] = send_grads(keep, got, taps, channel, bias)
+        small = [taps, channel, bias, *small]
+        pieces[k] = send_grads(keep, got, () if k else small)
         sides = pack_edges(place, grads, *edges)
         sides = from_columns(*sides)
         later = saved[0][3] if k else ()
@@ -678,12 +716,12 @@
         )
         if k:
             saved[0] = (*saved[0][:3], brought)
-    other = call(total_body, [((8, WIRE), BF16)], 1, 5_000_000)(pieces[1])[0]
+    other = call(total_body, [((8, FF), BF16)], 1, 5_000_000)(pieces[1])[0]
     scratch = [
-        pltpu.VMEM((32, 8, 2 * WIRE), BF16), pltpu.VMEM((8, WIRE), BF16), DMA((4,)),
+        pltpu.VMEM((32, 8, FF + WIRE), BF16), pltpu.VMEM((8, WIRE), BF16), DMA((5,)),
     ]
     copies = call(
-        merge_body, [((32, 8, 2 * WIRE), BF16)], 2, 5_000_000, scratch, grant=8, far_out=(0,)
+        merge_body, [((32, 8, FF + WIRE), BF16)], 2, 5_000_000, scratch, grant=8, far_out=(0,)
     )(other, pieces[0])[0]
     whole = lax.all_to_all(copies, SPACE, 0, 0, tiled=True)
     mate = swapped(whole, "core")

time: 278 us -> 288 us (1.036)
  waiting for transfers between devices: 58.8 us -> 69.8 us
  local copies, waits for them, and re-layouts: 14.6 us -> 9.92 us
  Pallas kernels: 85.5 us -> 88.6 us
    all_to_all x2, waiting for transfers between devices: 28.1 us -> 38.2 us  [send_grads(): return lax.all_to_all(pair, ('dp', *SPACE), 0, 0, tiled=True)]
    unnamed x82 -> x74, local copies, waits for them, and re-layouts: 11.3 us -> 6.62 us
    all_to_all x2, starting transfers between devices: 26.6 us -> 30 us  [send_grads(): return lax.all_to_all(pair, ('dp', *SPACE), 0, 0, tiled=True)]
    pallas_call x21, Pallas kernels: 78.2 us -> 81.2 us  [run(): made(*(pltpu.with_memory_space_constraint(arg, pltpu.HBM) if n in far els...]
  transfers between devices with their start and end apart: 29 -> 29, of which waited for: 12 -> 13; matrix products, arithmetic and copies ran while one was open for 0% -> 0% of each run, Pallas kernels for 24% -> 24%
where the time goes in v1:
time: 288 us; the launch traced here: 285 us
  Pallas kernels  88.6 us (31%)
  starting transfers between devices  77.7 us (27%)
  waiting for transfers between devices  69.8 us (24%)
  blocking collectives  37.2 us (13%)
  local copies, waits for them, and re-layouts  9.92 us (3%)
    pallas_call x21, Pallas kernels, run(): made(*(pltpu.with_memory_space_constraint(arg, pltpu.HBM) if n in far els...  81.2 us
    all_to_all x2, waiting for transfers between devices, send_grads(): return lax.all_to_all(pair, ('dp', *SPACE), 0, 0, tiled=True)  38.2 us
    all_to_all x1, blocking collectives, per_device(): whole = lax.all_to_all(copies, SPACE, 0, 0, tiled=True)  37.2 us
    all_to_all x2, starting transfers between devices, send_grads(): return lax.all_to_all(pair, ('dp', *SPACE), 0, 0, tiled=True)  30 us
    ppermute x4, starting transfers between devices, from_rows(): far = lax.ppermute(far, RANKS, pairs(1, 16))  15.3 us
    ppermute x4, waiting for transfers between devices, around_x(): lax.ppermute(value, ('xh', 'dp'), [(i, (i + step) % 4) for i in range(4)])  14.4 us
    ppermute x4, starting transfers between devices, from_columns(): near = lax.ppermute(near, 'z', pairs(0, 4))  13.1 us
    ppermute x7, starting transfers between devices, swapped(): return lax.ppermute(value, axis, [(0, 1), (1, 0)])  9.42 us
  transfers between devices with their start and end apart: 29, of which 13 were waited for; matrix products, arithmetic and copies ran while one was open for 0% of the time, Pallas kernels for 24%

profile of v1, /device:TPU:1, one launch (start us, length us, event | category | flops | bytes accessed | tf_op | source)
XLA Modules:
  0.0 284.5 jit_solution(3741022493528772241)
XLA Ops:
  0.7 2.4 constant_dynamic-slice_fusion.1
  3.1 2.1 collective-permute-start.4
  6.1 1.4 collective-permute-start.6
  7.6 2.5 collective-permute-start.14
  10.1 7.9 %collective-permute-done.4.refs_4_ = bf16[1,128,2048]{2,1,0:T(8,128)(2,1)} collective-permute-done((bf16[1,128,2048]{2,1,0:T(8,128)(2,1)}, bf16[1,128,2048]{2,1,0:T(8,128)(2,1)}, u32[]{:S(2)}, u32[]{:S(2)}) %collective-permute-start.4) | collective-permute-done | bytes 524320 | tf_op jit(solution)/shard_map/ppermute | solution.py:641
  18.1 2.8 collective-permute-start.5
  22.7 6.4 %collective-permute-done.12.refs_4_ = bf16[1,128,2048]{2,1,0:T(8,128)(2,1)S(1)} collective-permute-done((bf16[1,128,2048]{2,1,0:T(8,128)(2,1)}, bf16[1,128,2048]{2,1,0:T(8,128)(2,1)S(1)}, u32[]{:S(2)}, u32[]{:S(2)}) %collective-permute-start.12) | collective-permute-done | bytes 524320 | tf_op jit(solution)/shard_map/ppermute | solution.py:641
  29.2 1.6 collective-permute-start.13
  31.8 3.1 %collective-permute-start.1 = (bf16[96,512]{1,0:T(8,128)(2,1)S(1)}, bf16[96,512]{1,0:T(8,128)(2,1)S(1)}, u32[]{:S(2)}, u32[]{:S(2)}) collective-permute-start(bf16[96,512]{1,0:T(8,128)(2,1)S(1)} %get-tuple-element.78), channel_id=1, source_target_pairs={{8,16},{24,32},{40,48},{56,64},{72,80},{88,96},{104,112},{16,8},{3... | collective-permute-start | bytes 294920 | tf_op jit(solution)/shard_map/ppermute | solution.py:626
  34.9 2.8 collective-permute-done.1.edge_far
  38.6 1.7 collective-permute-start.2
  40.3 1.9 collective-permute-done.2.near
  42.9 7.2 %shard_map.164 = (f32[4480,128]{1,0:T(8,128)}, bf16[512,512]{1,0:T(8,128)(2,1)S(1)}, f32[512,512]{1,0:T(8,128)}, f32[512,128]{1,0:T(8,128)}) custom-call(s32[4]{0:T(128)S(1)} %pad_add_fusion.place.refs_0_, f32[4480,128]{1,0:T(8,128)S(1)} %get-tuple-element.79.old, bf16[336,128]{1,0:T(8,128)(2,1)S(1)} %collective-permute-done.2.near, ...), custom_call_target="tpu_custom_call" | custom-call | flops 40000000 | bytes 4000000 | tf_op jit(solution)/shard_map/pallas_call | solution.py:54
  50.1 1.6 copy-done.7
  51.7 7.4 %shard_map.165 = (bf16[512,512]{1,0:T(8,128)(2,1)S(1)}, bf16[96,512]{1,0:T(8,128)(2,1)S(1)}, bf16[96,512]{1,0:T(8,128)(2,1)S(1)}, bf16[512,2048]{1,0:T(8,128)(2,...) custom-call(s32[4]{0:T(128)S(1)} %pad_add_fusion.place.refs_0_, ...), custom_call_target="tpu_custom_call" | custom-call | flops 60000000 | bytes 4000000 | tf_op jit(solution)/shard_map/pallas_call | solution.py:54
  59.3 4.8 %collective-permute-start.9 = (bf16[96,512]{1,0:T(8,128)(2,1)S(1)}, bf16[96,512]{1,0:T(8,128)(2,1)S(1)}, u32[]{:S(2)}, u32[]{:S(2)}) collective-permute-start(bf16[96,512]{1,0:T(8,128)(2,1)S(1)} %get-tuple-element.85), channel_id=1, source_target_pairs={{8,16},{24,32},{40,48},{56,64},{72,80},{88,96},{104,112},{16,8},{3... | collective-permute-start | bytes 294920 | tf_op jit(solution)/shard_map/ppermute | solution.py:626
  64.1 2.3 collective-permute-done.9.edge_far
  67.2 7.5 %collective-permute-start.10 = (bf16[336,128]{1,0:T(8,128)(2,1)S(1)}, bf16[336,128]{1,0:T(8,128)(2,1)S(1)}, u32[]{:S(2)}, u32[]{:S(2)}) collective-permute-start(bf16[336,128]{1,0:T(8,128)(2,1)S(1)} %get-tuple-element.87), channel_id=1, source_target_pairs={{0,2},{4,6},{2,0},{6,4},{1,3},{5,7},{3,1},{7,5},{8,10},{12,14},{10... | collective-permute-start | bytes 258056 | tf_op jit(solution)/shard_map/ppermute | solution.py:631
  76.6 5.6 %shard_map.167 = (f32[4480,128]{1,0:T(8,128)S(1)}, bf16[512,512]{1,0:T(8,128)(2,1)S(1)}, f32[512,512]{1,0:T(8,128)S(1)}, f32[512,128]{1,0:T(8,128)S(1)}) custom-call(s32[4]{0:T(128)S(1)} %pad_add_fusion.place.refs_0_, f32[4480,128]{1,0:T(8,128)S(1)} %get-tuple-element.86.old, bf16[336,128]{1,0:T(8,128)(2,1)S(1)} %collective-permute-done.10.near, ...), custom_call_target="tpu_custom_call" | custom-call | flops 40000000 | bytes 4000000 | tf_op jit(solution)/shard_map/pallas_call | solution.py:54
  82.3 7.2 %shard_map.168 = (bf16[512,512]{1,0:T(8,128)(2,1)}, bf16[96,512]{1,0:T(8,128)(2,1)}, bf16[96,512]{1,0:T(8,128)(2,1)}, bf16[512,2048]{1,0:T(8,128)(2,1)S(1)}, bf1...) custom-call(s32[4]{0:T(128)S(1)} %pad_add_fusion.place.refs_0_, ...), custom_call_target="tpu_custom_call" | custom-call | flops 60000000 | bytes 4000000 | tf_op jit(solution)/shard_map/pallas_call | solution.py:54
  89.5 3.5 %shard_map.169 = (bf16[512,512]{1,0:T(8,128)(2,1)S(1)}, bf16[512,2048]{1,0:T(8,128)(2,1)S(1)}, f32[4480,128]{1,0:T(8,128)S(1)}, bf16[96,512]{1,0:T(8,128)(2,1)S(...) custom-call(s32[4]{0:T(128)S(1)} %pad_add_fusion.place.refs_0_, ...), custom_call_target="tpu_custom_call" | custom-call | flops 60000000 | bytes 4000000 | tf_op jit(solution)/shard_map/pallas_call | solution.py:54
  93.1 3.0 %shard_map.175 = (bf16[512,2048]{1,0:T(8,128)(2,1)S(1)}, bf16[512,2048]{1,0:T(8,128)(2,1)S(1)}) custom-call(s32[4]{0:T(128)S(1)} %pad_add_fusion.place.refs_0_, bf16[512,512]{1,0:T(8,128)(2,1)S(1)} %get-tuple-element.89.refs_2_.normal, bf16[512,512]{1,0:T(8,128)(2,1)S(1)} %get-tuple-element.120.low, bf16[512,2048]{1,0:T(8,128)(2,1)S(1)} %get-tuple-element.121.act, ...), custom_call_target="tpu_custom_call" | custom-call | flops 50000000 | bytes 4000000 | tf_op jit(solution)/shard_map/pallas_call | solution.py:54
  96.7 4.8 %collective-permute-start.17 = (bf16[96,512]{1,0:T(8,128)(2,1)S(1)}, bf16[96,512]{1,0:T(8,128)(2,1)S(1)}, u32[]{:S(2)}, u32[]{:S(2)}) collective-permute-start(bf16[96,512]{1,0:T(8,128)(2,1)S(1)} %get-tuple-element.99), channel_id=1, source_target_pairs={{8,16},{24,32},{40,48},{56,64},{72,80},{88,96},{104,112},{16,8},{3... | collective-permute-start | bytes 294920 | tf_op jit(solution)/shard_map/ppermute | solution.py:626
  101.6 2.3 collective-permute-done.17.edge_far
  104.4 3.6 %collective-permute-start.18 = (bf16[336,128]{1,0:T(8,128)(2,1)S(1)}, bf16[336,128]{1,0:T(8,128)(2,1)S(1)}, u32[]{:S(2)}, u32[]{:S(2)}) collective-permute-start(bf16[336,128]{1,0:T(8,128)(2,1)S(1)} %get-tuple-element.100), channel_id=1, source_target_pairs={{0,2},{4,6},{2,0},{6,4},{1,3},{5,7},{3,1},{7,5},{8,10},{12,14},{10... | collective-permute-start | bytes 258056 | tf_op jit(solution)/shard_map/ppermute | solution.py:631
  110.6 7.6 %shard_map.171 = (f32[512,512]{1,0:T(8,128)S(1)}, f32[512,512]{1,0:T(8,128)S(1)}, bf16[512,2048]{1,0:T(8,128)(2,1)S(1)}, f32[512,512]{1,0:T(8,128)S(1)}, f32[512...) custom-call(s32[4]{0:T(128)S(1)} %pad_add_fusion.place.refs_0_, ...), custom_call_target="tpu_custom_call" | custom-call | flops 40000000 | bytes 4000000 | tf_op jit(solution)/shard_map/pallas_call | solution.py:54
  118.2 3.4 %shard_map.172 = (bf16[512,512]{1,0:T(8,128)(2,1)S(1)}, bf16[512,2048]{1,0:T(8,128)(2,1)S(1)}, f32[4480,128]{1,0:T(8,128)S(1)}, bf16[96,512]{1,0:T(8,128)(2,1)S(...) custom-call(s32[4]{0:T(128)S(1)} %pad_add_fusion.place.refs_0_, ...), custom_call_target="tpu_custom_call" | custom-call | flops 60000000 | bytes 4000000 | tf_op jit(solution)/shard_map/pallas_call | solution.py:54
  121.7 3.7 %shard_map.178 = (bf16[512,2048]{1,0:T(8,128)(2,1)S(1)}, bf16[512,2048]{1,0:T(8,128)(2,1)}) custom-call(s32[4]{0:T(128)S(1)} %pad_add_fusion.place.refs_0_, bf16[512,512]{1,0:T(8,128)(2,1)S(1)} %get-tuple-element.82.refs_2_.normal, bf16[512,512]{1,0:T(8,128)(2,1)S(1)} %get-tuple-element.125.low, bf16[512,2048]{1,0:T(8,128)(2,1)S(1)} %copy-done.17, ...), custom_call_target="tpu_custom_call" | custom-call | flops 50000000 | bytes 4000000 | tf_op jit(solution)/shard_map/pallas_call | solution.py:54
  126.8 1.6 shard_map.176
  128.4 22.0 %all-to-all-start = ((bf16[64,8,2048]{2,1,0:T(8,128)(2,1)}), bf16[64,8,2048]{2,1,0:T(8,128)(2,1)}, u32[]{:S(2)}, u32[]{:S(2)}) async-start(bf16[64,8,2048]{2,1,0:T(8,128)(2,1)} %shard_map.176), calls=%async_computation | async-start | bytes 4194304 | tf_op jit(solution)/shard_map/all_to_all | solution.py:664
  150.4 1.6 copy-done.16
  152.1 6.0 %shard_map.180.refs_3_ = f32[196,128]{1,0:T(8,128)S(1)} custom-call(f32[4480,128]{1,0:T(8,128)S(1)} %copy-done.16, f32[4480,128]{1,0:T(8,128)S(1)} %copy-done.1), custom_call_target="tpu_custom_call" | custom-call | flops 40000000 | bytes 4000000 | tf_op jit(solution)/shard_map/pallas_call | solution.py:54
  158.1 6.0 %shard_map.179.refs_0_ = f32[196,128]{1,0:T(8,128)S(1)} custom-call(f32[4480,128]{1,0:T(8,128)S(1)} %copy-done.14, f32[4480,128]{1,0:T(8,128)S(1)} %copy-done.3), custom_call_target="tpu_custom_call" | custom-call | flops 40000000 | bytes 4000000 | tf_op jit(solution)/shard_map/pallas_call | solution.py:54
  164.2 3.2 %shard_map.181 = bf16[64,8,2304]{2,1,0:T(8,128)(2,1)} custom-call(bf16[512,2048]{1,0:T(8,128)(2,1)S(1)} %copy-done.19, bf16[512,2048]{1,0:T(8,128)(2,1)} %collective-permute-done.25.got, f32[196,128]{1,0:T(8,128)S(1)} %shard_map.179.refs_0_, f32[8,512]{1,0:T(8,128)S(1)} %get-tuple-element.131.refs_1_, f32[1,2048]{1,0:T(1,128)S(1)} %get-tuple-element.132.refs_2_, ...), custom_call_target="tpu_custom_call" | custom-call | flops 2000000 | bytes 4000000 | tf_op jit(solution)/shard_map/pallas_call | solution.py:54
  167.4 10.5 %all-to-all-done.pieces = bf16[64,8,2048]{2,1,0:T(8,128)(2,1)} async-done(((bf16[64,8,2048]{2,1,0:T(8,128)(2,1)}), bf16[64,8,2048]{2,1,0:T(8,128)(2,1)}, u32[]{:S(2)}, u32[]{:S(2)}) %all-to-all-start) | async-done | bytes 2097184 | tf_op jit(solution)/shard_map/all_to_all | solution.py:664
  177.9 8.0 %all-to-all-start.1 = ((bf16[64,8,2304]{2,1,0:T(8,128)(2,1)}), bf16[64,8,2304]{2,1,0:T(8,128)(2,1)S(1)}, u32[]{:S(2)}, u32[]{:S(2)}) async-start(bf16[64,8,2304]{2,1,0:T(8,128)(2,1)} %shard_map.181), calls=%async_computation.1 | async-start | bytes 4718592 | tf_op jit(solution)/shard_map/all_to_all | solution.py:664
  185.9 2.1 shard_map.177.other
  188.0 27.8 %all-to-all-done.1.pieces = bf16[64,8,2304]{2,1,0:T(8,128)(2,1)S(1)} async-done(((bf16[64,8,2304]{2,1,0:T(8,128)(2,1)}), bf16[64,8,2304]{2,1,0:T(8,128)(2,1)S(1)}, u32[]{:S(2)}, u32[]{:S(2)}) %all-to-all-start.1) | async-done | bytes 2359328 | tf_op jit(solution)/shard_map/all_to_all | solution.py:664
  215.7 1.8 shard_map.182
  217.6 37.2 %all_to_all.15.ref.whole0.whole1 = bf16[32,8,4352]{2,1,0:T(8,128)(2,1)S(1)} all-to-all(bf16[32,8,4352]{2,1,0:T(8,128)(2,1)} %shard_map.182), channel_id=1, replica_groups=mesh['xh'=2,'y'=4,'core'=2,'z'=4,'dp'=2] {'xh','y','z'}, dimensions={0} | all-to-all | bytes 4456448 | tf_op jit(solution)/shard_map/all_to_all | solution.py:726
  254.7 2.7 collective-permute-start.26
  257.6 2.5 collective-permute-start.21
  260.1 1.5 collective-permute-done.20.edge_near
  261.6 1.9 collective-permute-done.21.edge_far
  265.0 2.5 collective-permute-done.22.near
  268.8 8.3 %shard_map.174 = bf16[512,512]{1,0:T(8,128)(2,1)} custom-call(s32[4]{0:T(128)S(1)} %pad_add_fusion.place.refs_0_, f32[4480,128]{1,0:T(8,128)} %copy-done.2, bf16[96,512]{1,0:T(8,128)(2,1)} %copy-done.23, bf16[96,512]{1,0:T(8,128)(2,1)} %copy-done.24, bf16[336,128]{1,0:T(8,128)(2,1)} %copy-done.35, bf16[336,128]{1,0:T(8,128)(2,1)} %copy-done.36, ...), custom_call_target="tpu_custom_call" | custom-call | flops 40000000 | bytes 4000000 | tf_op jit(solution)/shard_map/pallas_call | solution.py:54
  277.1 3.3 %shard_map.183 = (f32[2,256,2048]{2,1,0:T(8,128)}, f32[2,2048,256]{2,1,0:T(8,128)}) custom-call(s32[4]{0:T(128)S(1)} %pad_add_fusion.place.refs_0_, bf16[32,8,4352]{2,1,0:T(8,128)(2,1)S(1)} %all_to_all.15.ref.whole0.whole1), custom_call_target="tpu_custom_call" | custom-call | flops 5000000 | bytes 6000000 | tf_op jit(solution)/shard_map/pallas_call | solution.py:571
  281.3 3.3 %shard_map.184 = (f32[2,256,2048]{2,1,0:T(8,128)}, f32[2,2048,256]{2,1,0:T(8,128)}) custom-call(s32[4]{0:T(128)S(1)} %pad_add_fusion.place.refs_0_, bf16[32,8,4352]{2,1,0:T(8,128)(2,1)S(1)} %collective-permute-done.26.ref.mate0.mate1, f32[2,256,2048]{2,1,0:T(8,128)} %get-tuple-element.136.refs_0_, ...), custom_call_target="tpu_custom_call", output_to_operand_aliasing={{0}: (2, {}), {1}: (3, {})} | custom-call | flops 5000000 | bytes 6000000 | tf_op jit(solution)/shard_map/pallas_call | solution.py:571
  (112 shorter events, 17.1 us)
Async XLA Ops:
  0.6 21.4 %copy-start.9 = (bf16[1,16,32,512]{3,2,1,0:T(8,128)(2,1)S(1)}, bf16[1,16,32,512]{3,2,1,0:T(8,128)(2,1)}, u32[]{:S(2)}) copy-start(bf16[1,16,32,512]{3,2,1,0:T(8,128)(2,1)} %param.11) | copy-start | bytes 1572868
  3.1 39.8 %copy-start.11 = (f32[2,7,7,512]{3,0,2,1:T(2,128)S(1)}, f32[2,7,7,512]{3,0,2,1:T(2,128)}, u32[]{:S(2)}) copy-start(f32[2,7,7,512]{3,0,2,1:T(2,128)} %param.13) | copy-start | bytes 602116
  3.1 39.8 %copy-start.26 = (f32[2,512]{1,0:T(2,128)S(1)}, f32[2,512]{1,0:T(2,128)}, u32[]{:S(2)}) copy-start(f32[2,512]{1,0:T(2,128)} %gain.7) | copy-start | bytes 12292
  3.1 39.8 %copy-start.28 = (f32[2,512]{1,0:T(2,128)S(1)}, f32[2,512]{1,0:T(2,128)}, u32[]{:S(2)}) copy-start(f32[2,512]{1,0:T(2,128)} %bias.3) | copy-start | bytes 12292
  3.1 39.8 %copy-start.29 = (f32[2,512]{1,0:T(2,128)S(1)}, f32[2,512]{1,0:T(2,128)}, u32[]{:S(2)}) copy-start(f32[2,512]{1,0:T(2,128)} %shift.3) | copy-start | bytes 12292
  3.1 14.9 %collective-permute-start.4 = (bf16[1,128,2048]{2,1,0:T(8,128)(2,1)}, bf16[1,128,2048]{2,1,0:T(8,128)(2,1)}, u32[]{:S(2)}, u32[]{:S(2)}) collective-permute-start(bf16[1,128,2048]{2,1,0:T(8,128)(2,1)} %get-tuple-element.146), channel_id=1, source_target_pairs={{0,1},{1,64},{64,65},{65,0},{2,3},{3,66},{66,67},{67,2},{4,5},{5,6... | collective-permute-start | bytes 1572872 | tf_op jit(solution)/shard_map/ppermute | solution.py:641
  6.1 44.0 %copy-start.5 = (bf16[2,256,2048]{2,1,0:T(8,128)(2,1)S(1)}, bf16[2,256,2048]{2,1,0:T(8,128)(2,1)}, u32[]{:S(2)}) copy-start(bf16[2,256,2048]{2,1,0:T(8,128)(2,1)} %refs_3_.3) | copy-start | bytes 6291460
  6.1 44.0 %copy-start.25 = (f32[2,2048]{1,0:T(2,128)S(1)}, f32[2,2048]{1,0:T(2,128)}, u32[]{:S(2)}) copy-start(f32[2,2048]{1,0:T(2,128)} %refs_9_.3) | copy-start | bytes 49156
  6.1 44.0 %copy-start.27 = (f32[2,512]{1,0:T(2,128)S(1)}, f32[2,512]{1,0:T(2,128)}, u32[]{:S(2)}) copy-start(f32[2,512]{1,0:T(2,128)} %scale.3) | copy-start | bytes 12292
  6.1 44.1 %copy-start.30 = (f32[2,512]{1,0:T(2,128)S(1)}, f32[2,512]{1,0:T(2,128)}, u32[]{:S(2)}) copy-start(f32[2,512]{1,0:T(2,128)} %refs_10_.3) | copy-start | bytes 12292
  6.1 14.8 %collective-permute-start.6 = (bf16[1,1024,256]{2,1,0:T(8,128)(2,1)S(1)}, bf16[1,1024,256]{2,1,0:T(8,128)(2,1)}, u32[]{:S(2)}, u32[]{:S(2)}) collective-permute-start(bf16[1,1024,256]{2,1,0:T(8,128)(2,1)S(1)} %get-tuple-element.144), channel_id=1, source_target_pairs={{0,65},{1,0},{64,1},{65,64},{2,67},{3,2},{66,3},{67,66},{4,69},{5,... | collective-permute-start | bytes 1572872 | tf_op jit(solution)/shard_map/ppermute | solution.py:641
  7.4 21.7 %collective-permute-start.12 = (bf16[1,128,2048]{2,1,0:T(8,128)(2,1)}, bf16[1,128,2048]{2,1,0:T(8,128)(2,1)S(1)}, u32[]{:S(2)}, u32[]{:S(2)}) collective-permute-start(bf16[1,128,2048]{2,1,0:T(8,128)(2,1)} %get-tuple-element.145), channel_id=1, source_target_pairs={{0,1},{1,64},{64,65},{65,0},{2,3},{3,66},{66,67},{67,2},{4,5},{5,6... | collective-permute-start | bytes 1572872 | tf_op jit(solution)/shard_map/ppermute | solution.py:641
  7.6 23.2 %collective-permute-start.14 = (bf16[1,1024,256]{2,1,0:T(8,128)(2,1)}, bf16[1,1024,256]{2,1,0:T(8,128)(2,1)}, u32[]{:S(2)}, u32[]{:S(2)}) collective-permute-start(bf16[1,1024,256]{2,1,0:T(8,128)(2,1)} %get-tuple-element.143), channel_id=1, source_target_pairs={{0,65},{1,0},{64,1},{65,64},{2,67},{3,2},{66,3},{67,66},{4,69},{5,... | collective-permute-start | bytes 1572872 | tf_op jit(solution)/shard_map/ppermute | solution.py:641
  18.1 32.0 %collective-permute-start.5 = (bf16[1,128,2048]{2,1,0:T(8,128)(2,1)}, bf16[1,128,2048]{2,1,0:T(8,128)(2,1)}, u32[]{:S(2)}, u32[]{:S(2)}) collective-permute-start(bf16[1,128,2048]{2,1,0:T(8,128)(2,1)} %collective-permute-done.4.refs_4_), channel_id=1, source_target_pairs={{0,8},{8,0},{1,9},{9,1},{2,10},{10,2},{3,11},{11,3},{4,12},{12,4},... | collective-permute-start | bytes 1572872 | tf_op jit(solution)/shard_map/ppermute | solution.py:637
  20.9 29.2 %collective-permute-start.7 = (bf16[1,1024,256]{2,1,0:T(8,128)(2,1)}, bf16[1,1024,256]{2,1,0:T(8,128)(2,1)}, u32[]{:S(2)}, u32[]{:S(2)}) collective-permute-start(bf16[1,1024,256]{2,1,0:T(8,128)(2,1)} %collective-permute-done.6.refs_7_), channel_id=1, source_target_pairs={{0,8},{8,0},{1,9},{9,1},{2,10},{10,2},{3,11},{11,3},{4,12},{12,4},... | collective-permute-start | bytes 1572872 | tf_op jit(solution)/shard_map/ppermute | solution.py:637
  22.7 9.2 %collective-permute-start = (bf16[96,512]{1,0:T(8,128)(2,1)S(1)}, bf16[96,512]{1,0:T(8,128)(2,1)S(1)}, u32[]{:S(2)}, u32[]{:S(2)}) collective-permute-start(bf16[96,512]{1,0:T(8,128)(2,1)S(1)} %get-tuple-element.77), channel_id=1, source_target_pairs={{0,8},{16,24},{32,40},{48,56},{64,72},{80,88},{96,104},{112,120},{... | collective-permute-start | bytes 294920 | tf_op jit(solution)/shard_map/ppermute | solution.py:625
  29.2 53.0 %collective-permute-start.13 = (bf16[1,128,2048]{2,1,0:T(8,128)(2,1)S(1)}, bf16[1,128,2048]{2,1,0:T(8,128)(2,1)S(1)}, u32[]{:S(2)}, u32[]{:S(2)}) collective-permute-start(bf16[1,128,2048]{2,1,0:T(8,128)(2,1)S(1)} %collective-permute-done.12.refs_4_), channel_id=1, source_target_pairs={{0,8},{8,0},{1,9},{9,1},{2,10},{10,2},{3,11},{11,3},{4,12},{12,4},... | collective-permute-start | bytes 1572872 | tf_op jit(solution)/shard_map/ppermute | solution.py:637
  30.8 51.4 %collective-permute-start.15 = (bf16[1,1024,256]{2,1,0:T(8,128)(2,1)}, bf16[1,1024,256]{2,1,0:T(8,128)(2,1)S(1)}, u32[]{:S(2)}, u32[]{:S(2)}) collective-permute-start(bf16[1,1024,256]{2,1,0:T(8,128)(2,1)} %collective-permute-done.14.refs_7_), channel_id=1, source_target_pairs={{0,8},{8,0},{1,9},{9,1},{2,10},{10,2},{3,11},{11,3},{4,12},{12,4},... | collective-permute-start | bytes 1572872 | tf_op jit(solution)/shard_map/ppermute | solution.py:637
  31.8 5.9 %collective-permute-start.1 = (bf16[96,512]{1,0:T(8,128)(2,1)S(1)}, bf16[96,512]{1,0:T(8,128)(2,1)S(1)}, u32[]{:S(2)}, u32[]{:S(2)}) collective-permute-start(bf16[96,512]{1,0:T(8,128)(2,1)S(1)} %get-tuple-element.78), channel_id=1, source_target_pairs={{8,16},{24,32},{40,48},{56,64},{72,80},{88,96},{104,112},{16,8},{3... | collective-permute-start | bytes 294920 | tf_op jit(solution)/shard_map/ppermute | solution.py:626
  38.6 3.6 %collective-permute-start.2 = (bf16[336,128]{1,0:T(8,128)(2,1)S(1)}, bf16[336,128]{1,0:T(8,128)(2,1)S(1)}, u32[]{:S(2)}, u32[]{:S(2)}) collective-permute-start(bf16[336,128]{1,0:T(8,128)(2,1)S(1)} %get-tuple-element.80), channel_id=1, source_target_pairs={{0,2},{4,6},{2,0},{6,4},{1,3},{5,7},{3,1},{7,5},{8,10},{12,14},{10... | collective-permute-start | bytes 258056 | tf_op jit(solution)/shard_map/ppermute | solution.py:631
  42.2 0.7 collective-permute-start.3
  59.2 23.1 %copy-start.8 = (bf16[2,2048,256]{2,1,0:T(8,128)(2,1)S(1)}, bf16[2,2048,256]{2,1,0:T(8,128)(2,1)}, u32[]{:S(2)}) copy-start(bf16[2,2048,256]{2,1,0:T(8,128)(2,1)} %refs_6_.3) | copy-start | bytes 6291460
  59.2 4.9 %collective-permute-start.8 = (bf16[96,512]{1,0:T(8,128)(2,1)S(1)}, bf16[96,512]{1,0:T(8,128)(2,1)S(1)}, u32[]{:S(2)}, u32[]{:S(2)}) collective-permute-start(bf16[96,512]{1,0:T(8,128)(2,1)S(1)} %get-tuple-element.84), channel_id=1, source_target_pairs={{0,8},{16,24},{32,40},{48,56},{64,72},{80,88},{96,104},{112,120},{... | collective-permute-start | bytes 294920 | tf_op jit(solution)/shard_map/ppermute | solution.py:625
  59.3 7.1 %collective-permute-start.9 = (bf16[96,512]{1,0:T(8,128)(2,1)S(1)}, bf16[96,512]{1,0:T(8,128)(2,1)S(1)}, u32[]{:S(2)}, u32[]{:S(2)}) collective-permute-start(bf16[96,512]{1,0:T(8,128)(2,1)S(1)} %get-tuple-element.85), channel_id=1, source_target_pairs={{8,16},{24,32},{40,48},{56,64},{72,80},{88,96},{104,112},{16,8},{3... | collective-permute-start | bytes 294920 | tf_op jit(solution)/shard_map/ppermute | solution.py:626
  67.2 9.3 %collective-permute-start.10 = (bf16[336,128]{1,0:T(8,128)(2,1)S(1)}, bf16[336,128]{1,0:T(8,128)(2,1)S(1)}, u32[]{:S(2)}, u32[]{:S(2)}) collective-permute-start(bf16[336,128]{1,0:T(8,128)(2,1)S(1)} %get-tuple-element.87), channel_id=1, source_target_pairs={{0,2},{4,6},{2,0},{6,4},{1,3},{5,7},{3,1},{7,5},{8,10},{12,14},{10... | collective-permute-start | bytes 258056 | tf_op jit(solution)/shard_map/ppermute | solution.py:631
  74.7 1.9 collective-permute-start.11
  82.2 7.3 %copy-start.15 = (f32[4480,128]{1,0:T(8,128)}, f32[4480,128]{1,0:T(8,128)S(1)}, u32[]{:S(2)}) copy-start(f32[4480,128]{1,0:T(8,128)S(1)} %get-tuple-element.133.seen) | copy-start | bytes 6881284
  82.3 7.2 %copy-start.20 = (bf16[1,16,32,512]{3,2,1,0:T(8,128)(2,1)S(1)}, bf16[1,16,32,512]{3,2,1,0:T(8,128)(2,1)}, u32[]{:S(2)}) copy-start(bf16[1,16,32,512]{3,2,1,0:T(8,128)(2,1)} %param.12) | copy-start | bytes 1572868
  93.0 10.8 %copy-start = (f32[4480,128]{1,0:T(8,128)}, f32[4480,128]{1,0:T(8,128)S(1)}, u32[]{:S(2)}) copy-start(f32[4480,128]{1,0:T(8,128)S(1)} %get-tuple-element.97.slab.old.grads) | copy-start | bytes 6881284
  96.1 14.5 %copy-start.12 = (f32[2,7,7,512]{3,0,2,1:T(2,128)S(1)}, f32[2,7,7,512]{3,0,2,1:T(2,128)}, u32[]{:S(2)}) copy-start(f32[2,7,7,512]{3,0,2,1:T(2,128)} %param.13) | copy-start | bytes 602116
  96.1 30.7 %collective-permute-start.24 = (bf16[512,2048]{1,0:T(8,128)(2,1)S(1)}, bf16[512,2048]{1,0:T(8,128)(2,1)S(1)}, u32[]{:S(2)}, u32[]{:S(2)}) collective-permute-start(bf16[512,2048]{1,0:T(8,128)(2,1)S(1)} %get-tuple-element.124), channel_id=1, source_target_pairs={{0,8},{8,0},{1,9},{9,1},{2,10},{10,2},{3,11},{11,3},{4,12},{12,4},... | collective-permute-start | bytes 6291464 | tf_op jit(solution)/shard_map/ppermute | solution.py:637
  96.2 5.3 %collective-permute-start.16 = (bf16[96,512]{1,0:T(8,128)(2,1)S(1)}, bf16[96,512]{1,0:T(8,128)(2,1)S(1)}, u32[]{:S(2)}, u32[]{:S(2)}) collective-permute-start(bf16[96,512]{1,0:T(8,128)(2,1)S(1)} %get-tuple-element.98), channel_id=1, source_target_pairs={{0,8},{16,24},{32,40},{48,56},{64,72},{80,88},{96,104},{112,120},{... | collective-permute-start | bytes 294920 | tf_op jit(solution)/shard_map/ppermute | solution.py:625
  96.7 7.1 %collective-permute-start.17 = (bf16[96,512]{1,0:T(8,128)(2,1)S(1)}, bf16[96,512]{1,0:T(8,128)(2,1)S(1)}, u32[]{:S(2)}, u32[]{:S(2)}) collective-permute-start(bf16[96,512]{1,0:T(8,128)(2,1)S(1)} %get-tuple-element.99), channel_id=1, source_target_pairs={{8,16},{24,32},{40,48},{56,64},{72,80},{88,96},{104,112},{16,8},{3... | collective-permute-start | bytes 294920 | tf_op jit(solution)/shard_map/ppermute | solution.py:626
  101.5 8.4 %copy-start.21 = (bf16[96,512]{1,0:T(8,128)(2,1)}, bf16[96,512]{1,0:T(8,128)(2,1)S(1)}, u32[]{:S(2)}) copy-start(bf16[96,512]{1,0:T(8,128)(2,1)S(1)} %collective-permute-done.16.edge_near) | copy-start | bytes 294916
  104.4 5.5 %collective-permute-start.18 = (bf16[336,128]{1,0:T(8,128)(2,1)S(1)}, bf16[336,128]{1,0:T(8,128)(2,1)S(1)}, u32[]{:S(2)}, u32[]{:S(2)}) collective-permute-start(bf16[336,128]{1,0:T(8,128)(2,1)S(1)} %get-tuple-element.100), channel_id=1, source_target_pairs={{0,2},{4,6},{2,0},{6,4},{1,3},{5,7},{3,1},{7,5},{8,10},{12,14},{10... | collective-permute-start | bytes 258056 | tf_op jit(solution)/shard_map/ppermute | solution.py:631
  108.0 1.9 collective-permute-start.19
  126.8 37.3 %collective-permute-start.25 = (bf16[512,2048]{1,0:T(8,128)(2,1)}, bf16[512,2048]{1,0:T(8,128)(2,1)}, u32[]{:S(2)}, u32[]{:S(2)}) collective-permute-start(bf16[512,2048]{1,0:T(8,128)(2,1)} %get-tuple-element.129), channel_id=1, source_target_pairs={{0,8},{8,0},{1,9},{9,1},{2,10},{10,2},{3,11},{11,3},{4,12},{12,4},... | collective-permute-start | bytes 6291464 | tf_op jit(solution)/shard_map/ppermute | solution.py:637
  128.4 22.0 %copy-start.1 = (f32[4480,128]{1,0:T(8,128)S(1)}, f32[4480,128]{1,0:T(8,128)}, u32[]{:S(2)}) copy-start(f32[4480,128]{1,0:T(8,128)} %copy-done) | copy-start | bytes 6881284
  128.4 49.4 %all-to-all-start = ((bf16[64,8,2048]{2,1,0:T(8,128)(2,1)}), bf16[64,8,2048]{2,1,0:T(8,128)(2,1)}, u32[]{:S(2)}, u32[]{:S(2)}) async-start(bf16[64,8,2048]{2,1,0:T(8,128)(2,1)} %shard_map.176), calls=%async_computation | async-start | bytes 4194304 | tf_op jit(solution)/shard_map/all_to_all | solution.py:664
  177.9 37.9 %all-to-all-start.1 = ((bf16[64,8,2304]{2,1,0:T(8,128)(2,1)}), bf16[64,8,2304]{2,1,0:T(8,128)(2,1)S(1)}, u32[]{:S(2)}, u32[]{:S(2)}) async-start(bf16[64,8,2304]{2,1,0:T(8,128)(2,1)} %shard_map.181), calls=%async_computation.1 | async-start | bytes 4718592 | tf_op jit(solution)/shard_map/all_to_all | solution.py:664
  217.5 39.9 %copy-start.32 = (bf16[96,512]{1,0:T(8,128)(2,1)S(1)}, bf16[96,512]{1,0:T(8,128)(2,1)}, u32[]{:S(2)}) copy-start(bf16[96,512]{1,0:T(8,128)(2,1)} %copy-done.31) | copy-start | bytes 294916
  217.6 45.9 %copy-start.4 = (f32[4480,128]{1,0:T(8,128)S(1)}, f32[4480,128]{1,0:T(8,128)}, u32[]{:S(2)}) copy-start(f32[4480,128]{1,0:T(8,128)} %copy-done.2) | copy-start | bytes 6881284
  254.7 14.0 %copy-start.13 = (f32[2,7,7,512]{3,0,2,1:T(2,128)S(1)}, f32[2,7,7,512]{3,0,2,1:T(2,128)}, u32[]{:S(2)}) copy-start(f32[2,7,7,512]{3,0,2,1:T(2,128)} %param.13) | copy-start | bytes 602116
  254.7 25.6 %collective-permute-start.26 = (bf16[32,8,4352]{2,1,0:T(8,128)(2,1)S(1)}, bf16[32,8,4352]{2,1,0:T(8,128)(2,1)S(1)}, u32[]{:S(2)}, u32[]{:S(2)}) collective-permute-start(bf16[32,8,4352]{2,1,0:T(8,128)(2,1)S(1)} %all_to_all.15.ref.whole0.whole1), channel_id=1, source_target_pairs={{0,8},{8,0},{1,9},{9,1},{2,10},{10,2},{3,11},{11,3},{4,12},{12,4},... | collective-permute-start | bytes 6684680 | tf_op jit(solution)/shard_map/ppermute | solution.py:637
  257.5 4.1 %collective-permute-start.20 = (bf16[96,512]{1,0:T(8,128)(2,1)S(1)}, bf16[96,512]{1,0:T(8,128)(2,1)S(1)}, u32[]{:S(2)}, u32[]{:S(2)}) collective-permute-start(bf16[96,512]{1,0:T(8,128)(2,1)S(1)} %copy-done.32), channel_id=1, source_target_pairs={{0,8},{16,24},{32,40},{48,56},{64,72},{80,88},{96,104},{112,120},{... | collective-permute-start | bytes 294920 | tf_op jit(solution)/shard_map/ppermute | solution.py:625
  257.6 5.9 %collective-permute-start.21 = (bf16[96,512]{1,0:T(8,128)(2,1)S(1)}, bf16[96,512]{1,0:T(8,128)(2,1)S(1)}, u32[]{:S(2)}, u32[]{:S(2)}) collective-permute-start(bf16[96,512]{1,0:T(8,128)(2,1)S(1)} %get-tuple-element.117), channel_id=1, source_target_pairs={{8,16},{24,32},{40,48},{56,64},{72,80},{88,96},{104,112},{16,8},{3... | collective-permute-start | bytes 294920 | tf_op jit(solution)/shard_map/ppermute | solution.py:626
  264.1 3.4 %collective-permute-start.22 = (bf16[336,128]{1,0:T(8,128)(2,1)S(1)}, bf16[336,128]{1,0:T(8,128)(2,1)S(1)}, u32[]{:S(2)}, u32[]{:S(2)}) collective-permute-start(bf16[336,128]{1,0:T(8,128)(2,1)S(1)} %get-tuple-element.118), channel_id=1, source_target_pairs={{0,2},{4,6},{2,0},{6,4},{1,3},{5,7},{3,1},{7,5},{8,10},{12,14},{10... | collective-permute-start | bytes 258056 | tf_op jit(solution)/shard_map/ppermute | solution.py:631
  264.4 3.2 %collective-permute-start.23 = (bf16[336,128]{1,0:T(8,128)(2,1)S(1)}, bf16[336,128]{1,0:T(8,128)(2,1)S(1)}, u32[]{:S(2)}, u32[]{:S(2)}) collective-permute-start(bf16[336,128]{1,0:T(8,128)(2,1)S(1)} %get-tuple-element.119), channel_id=1, source_target_pairs={{2,4},{4,2},{3,5},{5,3},{10,12},{12,10},{11,13},{13,11},{18,20},{2... | collective-permute-start | bytes 258056 | tf_op jit(solution)/shard_map/ppermute | solution.py:632
  (18 other events, 60.5 us)

commit v2 on v1

--- a/solution.py
+++ b/solution.py
@@ -344,25 +344,33 @@
             ).astype(BF16)
 
 
-def taps_body(seen, grads, out):
-    for p in range(7):
-
-        def step(n, sums, p=p):
-            row = n // 4
-            col = (n % 4) * 8
-            base = pl.multiple_of(((row + p) * WIDE + col) * 8, 8)
-            home = pl.multiple_of(((row + 3) * WIDE + col + 3) * 8, 8)
-            near = [seen[pl.ds(base + 8 * k, 8), :] for k in range(14)]
+def taps_body(seen, grads, out, wide):
+    def line(p, carry):
+        def step(row, sums):
             sums = list(sums)
-            for m in range(8):
-                grad = grads[pl.ds(home + 8 * m, 8), :]
-                for q in range(7):
-                    sums[q] = sums[q] + near[m + q] * grad
+            for part in range(4):
+                col = part * 8
+                base = pl.multiple_of(((row + p) * WIDE + col) * 8, 8)
+                home = pl.multiple_of(((row + 3) * WIDE + col + 3) * 8, 8)
+                near = [seen[pl.ds(base + 8 * k, 8), :] for k in range(14)]
+                for m in range(8):
+                    grad = grads[pl.ds(home + 8 * m, 8), :]
+                    for q in range(7):
+                        spot = q + 7 * (m % 2)
+                        sums[spot] = sums[spot] + near[m + q] * grad
             return tuple(sums)
 
-        sums = lax.fori_loop(0, 32, step, tuple(jnp.zeros((8, 128), F32) for _ in range(7)))
+        zero = jnp.zeros((8, 128), F32)
+        sums = lax.fori_loop(0, 8, step, (zero,) * 14)
+        base = pl.multiple_of(p * 56, 8)
         for q in range(7):
-            out[(p * 7 + q) * 4 : (p * 7 + q + 1) * 4, :] = sums[q][0:4] + sums[q][4:8]
+            wide[pl.ds(base + 8 * q, 8), :] = sums[q] + sums[q + 7]
+        return carry
+
+    lax.fori_loop(0, 7, line, 0)
+    for tap in range(49):
+        total = wide[tap * 8 : tap * 8 + 8, :]
+        out[tap * 4 : tap * 4 + 4, :] = total[0:4] + total[4:8]
 
 
 def up_body(
@@ -550,7 +558,9 @@
 
 
 def tap_grads(seen, grads):
-    return call(taps_body, [((49 * 4, 128), F32)], 2, 40_000_000)(seen, grads)[0]
+    return call(taps_body, [((49 * 4, 128), F32)], 2, 40_000_000, [TAPS])(
+        seen, grads
+    )[0]
 
 
 def upstream(k, place, slab, edge_near, edge_far, near, far, kernel, u, dtype, later=()):

time: 288 us -> 288 us (level)
  waiting for transfers between devices: 69.8 us -> 74.6 us
  Pallas kernels: 88.6 us -> 83.9 us
    pallas_call x21, Pallas kernels: 81.2 us -> 76.5 us  [run(): made(*(pltpu.with_memory_space_constraint(arg, pltpu.HBM) if n in far els...]
    all_to_all x2, waiting for transfers between devices: 38.2 us -> 43 us  [send_grads(): return lax.all_to_all(pair, ('dp', *SPACE), 0, 0, tiled=True)]
  transfers between devices with their start and end apart: 29 -> 29, of which waited for: 13 -> 13; matrix products, arithmetic and copies ran while one was open for 0% -> 0% of each run, Pallas kernels for 24% -> 23%
where the time goes in v2:
time: 288 us; the launch traced here: 285 us
  Pallas kernels  83.9 us (29%)
  starting transfers between devices  77.7 us (27%)
  waiting for transfers between devices  74.6 us (26%)
  blocking collectives  37.2 us (13%)
  local copies, waits for them, and re-layouts  9.92 us (3%)
    pallas_call x21, Pallas kernels, run(): made(*(pltpu.with_memory_space_constraint(arg, pltpu.HBM) if n in far els...  76.5 us
    all_to_all x2, waiting for transfers between devices, send_grads(): return lax.all_to_all(pair, ('dp', *SPACE), 0, 0, tiled=True)  43 us
    all_to_all x1, blocking collectives, per_device(): whole = lax.all_to_all(copies, SPACE, 0, 0, tiled=True)  37.2 us
    all_to_all x2, starting transfers between devices, send_grads(): return lax.all_to_all(pair, ('dp', *SPACE), 0, 0, tiled=True)  30 us
    ppermute x4, starting transfers between devices, from_rows(): far = lax.ppermute(far, RANKS, pairs(1, 16))  15.3 us
    ppermute x4, waiting for transfers between devices, around_x(): lax.ppermute(value, ('xh', 'dp'), [(i, (i + step) % 4) for i in range(4)])  14.4 us
    ppermute x4, starting transfers between devices, from_columns(): near = lax.ppermute(near, 'z', pairs(0, 4))  13.1 us
    ppermute x7, starting transfers between devices, swapped(): return lax.ppermute(value, axis, [(0, 1), (1, 0)])  9.42 us
  transfers between devices with their start and end apart: 29, of which 13 were waited for; matrix products, arithmetic and copies ran while one was open for 0% of the time, Pallas kernels for 23%

profile of v2, /device:TPU:1, one launch (start us, length us, event | category | flops | bytes accessed | tf_op | source)
XLA Modules:
  0.0 284.5 jit_solution(84975289484298869)
XLA Ops:
  0.7 2.4 constant_dynamic-slice_fusion.1
  3.1 2.1 collective-permute-start.4
  6.1 1.4 collective-permute-start.6
  7.6 2.5 collective-permute-start.14
  10.1 7.9 %collective-permute-done.4.refs_4_ = bf16[1,128,2048]{2,1,0:T(8,128)(2,1)} collective-permute-done((bf16[1,128,2048]{2,1,0:T(8,128)(2,1)}, bf16[1,128,2048]{2,1,0:T(8,128)(2,1)}, u32[]{:S(2)}, u32[]{:S(2)}) %collective-permute-start.4) | collective-permute-done | bytes 524320 | tf_op jit(solution)/shard_map/ppermute | solution.py:651
  18.1 2.8 collective-permute-start.5
  22.7 6.4 %collective-permute-done.12.refs_4_ = bf16[1,128,2048]{2,1,0:T(8,128)(2,1)S(1)} collective-permute-done((bf16[1,128,2048]{2,1,0:T(8,128)(2,1)}, bf16[1,128,2048]{2,1,0:T(8,128)(2,1)S(1)}, u32[]{:S(2)}, u32[]{:S(2)}) %collective-permute-start.12) | collective-permute-done | bytes 524320 | tf_op jit(solution)/shard_map/ppermute | solution.py:651
  29.2 1.6 collective-permute-start.13
  31.8 3.1 %collective-permute-start.1 = (bf16[96,512]{1,0:T(8,128)(2,1)S(1)}, bf16[96,512]{1,0:T(8,128)(2,1)S(1)}, u32[]{:S(2)}, u32[]{:S(2)}) collective-permute-start(bf16[96,512]{1,0:T(8,128)(2,1)S(1)} %get-tuple-element.78), channel_id=1, source_target_pairs={{8,16},{24,32},{40,48},{56,64},{72,80},{88,96},{104,112},{16,8},{3... | collective-permute-start | bytes 294920 | tf_op jit(solution)/shard_map/ppermute | solution.py:636
  34.9 2.8 collective-permute-done.1.edge_far
  38.6 1.7 collective-permute-start.2
  40.3 1.9 collective-permute-done.2.near
  42.9 7.2 %shard_map.164 = (f32[4480,128]{1,0:T(8,128)}, bf16[512,512]{1,0:T(8,128)(2,1)S(1)}, f32[512,512]{1,0:T(8,128)}, f32[512,128]{1,0:T(8,128)}) custom-call(s32[4]{0:T(128)S(1)} %pad_add_fusion.place.refs_0_, f32[4480,128]{1,0:T(8,128)S(1)} %get-tuple-element.79.old, bf16[336,128]{1,0:T(8,128)(2,1)S(1)} %collective-permute-done.2.near, ...), custom_call_target="tpu_custom_call" | custom-call | flops 40000000 | bytes 4000000 | tf_op jit(solution)/shard_map/pallas_call | solution.py:54
  50.1 1.6 copy-done.7
  51.7 7.4 %shard_map.165 = (bf16[512,512]{1,0:T(8,128)(2,1)S(1)}, bf16[96,512]{1,0:T(8,128)(2,1)S(1)}, bf16[96,512]{1,0:T(8,128)(2,1)S(1)}, bf16[512,2048]{1,0:T(8,128)(2,...) custom-call(s32[4]{0:T(128)S(1)} %pad_add_fusion.place.refs_0_, ...), custom_call_target="tpu_custom_call" | custom-call | flops 60000000 | bytes 4000000 | tf_op jit(solution)/shard_map/pallas_call | solution.py:54
  59.3 4.8 %collective-permute-start.9 = (bf16[96,512]{1,0:T(8,128)(2,1)S(1)}, bf16[96,512]{1,0:T(8,128)(2,1)S(1)}, u32[]{:S(2)}, u32[]{:S(2)}) collective-permute-start(bf16[96,512]{1,0:T(8,128)(2,1)S(1)} %get-tuple-element.85), channel_id=1, source_target_pairs={{8,16},{24,32},{40,48},{56,64},{72,80},{88,96},{104,112},{16,8},{3... | collective-permute-start | bytes 294920 | tf_op jit(solution)/shard_map/ppermute | solution.py:636
  64.1 2.3 collective-permute-done.9.edge_far
  67.2 7.5 %collective-permute-start.10 = (bf16[336,128]{1,0:T(8,128)(2,1)S(1)}, bf16[336,128]{1,0:T(8,128)(2,1)S(1)}, u32[]{:S(2)}, u32[]{:S(2)}) collective-permute-start(bf16[336,128]{1,0:T(8,128)(2,1)S(1)} %get-tuple-element.87), channel_id=1, source_target_pairs={{0,2},{4,6},{2,0},{6,4},{1,3},{5,7},{3,1},{7,5},{8,10},{12,14},{10... | collective-permute-start | bytes 258056 | tf_op jit(solution)/shard_map/ppermute | solution.py:641
  76.6 5.6 %shard_map.167 = (f32[4480,128]{1,0:T(8,128)S(1)}, bf16[512,512]{1,0:T(8,128)(2,1)S(1)}, f32[512,512]{1,0:T(8,128)S(1)}, f32[512,128]{1,0:T(8,128)S(1)}) custom-call(s32[4]{0:T(128)S(1)} %pad_add_fusion.place.refs_0_, f32[4480,128]{1,0:T(8,128)S(1)} %get-tuple-element.86.old, bf16[336,128]{1,0:T(8,128)(2,1)S(1)} %collective-permute-done.10.near, ...), custom_call_target="tpu_custom_call" | custom-call | flops 40000000 | bytes 4000000 | tf_op jit(solution)/shard_map/pallas_call | solution.py:54
  82.3 7.2 %shard_map.168 = (bf16[512,512]{1,0:T(8,128)(2,1)}, bf16[96,512]{1,0:T(8,128)(2,1)}, bf16[96,512]{1,0:T(8,128)(2,1)}, bf16[512,2048]{1,0:T(8,128)(2,1)S(1)}, bf1...) custom-call(s32[4]{0:T(128)S(1)} %pad_add_fusion.place.refs_0_, ...), custom_call_target="tpu_custom_call" | custom-call | flops 60000000 | bytes 4000000 | tf_op jit(solution)/shard_map/pallas_call | solution.py:54
  89.5 3.5 %shard_map.169 = (bf16[512,512]{1,0:T(8,128)(2,1)S(1)}, bf16[512,2048]{1,0:T(8,128)(2,1)S(1)}, f32[4480,128]{1,0:T(8,128)S(1)}, bf16[96,512]{1,0:T(8,128)(2,1)S(...) custom-call(s32[4]{0:T(128)S(1)} %pad_add_fusion.place.refs_0_, ...), custom_call_target="tpu_custom_call" | custom-call | flops 60000000 | bytes 4000000 | tf_op jit(solution)/shard_map/pallas_call | solution.py:54
  93.1 3.0 %shard_map.175 = (bf16[512,2048]{1,0:T(8,128)(2,1)S(1)}, bf16[512,2048]{1,0:T(8,128)(2,1)S(1)}) custom-call(s32[4]{0:T(128)S(1)} %pad_add_fusion.place.refs_0_, bf16[512,512]{1,0:T(8,128)(2,1)S(1)} %get-tuple-element.89.refs_2_.normal, bf16[512,512]{1,0:T(8,128)(2,1)S(1)} %get-tuple-element.120.low, bf16[512,2048]{1,0:T(8,128)(2,1)S(1)} %get-tuple-element.121.act, ...), custom_call_target="tpu_custom_call" | custom-call | flops 50000000 | bytes 4000000 | tf_op jit(solution)/shard_map/pallas_call | solution.py:54
  96.7 4.8 %collective-permute-start.17 = (bf16[96,512]{1,0:T(8,128)(2,1)S(1)}, bf16[96,512]{1,0:T(8,128)(2,1)S(1)}, u32[]{:S(2)}, u32[]{:S(2)}) collective-permute-start(bf16[96,512]{1,0:T(8,128)(2,1)S(1)} %get-tuple-element.99), channel_id=1, source_target_pairs={{8,16},{24,32},{40,48},{56,64},{72,80},{88,96},{104,112},{16,8},{3... | collective-permute-start | bytes 294920 | tf_op jit(solution)/shard_map/ppermute | solution.py:636
  101.6 2.3 collective-permute-done.17.edge_far
  104.4 3.6 %collective-permute-start.18 = (bf16[336,128]{1,0:T(8,128)(2,1)S(1)}, bf16[336,128]{1,0:T(8,128)(2,1)S(1)}, u32[]{:S(2)}, u32[]{:S(2)}) collective-permute-start(bf16[336,128]{1,0:T(8,128)(2,1)S(1)} %get-tuple-element.100), channel_id=1, source_target_pairs={{0,2},{4,6},{2,0},{6,4},{1,3},{5,7},{3,1},{7,5},{8,10},{12,14},{10... | collective-permute-start | bytes 258056 | tf_op jit(solution)/shard_map/ppermute | solution.py:641
  110.6 7.6 %shard_map.171 = (f32[512,512]{1,0:T(8,128)S(1)}, f32[512,512]{1,0:T(8,128)S(1)}, bf16[512,2048]{1,0:T(8,128)(2,1)S(1)}, f32[512,512]{1,0:T(8,128)S(1)}, f32[512...) custom-call(s32[4]{0:T(128)S(1)} %pad_add_fusion.place.refs_0_, ...), custom_call_target="tpu_custom_call" | custom-call | flops 40000000 | bytes 4000000 | tf_op jit(solution)/shard_map/pallas_call | solution.py:54
  118.2 3.4 %shard_map.172 = (bf16[512,512]{1,0:T(8,128)(2,1)S(1)}, bf16[512,2048]{1,0:T(8,128)(2,1)S(1)}, f32[4480,128]{1,0:T(8,128)S(1)}, bf16[96,512]{1,0:T(8,128)(2,1)S(...) custom-call(s32[4]{0:T(128)S(1)} %pad_add_fusion.place.refs_0_, ...), custom_call_target="tpu_custom_call" | custom-call | flops 60000000 | bytes 4000000 | tf_op jit(solution)/shard_map/pallas_call | solution.py:54
  121.7 3.7 %shard_map.178 = (bf16[512,2048]{1,0:T(8,128)(2,1)S(1)}, bf16[512,2048]{1,0:T(8,128)(2,1)}) custom-call(s32[4]{0:T(128)S(1)} %pad_add_fusion.place.refs_0_, bf16[512,512]{1,0:T(8,128)(2,1)S(1)} %get-tuple-element.82.refs_2_.normal, bf16[512,512]{1,0:T(8,128)(2,1)S(1)} %get-tuple-element.125.low, bf16[512,2048]{1,0:T(8,128)(2,1)S(1)} %copy-done.17, ...), custom_call_target="tpu_custom_call" | custom-call | flops 50000000 | bytes 4000000 | tf_op jit(solution)/shard_map/pallas_call | solution.py:54
  126.8 1.6 shard_map.176
  128.4 22.0 %all-to-all-start = ((bf16[64,8,2048]{2,1,0:T(8,128)(2,1)}), bf16[64,8,2048]{2,1,0:T(8,128)(2,1)}, u32[]{:S(2)}, u32[]{:S(2)}) async-start(bf16[64,8,2048]{2,1,0:T(8,128)(2,1)} %shard_map.176), calls=%async_computation | async-start | bytes 4194304 | tf_op jit(solution)/shard_map/all_to_all | solution.py:674
  150.4 1.6 copy-done.16
  152.1 3.6 %shard_map.180.refs_3_ = f32[196,128]{1,0:T(8,128)S(1)} custom-call(f32[4480,128]{1,0:T(8,128)S(1)} %copy-done.16, f32[4480,128]{1,0:T(8,128)S(1)} %copy-done.1), custom_call_target="tpu_custom_call" | custom-call | flops 40000000 | bytes 4000000 | tf_op jit(solution)/shard_map/pallas_call | solution.py:54
  155.8 3.7 %shard_map.179.refs_0_ = f32[196,128]{1,0:T(8,128)S(1)} custom-call(f32[4480,128]{1,0:T(8,128)S(1)} %copy-done.14, f32[4480,128]{1,0:T(8,128)S(1)} %copy-done.3), custom_call_target="tpu_custom_call" | custom-call | flops 40000000 | bytes 4000000 | tf_op jit(solution)/shard_map/pallas_call | solution.py:54
  159.4 3.2 %shard_map.181 = bf16[64,8,2304]{2,1,0:T(8,128)(2,1)} custom-call(bf16[512,2048]{1,0:T(8,128)(2,1)S(1)} %copy-done.19, bf16[512,2048]{1,0:T(8,128)(2,1)} %collective-permute-done.25.got, f32[196,128]{1,0:T(8,128)S(1)} %shard_map.179.refs_0_, f32[8,512]{1,0:T(8,128)S(1)} %get-tuple-element.131.refs_1_, f32[1,2048]{1,0:T(1,128)S(1)} %get-tuple-element.132.refs_2_, ...), custom_call_target="tpu_custom_call" | custom-call | flops 2000000 | bytes 4000000 | tf_op jit(solution)/shard_map/pallas_call | solution.py:54
  162.6 15.2 %all-to-all-done.pieces = bf16[64,8,2048]{2,1,0:T(8,128)(2,1)} async-done(((bf16[64,8,2048]{2,1,0:T(8,128)(2,1)}), bf16[64,8,2048]{2,1,0:T(8,128)(2,1)}, u32[]{:S(2)}, u32[]{:S(2)}) %all-to-all-start) | async-done | bytes 2097184 | tf_op jit(solution)/shard_map/all_to_all | solution.py:674
  177.9 8.0 %all-to-all-start.1 = ((bf16[64,8,2304]{2,1,0:T(8,128)(2,1)}), bf16[64,8,2304]{2,1,0:T(8,128)(2,1)S(1)}, u32[]{:S(2)}, u32[]{:S(2)}) async-start(bf16[64,8,2304]{2,1,0:T(8,128)(2,1)} %shard_map.181), calls=%async_computation.1 | async-start | bytes 4718592 | tf_op jit(solution)/shard_map/all_to_all | solution.py:674
  185.9 2.1 shard_map.177.other
  188.0 27.8 %all-to-all-done.1.pieces = bf16[64,8,2304]{2,1,0:T(8,128)(2,1)S(1)} async-done(((bf16[64,8,2304]{2,1,0:T(8,128)(2,1)}), bf16[64,8,2304]{2,1,0:T(8,128)(2,1)S(1)}, u32[]{:S(2)}, u32[]{:S(2)}) %all-to-all-start.1) | async-done | bytes 2359328 | tf_op jit(solution)/shard_map/all_to_all | solution.py:674
  215.7 1.8 shard_map.182
  217.6 37.2 %all_to_all.15.ref.whole0.whole1 = bf16[32,8,4352]{2,1,0:T(8,128)(2,1)S(1)} all-to-all(bf16[32,8,4352]{2,1,0:T(8,128)(2,1)} %shard_map.182), channel_id=1, replica_groups=mesh['xh'=2,'y'=4,'core'=2,'z'=4,'dp'=2] {'xh','y','z'}, dimensions={0} | all-to-all | bytes 4456448 | tf_op jit(solution)/shard_map/all_to_all | solution.py:736
  254.7 2.7 collective-permute-start.26
  257.6 2.5 collective-permute-start.21
  260.1 1.5 collective-permute-done.20.edge_near
  261.6 1.9 collective-permute-done.21.edge_far
  265.0 2.5 collective-permute-done.22.near
  268.8 8.3 %shard_map.174 = bf16[512,512]{1,0:T(8,128)(2,1)} custom-call(s32[4]{0:T(128)S(1)} %pad_add_fusion.place.refs_0_, f32[4480,128]{1,0:T(8,128)} %copy-done.2, bf16[96,512]{1,0:T(8,128)(2,1)} %copy-done.23, bf16[96,512]{1,0:T(8,128)(2,1)} %copy-done.24, bf16[336,128]{1,0:T(8,128)(2,1)} %copy-done.35, bf16[336,128]{1,0:T(8,128)(2,1)} %copy-done.36, ...), custom_call_target="tpu_custom_call" | custom-call | flops 40000000 | bytes 4000000 | tf_op jit(solution)/shard_map/pallas_call | solution.py:54
  277.1 3.3 %shard_map.183 = (f32[2,256,2048]{2,1,0:T(8,128)}, f32[2,2048,256]{2,1,0:T(8,128)}) custom-call(s32[4]{0:T(128)S(1)} %pad_add_fusion.place.refs_0_, bf16[32,8,4352]{2,1,0:T(8,128)(2,1)S(1)} %all_to_all.15.ref.whole0.whole1), custom_call_target="tpu_custom_call" | custom-call | flops 5000000 | bytes 6000000 | tf_op jit(solution)/shard_map/pallas_call | solution.py:581
  281.3 3.3 %shard_map.184 = (f32[2,256,2048]{2,1,0:T(8,128)}, f32[2,2048,256]{2,1,0:T(8,128)}) custom-call(s32[4]{0:T(128)S(1)} %pad_add_fusion.place.refs_0_, bf16[32,8,4352]{2,1,0:T(8,128)(2,1)S(1)} %collective-permute-done.26.ref.mate0.mate1, f32[2,256,2048]{2,1,0:T(8,128)} %get-tuple-element.136.refs_0_, ...), custom_call_target="tpu_custom_call", output_to_operand_aliasing={{0}: (2, {}), {1}: (3, {})} | custom-call | flops 5000000 | bytes 6000000 | tf_op jit(solution)/shard_map/pallas_call | solution.py:581
  (112 shorter events, 17.1 us)
Async XLA Ops:
  0.6 21.4 %copy-start.9 = (bf16[1,16,32,512]{3,2,1,0:T(8,128)(2,1)S(1)}, bf16[1,16,32,512]{3,2,1,0:T(8,128)(2,1)}, u32[]{:S(2)}) copy-start(bf16[1,16,32,512]{3,2,1,0:T(8,128)(2,1)} %param.11) | copy-start | bytes 1572868
  3.1 39.8 %copy-start.11 = (f32[2,7,7,512]{3,0,2,1:T(2,128)S(1)}, f32[2,7,7,512]{3,0,2,1:T(2,128)}, u32[]{:S(2)}) copy-start(f32[2,7,7,512]{3,0,2,1:T(2,128)} %param.13) | copy-start | bytes 602116
  3.1 39.8 %copy-start.26 = (f32[2,512]{1,0:T(2,128)S(1)}, f32[2,512]{1,0:T(2,128)}, u32[]{:S(2)}) copy-start(f32[2,512]{1,0:T(2,128)} %gain.7) | copy-start | bytes 12292
  3.1 39.8 %copy-start.28 = (f32[2,512]{1,0:T(2,128)S(1)}, f32[2,512]{1,0:T(2,128)}, u32[]{:S(2)}) copy-start(f32[2,512]{1,0:T(2,128)} %bias.3) | copy-start | bytes 12292
  3.1 39.8 %copy-start.29 = (f32[2,512]{1,0:T(2,128)S(1)}, f32[2,512]{1,0:T(2,128)}, u32[]{:S(2)}) copy-start(f32[2,512]{1,0:T(2,128)} %shift.3) | copy-start | bytes 12292
  3.1 14.9 %collective-permute-start.4 = (bf16[1,128,2048]{2,1,0:T(8,128)(2,1)}, bf16[1,128,2048]{2,1,0:T(8,128)(2,1)}, u32[]{:S(2)}, u32[]{:S(2)}) collective-permute-start(bf16[1,128,2048]{2,1,0:T(8,128)(2,1)} %get-tuple-element.146), channel_id=1, source_target_pairs={{0,1},{1,64},{64,65},{65,0},{2,3},{3,66},{66,67},{67,2},{4,5},{5,6... | collective-permute-start | bytes 1572872 | tf_op jit(solution)/shard_map/ppermute | solution.py:651
  6.1 44.0 %copy-start.5 = (bf16[2,256,2048]{2,1,0:T(8,128)(2,1)S(1)}, bf16[2,256,2048]{2,1,0:T(8,128)(2,1)}, u32[]{:S(2)}) copy-start(bf16[2,256,2048]{2,1,0:T(8,128)(2,1)} %refs_3_.3) | copy-start | bytes 6291460
  6.1 44.0 %copy-start.25 = (f32[2,2048]{1,0:T(2,128)S(1)}, f32[2,2048]{1,0:T(2,128)}, u32[]{:S(2)}) copy-start(f32[2,2048]{1,0:T(2,128)} %refs_9_.3) | copy-start | bytes 49156
  6.1 44.0 %copy-start.27 = (f32[2,512]{1,0:T(2,128)S(1)}, f32[2,512]{1,0:T(2,128)}, u32[]{:S(2)}) copy-start(f32[2,512]{1,0:T(2,128)} %scale.3) | copy-start | bytes 12292
  6.1 44.1 %copy-start.30 = (f32[2,512]{1,0:T(2,128)S(1)}, f32[2,512]{1,0:T(2,128)}, u32[]{:S(2)}) copy-start(f32[2,512]{1,0:T(2,128)} %refs_10_.3) | copy-start | bytes 12292
  6.1 14.8 %collective-permute-start.6 = (bf16[1,1024,256]{2,1,0:T(8,128)(2,1)S(1)}, bf16[1,1024,256]{2,1,0:T(8,128)(2,1)}, u32[]{:S(2)}, u32[]{:S(2)}) collective-permute-start(bf16[1,1024,256]{2,1,0:T(8,128)(2,1)S(1)} %get-tuple-element.144), channel_id=1, source_target_pairs={{0,65},{1,0},{64,1},{65,64},{2,67},{3,2},{66,3},{67,66},{4,69},{5,... | collective-permute-start | bytes 1572872 | tf_op jit(solution)/shard_map/ppermute | solution.py:651
  7.4 21.7 %collective-permute-start.12 = (bf16[1,128,2048]{2,1,0:T(8,128)(2,1)}, bf16[1,128,2048]{2,1,0:T(8,128)(2,1)S(1)}, u32[]{:S(2)}, u32[]{:S(2)}) collective-permute-start(bf16[1,128,2048]{2,1,0:T(8,128)(2,1)} %get-tuple-element.145), channel_id=1, source_target_pairs={{0,1},{1,64},{64,65},{65,0},{2,3},{3,66},{66,67},{67,2},{4,5},{5,6... | collective-permute-start | bytes 1572872 | tf_op jit(solution)/shard_map/ppermute | solution.py:651
  7.6 23.2 %collective-permute-start.14 = (bf16[1,1024,256]{2,1,0:T(8,128)(2,1)}, bf16[1,1024,256]{2,1,0:T(8,128)(2,1)}, u32[]{:S(2)}, u32[]{:S(2)}) collective-permute-start(bf16[1,1024,256]{2,1,0:T(8,128)(2,1)} %get-tuple-element.143), channel_id=1, source_target_pairs={{0,65},{1,0},{64,1},{65,64},{2,67},{3,2},{66,3},{67,66},{4,69},{5,... | collective-permute-start | bytes 1572872 | tf_op jit(solution)/shard_map/ppermute | solution.py:651
  18.1 32.0 %collective-permute-start.5 = (bf16[1,128,2048]{2,1,0:T(8,128)(2,1)}, bf16[1,128,2048]{2,1,0:T(8,128)(2,1)}, u32[]{:S(2)}, u32[]{:S(2)}) collective-permute-start(bf16[1,128,2048]{2,1,0:T(8,128)(2,1)} %collective-permute-done.4.refs_4_), channel_id=1, source_target_pairs={{0,8},{8,0},{1,9},{9,1},{2,10},{10,2},{3,11},{11,3},{4,12},{12,4},... | collective-permute-start | bytes 1572872 | tf_op jit(solution)/shard_map/ppermute | solution.py:647
  20.9 29.2 %collective-permute-start.7 = (bf16[1,1024,256]{2,1,0:T(8,128)(2,1)}, bf16[1,1024,256]{2,1,0:T(8,128)(2,1)}, u32[]{:S(2)}, u32[]{:S(2)}) collective-permute-start(bf16[1,1024,256]{2,1,0:T(8,128)(2,1)} %collective-permute-done.6.refs_7_), channel_id=1, source_target_pairs={{0,8},{8,0},{1,9},{9,1},{2,10},{10,2},{3,11},{11,3},{4,12},{12,4},... | collective-permute-start | bytes 1572872 | tf_op jit(solution)/shard_map/ppermute | solution.py:647
  22.7 9.2 %collective-permute-start = (bf16[96,512]{1,0:T(8,128)(2,1)S(1)}, bf16[96,512]{1,0:T(8,128)(2,1)S(1)}, u32[]{:S(2)}, u32[]{:S(2)}) collective-permute-start(bf16[96,512]{1,0:T(8,128)(2,1)S(1)} %get-tuple-element.77), channel_id=1, source_target_pairs={{0,8},{16,24},{32,40},{48,56},{64,72},{80,88},{96,104},{112,120},{... | collective-permute-start | bytes 294920 | tf_op jit(solution)/shard_map/ppermute | solution.py:635
  29.2 53.0 %collective-permute-start.13 = (bf16[1,128,2048]{2,1,0:T(8,128)(2,1)S(1)}, bf16[1,128,2048]{2,1,0:T(8,128)(2,1)S(1)}, u32[]{:S(2)}, u32[]{:S(2)}) collective-permute-start(bf16[1,128,2048]{2,1,0:T(8,128)(2,1)S(1)} %collective-permute-done.12.refs_4_), channel_id=1, source_target_pairs={{0,8},{8,0},{1,9},{9,1},{2,10},{10,2},{3,11},{11,3},{4,12},{12,4},... | collective-permute-start | bytes 1572872 | tf_op jit(solution)/shard_map/ppermute | solution.py:647
  30.8 51.4 %collective-permute-start.15 = (bf16[1,1024,256]{2,1,0:T(8,128)(2,1)}, bf16[1,1024,256]{2,1,0:T(8,128)(2,1)S(1)}, u32[]{:S(2)}, u32[]{:S(2)}) collective-permute-start(bf16[1,1024,256]{2,1,0:T(8,128)(2,1)} %collective-permute-done.14.refs_7_), channel_id=1, source_target_pairs={{0,8},{8,0},{1,9},{9,1},{2,10},{10,2},{3,11},{11,3},{4,12},{12,4},... | collective-permute-start | bytes 1572872 | tf_op jit(solution)/shard_map/ppermute | solution.py:647
  31.8 5.9 %collective-permute-start.1 = (bf16[96,512]{1,0:T(8,128)(2,1)S(1)}, bf16[96,512]{1,0:T(8,128)(2,1)S(1)}, u32[]{:S(2)}, u32[]{:S(2)}) collective-permute-start(bf16[96,512]{1,0:T(8,128)(2,1)S(1)} %get-tuple-element.78), channel_id=1, source_target_pairs={{8,16},{24,32},{40,48},{56,64},{72,80},{88,96},{104,112},{16,8},{3... | collective-permute-start | bytes 294920 | tf_op jit(solution)/shard_map/ppermute | solution.py:636
  38.6 3.6 %collective-permute-start.2 = (bf16[336,128]{1,0:T(8,128)(2,1)S(1)}, bf16[336,128]{1,0:T(8,128)(2,1)S(1)}, u32[]{:S(2)}, u32[]{:S(2)}) collective-permute-start(bf16[336,128]{1,0:T(8,128)(2,1)S(1)} %get-tuple-element.80), channel_id=1, source_target_pairs={{0,2},{4,6},{2,0},{6,4},{1,3},{5,7},{3,1},{7,5},{8,10},{12,14},{10... | collective-permute-start | bytes 258056 | tf_op jit(solution)/shard_map/ppermute | solution.py:641
  42.2 0.7 collective-permute-start.3
  59.2 23.1 %copy-start.8 = (bf16[2,2048,256]{2,1,0:T(8,128)(2,1)S(1)}, bf16[2,2048,256]{2,1,0:T(8,128)(2,1)}, u32[]{:S(2)}) copy-start(bf16[2,2048,256]{2,1,0:T(8,128)(2,1)} %refs_6_.3) | copy-start | bytes 6291460
  59.2 4.9 %collective-permute-start.8 = (bf16[96,512]{1,0:T(8,128)(2,1)S(1)}, bf16[96,512]{1,0:T(8,128)(2,1)S(1)}, u32[]{:S(2)}, u32[]{:S(2)}) collective-permute-start(bf16[96,512]{1,0:T(8,128)(2,1)S(1)} %get-tuple-element.84), channel_id=1, source_target_pairs={{0,8},{16,24},{32,40},{48,56},{64,72},{80,88},{96,104},{112,120},{... | collective-permute-start | bytes 294920 | tf_op jit(solution)/shard_map/ppermute | solution.py:635
  59.3 7.1 %collective-permute-start.9 = (bf16[96,512]{1,0:T(8,128)(2,1)S(1)}, bf16[96,512]{1,0:T(8,128)(2,1)S(1)}, u32[]{:S(2)}, u32[]{:S(2)}) collective-permute-start(bf16[96,512]{1,0:T(8,128)(2,1)S(1)} %get-tuple-element.85), channel_id=1, source_target_pairs={{8,16},{24,32},{40,48},{56,64},{72,80},{88,96},{104,112},{16,8},{3... | collective-permute-start | bytes 294920 | tf_op jit(solution)/shard_map/ppermute | solution.py:636
  67.2 9.3 %collective-permute-start.10 = (bf16[336,128]{1,0:T(8,128)(2,1)S(1)}, bf16[336,128]{1,0:T(8,128)(2,1)S(1)}, u32[]{:S(2)}, u32[]{:S(2)}) collective-permute-start(bf16[336,128]{1,0:T(8,128)(2,1)S(1)} %get-tuple-element.87), channel_id=1, source_target_pairs={{0,2},{4,6},{2,0},{6,4},{1,3},{5,7},{3,1},{7,5},{8,10},{12,14},{10... | collective-permute-start | bytes 258056 | tf_op jit(solution)/shard_map/ppermute | solution.py:641
  74.7 1.9 collective-permute-start.11
  82.2 7.3 %copy-start.15 = (f32[4480,128]{1,0:T(8,128)}, f32[4480,128]{1,0:T(8,128)S(1)}, u32[]{:S(2)}) copy-start(f32[4480,128]{1,0:T(8,128)S(1)} %get-tuple-element.133.seen) | copy-start | bytes 6881284
  82.3 7.2 %copy-start.20 = (bf16[1,16,32,512]{3,2,1,0:T(8,128)(2,1)S(1)}, bf16[1,16,32,512]{3,2,1,0:T(8,128)(2,1)}, u32[]{:S(2)}) copy-start(bf16[1,16,32,512]{3,2,1,0:T(8,128)(2,1)} %param.12) | copy-start | bytes 1572868
  93.0 10.8 %copy-start = (f32[4480,128]{1,0:T(8,128)}, f32[4480,128]{1,0:T(8,128)S(1)}, u32[]{:S(2)}) copy-start(f32[4480,128]{1,0:T(8,128)S(1)} %get-tuple-element.97.slab.old.grads) | copy-start | bytes 6881284
  96.1 14.5 %copy-start.12 = (f32[2,7,7,512]{3,0,2,1:T(2,128)S(1)}, f32[2,7,7,512]{3,0,2,1:T(2,128)}, u32[]{:S(2)}) copy-start(f32[2,7,7,512]{3,0,2,1:T(2,128)} %param.13) | copy-start | bytes 602116
  96.1 30.7 %collective-permute-start.24 = (bf16[512,2048]{1,0:T(8,128)(2,1)S(1)}, bf16[512,2048]{1,0:T(8,128)(2,1)S(1)}, u32[]{:S(2)}, u32[]{:S(2)}) collective-permute-start(bf16[512,2048]{1,0:T(8,128)(2,1)S(1)} %get-tuple-element.124), channel_id=1, source_target_pairs={{0,8},{8,0},{1,9},{9,1},{2,10},{10,2},{3,11},{11,3},{4,12},{12,4},... | collective-permute-start | bytes 6291464 | tf_op jit(solution)/shard_map/ppermute | solution.py:647
  96.2 5.3 %collective-permute-start.16 = (bf16[96,512]{1,0:T(8,128)(2,1)S(1)}, bf16[96,512]{1,0:T(8,128)(2,1)S(1)}, u32[]{:S(2)}, u32[]{:S(2)}) collective-permute-start(bf16[96,512]{1,0:T(8,128)(2,1)S(1)} %get-tuple-element.98), channel_id=1, source_target_pairs={{0,8},{16,24},{32,40},{48,56},{64,72},{80,88},{96,104},{112,120},{... | collective-permute-start | bytes 294920 | tf_op jit(solution)/shard_map/ppermute | solution.py:635
  96.7 7.1 %collective-permute-start.17 = (bf16[96,512]{1,0:T(8,128)(2,1)S(1)}, bf16[96,512]{1,0:T(8,128)(2,1)S(1)}, u32[]{:S(2)}, u32[]{:S(2)}) collective-permute-start(bf16[96,512]{1,0:T(8,128)(2,1)S(1)} %get-tuple-element.99), channel_id=1, source_target_pairs={{8,16},{24,32},{40,48},{56,64},{72,80},{88,96},{104,112},{16,8},{3... | collective-permute-start | bytes 294920 | tf_op jit(solution)/shard_map/ppermute | solution.py:636
  101.5 8.4 %copy-start.21 = (bf16[96,512]{1,0:T(8,128)(2,1)}, bf16[96,512]{1,0:T(8,128)(2,1)S(1)}, u32[]{:S(2)}) copy-start(bf16[96,512]{1,0:T(8,128)(2,1)S(1)} %collective-permute-done.16.edge_near) | copy-start | bytes 294916
  104.4 5.5 %collective-permute-start.18 = (bf16[336,128]{1,0:T(8,128)(2,1)S(1)}, bf16[336,128]{1,0:T(8,128)(2,1)S(1)}, u32[]{:S(2)}, u32[]{:S(2)}) collective-permute-start(bf16[336,128]{1,0:T(8,128)(2,1)S(1)} %get-tuple-element.100), channel_id=1, source_target_pairs={{0,2},{4,6},{2,0},{6,4},{1,3},{5,7},{3,1},{7,5},{8,10},{12,14},{10... | collective-permute-start | bytes 258056 | tf_op jit(solution)/shard_map/ppermute | solution.py:641
  108.0 1.9 collective-permute-start.19
  126.8 32.6 %collective-permute-start.25 = (bf16[512,2048]{1,0:T(8,128)(2,1)}, bf16[512,2048]{1,0:T(8,128)(2,1)}, u32[]{:S(2)}, u32[]{:S(2)}) collective-permute-start(bf16[512,2048]{1,0:T(8,128)(2,1)} %get-tuple-element.129), channel_id=1, source_target_pairs={{0,8},{8,0},{1,9},{9,1},{2,10},{10,2},{3,11},{11,3},{4,12},{12,4},... | collective-permute-start | bytes 6291464 | tf_op jit(solution)/shard_map/ppermute | solution.py:647
  128.4 22.0 %copy-start.1 = (f32[4480,128]{1,0:T(8,128)S(1)}, f32[4480,128]{1,0:T(8,128)}, u32[]{:S(2)}) copy-start(f32[4480,128]{1,0:T(8,128)} %copy-done) | copy-start | bytes 6881284
  128.4 49.4 %all-to-all-start = ((bf16[64,8,2048]{2,1,0:T(8,128)(2,1)}), bf16[64,8,2048]{2,1,0:T(8,128)(2,1)}, u32[]{:S(2)}, u32[]{:S(2)}) async-start(bf16[64,8,2048]{2,1,0:T(8,128)(2,1)} %shard_map.176), calls=%async_computation | async-start | bytes 4194304 | tf_op jit(solution)/shard_map/all_to_all | solution.py:674
  177.9 37.9 %all-to-all-start.1 = ((bf16[64,8,2304]{2,1,0:T(8,128)(2,1)}), bf16[64,8,2304]{2,1,0:T(8,128)(2,1)S(1)}, u32[]{:S(2)}, u32[]{:S(2)}) async-start(bf16[64,8,2304]{2,1,0:T(8,128)(2,1)} %shard_map.181), calls=%async_computation.1 | async-start | bytes 4718592 | tf_op jit(solution)/shard_map/all_to_all | solution.py:674
  217.5 39.9 %copy-start.32 = (bf16[96,512]{1,0:T(8,128)(2,1)S(1)}, bf16[96,512]{1,0:T(8,128)(2,1)}, u32[]{:S(2)}) copy-start(bf16[96,512]{1,0:T(8,128)(2,1)} %copy-done.31) | copy-start | bytes 294916
  217.6 45.9 %copy-start.4 = (f32[4480,128]{1,0:T(8,128)S(1)}, f32[4480,128]{1,0:T(8,128)}, u32[]{:S(2)}) copy-start(f32[4480,128]{1,0:T(8,128)} %copy-done.2) | copy-start | bytes 6881284
  254.7 14.0 %copy-start.13 = (f32[2,7,7,512]{3,0,2,1:T(2,128)S(1)}, f32[2,7,7,512]{3,0,2,1:T(2,128)}, u32[]{:S(2)}) copy-start(f32[2,7,7,512]{3,0,2,1:T(2,128)} %param.13) | copy-start | bytes 602116
  254.7 25.6 %collective-permute-start.26 = (bf16[32,8,4352]{2,1,0:T(8,128)(2,1)S(1)}, bf16[32,8,4352]{2,1,0:T(8,128)(2,1)S(1)}, u32[]{:S(2)}, u32[]{:S(2)}) collective-permute-start(bf16[32,8,4352]{2,1,0:T(8,128)(2,1)S(1)} %all_to_all.15.ref.whole0.whole1), channel_id=1, source_target_pairs={{0,8},{8,0},{1,9},{9,1},{2,10},{10,2},{3,11},{11,3},{4,12},{12,4},... | collective-permute-start | bytes 6684680 | tf_op jit(solution)/shard_map/ppermute | solution.py:647
  257.5 4.1 %collective-permute-start.20 = (bf16[96,512]{1,0:T(8,128)(2,1)S(1)}, bf16[96,512]{1,0:T(8,128)(2,1)S(1)}, u32[]{:S(2)}, u32[]{:S(2)}) collective-permute-start(bf16[96,512]{1,0:T(8,128)(2,1)S(1)} %copy-done.32), channel_id=1, source_target_pairs={{0,8},{16,24},{32,40},{48,56},{64,72},{80,88},{96,104},{112,120},{... | collective-permute-start | bytes 294920 | tf_op jit(solution)/shard_map/ppermute | solution.py:635
  257.6 5.9 %collective-permute-start.21 = (bf16[96,512]{1,0:T(8,128)(2,1)S(1)}, bf16[96,512]{1,0:T(8,128)(2,1)S(1)}, u32[]{:S(2)}, u32[]{:S(2)}) collective-permute-start(bf16[96,512]{1,0:T(8,128)(2,1)S(1)} %get-tuple-element.117), channel_id=1, source_target_pairs={{8,16},{24,32},{40,48},{56,64},{72,80},{88,96},{104,112},{16,8},{3... | collective-permute-start | bytes 294920 | tf_op jit(solution)/shard_map/ppermute | solution.py:636
  264.1 3.4 %collective-permute-start.22 = (bf16[336,128]{1,0:T(8,128)(2,1)S(1)}, bf16[336,128]{1,0:T(8,128)(2,1)S(1)}, u32[]{:S(2)}, u32[]{:S(2)}) collective-permute-start(bf16[336,128]{1,0:T(8,128)(2,1)S(1)} %get-tuple-element.118), channel_id=1, source_target_pairs={{0,2},{4,6},{2,0},{6,4},{1,3},{5,7},{3,1},{7,5},{8,10},{12,14},{10... | collective-permute-start | bytes 258056 | tf_op jit(solution)/shard_map/ppermute | solution.py:641
  264.4 3.2 %collective-permute-start.23 = (bf16[336,128]{1,0:T(8,128)(2,1)S(1)}, bf16[336,128]{1,0:T(8,128)(2,1)S(1)}, u32[]{:S(2)}, u32[]{:S(2)}) collective-permute-start(bf16[336,128]{1,0:T(8,128)(2,1)S(1)} %get-tuple-element.119), channel_id=1, source_target_pairs={{2,4},{4,2},{3,5},{5,3},{10,12},{12,10},{11,13},{13,11},{18,20},{2... | collective-permute-start | bytes 258056 | tf_op jit(solution)/shard_map/ppermute | solution.py:642
  (18 other events, 53.4 us)

commit v3 on v2

--- a/solution.py
+++ b/solution.py
@@ -193,13 +193,14 @@
     store, taps, *held,
 ):
     kept = slab, normed, rstd
+    slab, sems = held[0], held[-1]
     if far:
-        slab, normed, rstd, sems = held
+        normed, rstd = held[1:3]
     one = slice(k, k + 1)
     spread(kernel, k, taps)
     slab[...] = old[...]
     put_columns(slab, place[3], near, far_side)
-    copies = [started(slab, kept[0], sems.at[0])] if far else []
+    copies = [started(slab, kept[0], sems.at[0])]
     filtered(slab, taps, store, False)
     for row in range(ROWS):
         a, b = row * COLS, (row + 1) * COLS
@@ -519,12 +520,11 @@
 def normalise(k, place, slab, near, far_side, kernel, bias, gain, shift):
     outs = [((SLAB, 128), F32), ((PIX, CH), BF16), ((PIX, CH), F32), ((PIX, 128), F32)]
     far = k == 0
-    scratch = [STORE, TAPS]
-    if far:
-        scratch += [pltpu.VMEM(*outs[n]) for n in (0, 2, 3)] + [DMA((5,))]
+    leaving = (0, 2, 3) if far else (0,)
+    scratch = [STORE, TAPS, *(pltpu.VMEM(*outs[n]) for n in leaving), DMA((5,))]
     return call(
         functools.partial(norm_body, k, far), outs, 8, 40_000_000, scratch, scalars=1,
-        grant=8 if far else 5, far_out=(0, 2, 3) if far else (),
+        grant=8, far_out=leaving,
     )(place, slab, near, far_side, kernel, bias, gain, shift)
 
 

time: 288 us -> 288 us (level)
    unnamed x74 -> x72, local copies, waits for them, and re-layouts: 6.62 us -> 6.64 us
where the time goes in v3:
time: 288 us; the launch traced here: 285 us
  Pallas kernels  83.9 us (29%)
  starting transfers between devices  77.6 us (27%)
  waiting for transfers between devices  74.6 us (26%)
  blocking collectives  37.2 us (13%)
  local copies, waits for them, and re-layouts  9.93 us (3%)
    pallas_call x21, Pallas kernels, run(): made(*(pltpu.with_memory_space_constraint(arg, pltpu.HBM) if n in far els...  76.5 us
    all_to_all x2, waiting for transfers between devices, send_grads(): return lax.all_to_all(pair, ('dp', *SPACE), 0, 0, tiled=True)  43 us
    all_to_all x1, blocking collectives, per_device(): whole = lax.all_to_all(copies, SPACE, 0, 0, tiled=True)  37.2 us
    all_to_all x2, starting transfers between devices, send_grads(): return lax.all_to_all(pair, ('dp', *SPACE), 0, 0, tiled=True)  30 us
    ppermute x4, starting transfers between devices, from_rows(): far = lax.ppermute(far, RANKS, pairs(1, 16))  15.3 us
    ppermute x4, waiting for transfers between devices, around_x(): lax.ppermute(value, ('xh', 'dp'), [(i, (i + step) % 4) for i in range(4)])  14.4 us
    ppermute x4, starting transfers between devices, from_columns(): near = lax.ppermute(near, 'z', pairs(0, 4))  13.1 us
    ppermute x7, starting transfers between devices, swapped(): return lax.ppermute(value, axis, [(0, 1), (1, 0)])  9.42 us
  transfers between devices with their start and end apart: 29, of which 13 were waited for; matrix products, arithmetic and copies ran while one was open for 0% of the time, Pallas kernels for 23%

profile of v3, /device:TPU:1, one launch (start us, length us, event | category | flops | bytes accessed | tf_op | source)
XLA Modules:
  0.0 284.6 jit_solution(1925123750069908549)
XLA Ops:
  0.7 2.4 constant_dynamic-slice_fusion.1
  3.1 2.1 collective-permute-start.4
  6.1 1.4 collective-permute-start.6
  7.6 2.5 collective-permute-start.14
  10.1 7.9 %collective-permute-done.4.refs_4_ = bf16[1,128,2048]{2,1,0:T(8,128)(2,1)} collective-permute-done((bf16[1,128,2048]{2,1,0:T(8,128)(2,1)}, bf16[1,128,2048]{2,1,0:T(8,128)(2,1)}, u32[]{:S(2)}, u32[]{:S(2)}) %collective-permute-start.4) | collective-permute-done | bytes 524320 | tf_op jit(solution)/shard_map/ppermute | solution.py:651
  18.1 2.8 collective-permute-start.5
  22.7 6.4 %collective-permute-done.12.refs_4_ = bf16[1,128,2048]{2,1,0:T(8,128)(2,1)S(1)} collective-permute-done((bf16[1,128,2048]{2,1,0:T(8,128)(2,1)}, bf16[1,128,2048]{2,1,0:T(8,128)(2,1)S(1)}, u32[]{:S(2)}, u32[]{:S(2)}) %collective-permute-start.12) | collective-permute-done | bytes 524320 | tf_op jit(solution)/shard_map/ppermute | solution.py:651
  29.2 1.6 collective-permute-start.13
  31.8 3.1 %collective-permute-start.1 = (bf16[96,512]{1,0:T(8,128)(2,1)S(1)}, bf16[96,512]{1,0:T(8,128)(2,1)S(1)}, u32[]{:S(2)}, u32[]{:S(2)}) collective-permute-start(bf16[96,512]{1,0:T(8,128)(2,1)S(1)} %get-tuple-element.78), channel_id=1, source_target_pairs={{8,16},{24,32},{40,48},{56,64},{72,80},{88,96},{104,112},{16,8},{3... | collective-permute-start | bytes 294920 | tf_op jit(solution)/shard_map/ppermute | solution.py:636
  34.9 2.8 collective-permute-done.1.edge_far
  38.6 1.7 collective-permute-start.2
  40.3 1.9 collective-permute-done.2.near
  42.9 7.2 %shard_map.164 = (f32[4480,128]{1,0:T(8,128)}, bf16[512,512]{1,0:T(8,128)(2,1)S(1)}, f32[512,512]{1,0:T(8,128)}, f32[512,128]{1,0:T(8,128)}) custom-call(s32[4]{0:T(128)S(1)} %pad_add_fusion.place.refs_0_, f32[4480,128]{1,0:T(8,128)S(1)} %get-tuple-element.79.old, bf16[336,128]{1,0:T(8,128)(2,1)S(1)} %collective-permute-done.2.near, ...), custom_call_target="tpu_custom_call" | custom-call | flops 40000000 | bytes 4000000 | tf_op jit(solution)/shard_map/pallas_call | solution.py:54
  50.1 1.6 copy-done.7
  51.7 7.4 %shard_map.165 = (bf16[512,512]{1,0:T(8,128)(2,1)S(1)}, bf16[96,512]{1,0:T(8,128)(2,1)S(1)}, bf16[96,512]{1,0:T(8,128)(2,1)S(1)}, bf16[512,2048]{1,0:T(8,128)(2,...) custom-call(s32[4]{0:T(128)S(1)} %pad_add_fusion.place.refs_0_, ...), custom_call_target="tpu_custom_call" | custom-call | flops 60000000 | bytes 4000000 | tf_op jit(solution)/shard_map/pallas_call | solution.py:54
  59.3 4.8 %collective-permute-start.9 = (bf16[96,512]{1,0:T(8,128)(2,1)S(1)}, bf16[96,512]{1,0:T(8,128)(2,1)S(1)}, u32[]{:S(2)}, u32[]{:S(2)}) collective-permute-start(bf16[96,512]{1,0:T(8,128)(2,1)S(1)} %get-tuple-element.85), channel_id=1, source_target_pairs={{8,16},{24,32},{40,48},{56,64},{72,80},{88,96},{104,112},{16,8},{3... | collective-permute-start | bytes 294920 | tf_op jit(solution)/shard_map/ppermute | solution.py:636
  64.1 2.3 collective-permute-done.9.edge_far
  67.2 7.5 %collective-permute-start.10 = (bf16[336,128]{1,0:T(8,128)(2,1)S(1)}, bf16[336,128]{1,0:T(8,128)(2,1)S(1)}, u32[]{:S(2)}, u32[]{:S(2)}) collective-permute-start(bf16[336,128]{1,0:T(8,128)(2,1)S(1)} %get-tuple-element.87), channel_id=1, source_target_pairs={{0,2},{4,6},{2,0},{6,4},{1,3},{5,7},{3,1},{7,5},{8,10},{12,14},{10... | collective-permute-start | bytes 258056 | tf_op jit(solution)/shard_map/ppermute | solution.py:641
  76.6 6.2 %shard_map.167 = (f32[4480,128]{1,0:T(8,128)}, bf16[512,512]{1,0:T(8,128)(2,1)S(1)}, f32[512,512]{1,0:T(8,128)S(1)}, f32[512,128]{1,0:T(8,128)S(1)}) custom-call(s32[4]{0:T(128)S(1)} %pad_add_fusion.place.refs_0_, f32[4480,128]{1,0:T(8,128)S(1)} %get-tuple-element.86.old, bf16[336,128]{1,0:T(8,128)(2,1)S(1)} %collective-permute-done.10.near, ...), custom_call_target="tpu_custom_call" | custom-call | flops 40000000 | bytes 4000000 | tf_op jit(solution)/shard_map/pallas_call | solution.py:54
  82.8 6.8 %shard_map.168 = (bf16[512,512]{1,0:T(8,128)(2,1)}, bf16[96,512]{1,0:T(8,128)(2,1)}, bf16[96,512]{1,0:T(8,128)(2,1)}, bf16[512,2048]{1,0:T(8,128)(2,1)S(1)}, bf1...) custom-call(s32[4]{0:T(128)S(1)} %pad_add_fusion.place.refs_0_, ...), custom_call_target="tpu_custom_call" | custom-call | flops 60000000 | bytes 4000000 | tf_op jit(solution)/shard_map/pallas_call | solution.py:54
  89.6 3.4 %shard_map.169 = (bf16[512,512]{1,0:T(8,128)(2,1)S(1)}, bf16[512,2048]{1,0:T(8,128)(2,1)S(1)}, f32[4480,128]{1,0:T(8,128)S(1)}, bf16[96,512]{1,0:T(8,128)(2,1)S(...) custom-call(s32[4]{0:T(128)S(1)} %pad_add_fusion.place.refs_0_, ...), custom_call_target="tpu_custom_call" | custom-call | flops 60000000 | bytes 4000000 | tf_op jit(solution)/shard_map/pallas_call | solution.py:54
  93.1 3.1 %shard_map.175 = (bf16[512,2048]{1,0:T(8,128)(2,1)S(1)}, bf16[512,2048]{1,0:T(8,128)(2,1)S(1)}) custom-call(s32[4]{0:T(128)S(1)} %pad_add_fusion.place.refs_0_, bf16[512,512]{1,0:T(8,128)(2,1)S(1)} %get-tuple-element.89.refs_2_.normal, bf16[512,512]{1,0:T(8,128)(2,1)S(1)} %get-tuple-element.120.low, bf16[512,2048]{1,0:T(8,128)(2,1)S(1)} %get-tuple-element.121.act, ...), custom_call_target="tpu_custom_call" | custom-call | flops 50000000 | bytes 4000000 | tf_op jit(solution)/shard_map/pallas_call | solution.py:54
  96.8 4.8 %collective-permute-start.17 = (bf16[96,512]{1,0:T(8,128)(2,1)S(1)}, bf16[96,512]{1,0:T(8,128)(2,1)S(1)}, u32[]{:S(2)}, u32[]{:S(2)}) collective-permute-start(bf16[96,512]{1,0:T(8,128)(2,1)S(1)} %get-tuple-element.99), channel_id=1, source_target_pairs={{8,16},{24,32},{40,48},{56,64},{72,80},{88,96},{104,112},{16,8},{3... | collective-permute-start | bytes 294920 | tf_op jit(solution)/shard_map/ppermute | solution.py:636
  101.6 2.3 collective-permute-done.17.edge_far
  104.5 3.6 %collective-permute-start.18 = (bf16[336,128]{1,0:T(8,128)(2,1)S(1)}, bf16[336,128]{1,0:T(8,128)(2,1)S(1)}, u32[]{:S(2)}, u32[]{:S(2)}) collective-permute-start(bf16[336,128]{1,0:T(8,128)(2,1)S(1)} %get-tuple-element.100), channel_id=1, source_target_pairs={{0,2},{4,6},{2,0},{6,4},{1,3},{5,7},{3,1},{7,5},{8,10},{12,14},{10... | collective-permute-start | bytes 258056 | tf_op jit(solution)/shard_map/ppermute | solution.py:641
  110.7 7.6 %shard_map.171 = (f32[512,512]{1,0:T(8,128)S(1)}, f32[512,512]{1,0:T(8,128)S(1)}, bf16[512,2048]{1,0:T(8,128)(2,1)S(1)}, f32[512,512]{1,0:T(8,128)S(1)}, f32[512...) custom-call(s32[4]{0:T(128)S(1)} %pad_add_fusion.place.refs_0_, ...), custom_call_target="tpu_custom_call" | custom-call | flops 40000000 | bytes 4000000 | tf_op jit(solution)/shard_map/pallas_call | solution.py:54
  118.3 3.4 %shard_map.172 = (bf16[512,512]{1,0:T(8,128)(2,1)S(1)}, bf16[512,2048]{1,0:T(8,128)(2,1)S(1)}, f32[4480,128]{1,0:T(8,128)S(1)}, bf16[96,512]{1,0:T(8,128)(2,1)S(...) custom-call(s32[4]{0:T(128)S(1)} %pad_add_fusion.place.refs_0_, ...), custom_call_target="tpu_custom_call" | custom-call | flops 60000000 | bytes 4000000 | tf_op jit(solution)/shard_map/pallas_call | solution.py:54
  121.8 3.7 %shard_map.178 = (bf16[512,2048]{1,0:T(8,128)(2,1)S(1)}, bf16[512,2048]{1,0:T(8,128)(2,1)}) custom-call(s32[4]{0:T(128)S(1)} %pad_add_fusion.place.refs_0_, bf16[512,512]{1,0:T(8,128)(2,1)S(1)} %get-tuple-element.82.refs_2_.normal, bf16[512,512]{1,0:T(8,128)(2,1)S(1)} %get-tuple-element.125.low, bf16[512,2048]{1,0:T(8,128)(2,1)S(1)} %copy-done.16, ...), custom_call_target="tpu_custom_call" | custom-call | flops 50000000 | bytes 4000000 | tf_op jit(solution)/shard_map/pallas_call | solution.py:54
  126.9 1.5 shard_map.176
  128.5 22.0 %all-to-all-start = ((bf16[64,8,2048]{2,1,0:T(8,128)(2,1)}), bf16[64,8,2048]{2,1,0:T(8,128)(2,1)}, u32[]{:S(2)}, u32[]{:S(2)}) async-start(bf16[64,8,2048]{2,1,0:T(8,128)(2,1)} %shard_map.176), calls=%async_computation | async-start | bytes 4194304 | tf_op jit(solution)/shard_map/all_to_all | solution.py:674
  150.5 1.6 copy-done.15
  152.1 3.6 %shard_map.180.refs_3_ = f32[196,128]{1,0:T(8,128)S(1)} custom-call(f32[4480,128]{1,0:T(8,128)S(1)} %copy-done.15, f32[4480,128]{1,0:T(8,128)S(1)} %copy-done.1), custom_call_target="tpu_custom_call" | custom-call | flops 40000000 | bytes 4000000 | tf_op jit(solution)/shard_map/pallas_call | solution.py:54
  155.8 3.7 %shard_map.179.refs_0_ = f32[196,128]{1,0:T(8,128)S(1)} custom-call(f32[4480,128]{1,0:T(8,128)S(1)} %copy-done.14, f32[4480,128]{1,0:T(8,128)S(1)} %copy-done.3), custom_call_target="tpu_custom_call" | custom-call | flops 40000000 | bytes 4000000 | tf_op jit(solution)/shard_map/pallas_call | solution.py:54
  159.5 3.2 %shard_map.181 = bf16[64,8,2304]{2,1,0:T(8,128)(2,1)} custom-call(bf16[512,2048]{1,0:T(8,128)(2,1)S(1)} %copy-done.18, bf16[512,2048]{1,0:T(8,128)(2,1)} %collective-permute-done.25.got, f32[196,128]{1,0:T(8,128)S(1)} %shard_map.179.refs_0_, f32[8,512]{1,0:T(8,128)S(1)} %get-tuple-element.131.refs_1_, f32[1,2048]{1,0:T(1,128)S(1)} %get-tuple-element.132.refs_2_, ...), custom_call_target="tpu_custom_call" | custom-call | flops 2000000 | bytes 4000000 | tf_op jit(solution)/shard_map/pallas_call | solution.py:54
  162.7 15.2 %all-to-all-done.pieces = bf16[64,8,2048]{2,1,0:T(8,128)(2,1)} async-done(((bf16[64,8,2048]{2,1,0:T(8,128)(2,1)}), bf16[64,8,2048]{2,1,0:T(8,128)(2,1)}, u32[]{:S(2)}, u32[]{:S(2)}) %all-to-all-start) | async-done | bytes 2097184 | tf_op jit(solution)/shard_map/all_to_all | solution.py:674
  177.9 8.0 %all-to-all-start.1 = ((bf16[64,8,2304]{2,1,0:T(8,128)(2,1)}), bf16[64,8,2304]{2,1,0:T(8,128)(2,1)S(1)}, u32[]{:S(2)}, u32[]{:S(2)}) async-start(bf16[64,8,2304]{2,1,0:T(8,128)(2,1)} %shard_map.181), calls=%async_computation.1 | async-start | bytes 4718592 | tf_op jit(solution)/shard_map/all_to_all | solution.py:674
  185.9 2.1 shard_map.177.other
  188.0 27.8 %all-to-all-done.1.pieces = bf16[64,8,2304]{2,1,0:T(8,128)(2,1)S(1)} async-done(((bf16[64,8,2304]{2,1,0:T(8,128)(2,1)}), bf16[64,8,2304]{2,1,0:T(8,128)(2,1)S(1)}, u32[]{:S(2)}, u32[]{:S(2)}) %all-to-all-start.1) | async-done | bytes 2359328 | tf_op jit(solution)/shard_map/all_to_all | solution.py:674
  215.8 1.8 shard_map.182
  217.6 37.2 %all_to_all.15.ref.whole0.whole1 = bf16[32,8,4352]{2,1,0:T(8,128)(2,1)S(1)} all-to-all(bf16[32,8,4352]{2,1,0:T(8,128)(2,1)} %shard_map.182), channel_id=1, replica_groups=mesh['xh'=2,'y'=4,'core'=2,'z'=4,'dp'=2] {'xh','y','z'}, dimensions={0} | all-to-all | bytes 4456448 | tf_op jit(solution)/shard_map/all_to_all | solution.py:736
  254.8 2.7 collective-permute-start.26
  257.6 2.5 collective-permute-start.21
  260.1 1.5 collective-permute-done.20.edge_near
  261.6 1.9 collective-permute-done.21.edge_far
  265.1 2.5 collective-permute-done.22.near
  268.8 8.3 %shard_map.174 = bf16[512,512]{1,0:T(8,128)(2,1)} custom-call(s32[4]{0:T(128)S(1)} %pad_add_fusion.place.refs_0_, f32[4480,128]{1,0:T(8,128)} %copy-done.2, bf16[96,512]{1,0:T(8,128)(2,1)} %copy-done.22, bf16[96,512]{1,0:T(8,128)(2,1)} %copy-done.23, bf16[336,128]{1,0:T(8,128)(2,1)} %copy-done.34, bf16[336,128]{1,0:T(8,128)(2,1)} %copy-done.35, ...), custom_call_target="tpu_custom_call" | custom-call | flops 40000000 | bytes 4000000 | tf_op jit(solution)/shard_map/pallas_call | solution.py:54
  277.2 3.3 %shard_map.183 = (f32[2,256,2048]{2,1,0:T(8,128)}, f32[2,2048,256]{2,1,0:T(8,128)}) custom-call(s32[4]{0:T(128)S(1)} %pad_add_fusion.place.refs_0_, bf16[32,8,4352]{2,1,0:T(8,128)(2,1)S(1)} %all_to_all.15.ref.whole0.whole1), custom_call_target="tpu_custom_call" | custom-call | flops 5000000 | bytes 6000000 | tf_op jit(solution)/shard_map/pallas_call | solution.py:581
  281.3 3.3 %shard_map.184 = (f32[2,256,2048]{2,1,0:T(8,128)}, f32[2,2048,256]{2,1,0:T(8,128)}) custom-call(s32[4]{0:T(128)S(1)} %pad_add_fusion.place.refs_0_, bf16[32,8,4352]{2,1,0:T(8,128)(2,1)S(1)} %collective-permute-done.26.ref.mate0.mate1, f32[2,256,2048]{2,1,0:T(8,128)} %get-tuple-element.136.refs_0_, ...), custom_call_target="tpu_custom_call", output_to_operand_aliasing={{0}: (2, {}), {1}: (3, {})} | custom-call | flops 5000000 | bytes 6000000 | tf_op jit(solution)/shard_map/pallas_call | solution.py:581
  (110 shorter events, 17.1 us)
Async XLA Ops:
  0.6 21.4 %copy-start.9 = (bf16[1,16,32,512]{3,2,1,0:T(8,128)(2,1)S(1)}, bf16[1,16,32,512]{3,2,1,0:T(8,128)(2,1)}, u32[]{:S(2)}) copy-start(bf16[1,16,32,512]{3,2,1,0:T(8,128)(2,1)} %param.11) | copy-start | bytes 1572868
  3.1 39.8 %copy-start.11 = (f32[2,7,7,512]{3,0,2,1:T(2,128)S(1)}, f32[2,7,7,512]{3,0,2,1:T(2,128)}, u32[]{:S(2)}) copy-start(f32[2,7,7,512]{3,0,2,1:T(2,128)} %param.13) | copy-start | bytes 602116
  3.1 39.8 %copy-start.25 = (f32[2,512]{1,0:T(2,128)S(1)}, f32[2,512]{1,0:T(2,128)}, u32[]{:S(2)}) copy-start(f32[2,512]{1,0:T(2,128)} %gain.7) | copy-start | bytes 12292
  3.1 39.8 %copy-start.27 = (f32[2,512]{1,0:T(2,128)S(1)}, f32[2,512]{1,0:T(2,128)}, u32[]{:S(2)}) copy-start(f32[2,512]{1,0:T(2,128)} %bias.3) | copy-start | bytes 12292
  3.1 39.8 %copy-start.28 = (f32[2,512]{1,0:T(2,128)S(1)}, f32[2,512]{1,0:T(2,128)}, u32[]{:S(2)}) copy-start(f32[2,512]{1,0:T(2,128)} %shift.3) | copy-start | bytes 12292
  3.1 14.9 %collective-permute-start.4 = (bf16[1,128,2048]{2,1,0:T(8,128)(2,1)}, bf16[1,128,2048]{2,1,0:T(8,128)(2,1)}, u32[]{:S(2)}, u32[]{:S(2)}) collective-permute-start(bf16[1,128,2048]{2,1,0:T(8,128)(2,1)} %get-tuple-element.146), channel_id=1, source_target_pairs={{0,1},{1,64},{64,65},{65,0},{2,3},{3,66},{66,67},{67,2},{4,5},{5,6... | collective-permute-start | bytes 1572872 | tf_op jit(solution)/shard_map/ppermute | solution.py:651
  6.1 44.0 %copy-start.5 = (bf16[2,256,2048]{2,1,0:T(8,128)(2,1)S(1)}, bf16[2,256,2048]{2,1,0:T(8,128)(2,1)}, u32[]{:S(2)}) copy-start(bf16[2,256,2048]{2,1,0:T(8,128)(2,1)} %refs_3_.3) | copy-start | bytes 6291460
  6.1 44.0 %copy-start.24 = (f32[2,2048]{1,0:T(2,128)S(1)}, f32[2,2048]{1,0:T(2,128)}, u32[]{:S(2)}) copy-start(f32[2,2048]{1,0:T(2,128)} %refs_9_.3) | copy-start | bytes 49156
  6.1 44.0 %copy-start.26 = (f32[2,512]{1,0:T(2,128)S(1)}, f32[2,512]{1,0:T(2,128)}, u32[]{:S(2)}) copy-start(f32[2,512]{1,0:T(2,128)} %scale.3) | copy-start | bytes 12292
  6.1 44.1 %copy-start.29 = (f32[2,512]{1,0:T(2,128)S(1)}, f32[2,512]{1,0:T(2,128)}, u32[]{:S(2)}) copy-start(f32[2,512]{1,0:T(2,128)} %refs_10_.3) | copy-start | bytes 12292
  6.1 14.8 %collective-permute-start.6 = (bf16[1,1024,256]{2,1,0:T(8,128)(2,1)S(1)}, bf16[1,1024,256]{2,1,0:T(8,128)(2,1)}, u32[]{:S(2)}, u32[]{:S(2)}) collective-permute-start(bf16[1,1024,256]{2,1,0:T(8,128)(2,1)S(1)} %get-tuple-element.144), channel_id=1, source_target_pairs={{0,65},{1,0},{64,1},{65,64},{2,67},{3,2},{66,3},{67,66},{4,69},{5,... | collective-permute-start | bytes 1572872 | tf_op jit(solution)/shard_map/ppermute | solution.py:651
  7.4 21.7 %collective-permute-start.12 = (bf16[1,128,2048]{2,1,0:T(8,128)(2,1)}, bf16[1,128,2048]{2,1,0:T(8,128)(2,1)S(1)}, u32[]{:S(2)}, u32[]{:S(2)}) collective-permute-start(bf16[1,128,2048]{2,1,0:T(8,128)(2,1)} %get-tuple-element.145), channel_id=1, source_target_pairs={{0,1},{1,64},{64,65},{65,0},{2,3},{3,66},{66,67},{67,2},{4,5},{5,6... | collective-permute-start | bytes 1572872 | tf_op jit(solution)/shard_map/ppermute | solution.py:651
  7.6 23.2 %collective-permute-start.14 = (bf16[1,1024,256]{2,1,0:T(8,128)(2,1)}, bf16[1,1024,256]{2,1,0:T(8,128)(2,1)}, u32[]{:S(2)}, u32[]{:S(2)}) collective-permute-start(bf16[1,1024,256]{2,1,0:T(8,128)(2,1)} %get-tuple-element.143), channel_id=1, source_target_pairs={{0,65},{1,0},{64,1},{65,64},{2,67},{3,2},{66,3},{67,66},{4,69},{5,... | collective-permute-start | bytes 1572872 | tf_op jit(solution)/shard_map/ppermute | solution.py:651
  18.1 32.0 %collective-permute-start.5 = (bf16[1,128,2048]{2,1,0:T(8,128)(2,1)}, bf16[1,128,2048]{2,1,0:T(8,128)(2,1)}, u32[]{:S(2)}, u32[]{:S(2)}) collective-permute-start(bf16[1,128,2048]{2,1,0:T(8,128)(2,1)} %collective-permute-done.4.refs_4_), channel_id=1, source_target_pairs={{0,8},{8,0},{1,9},{9,1},{2,10},{10,2},{3,11},{11,3},{4,12},{12,4},... | collective-permute-start | bytes 1572872 | tf_op jit(solution)/shard_map/ppermute | solution.py:647
  20.9 29.2 %collective-permute-start.7 = (bf16[1,1024,256]{2,1,0:T(8,128)(2,1)}, bf16[1,1024,256]{2,1,0:T(8,128)(2,1)}, u32[]{:S(2)}, u32[]{:S(2)}) collective-permute-start(bf16[1,1024,256]{2,1,0:T(8,128)(2,1)} %collective-permute-done.6.refs_7_), channel_id=1, source_target_pairs={{0,8},{8,0},{1,9},{9,1},{2,10},{10,2},{3,11},{11,3},{4,12},{12,4},... | collective-permute-start | bytes 1572872 | tf_op jit(solution)/shard_map/ppermute | solution.py:647
  22.7 9.2 %collective-permute-start = (bf16[96,512]{1,0:T(8,128)(2,1)S(1)}, bf16[96,512]{1,0:T(8,128)(2,1)S(1)}, u32[]{:S(2)}, u32[]{:S(2)}) collective-permute-start(bf16[96,512]{1,0:T(8,128)(2,1)S(1)} %get-tuple-element.77), channel_id=1, source_target_pairs={{0,8},{16,24},{32,40},{48,56},{64,72},{80,88},{96,104},{112,120},{... | collective-permute-start | bytes 294920 | tf_op jit(solution)/shard_map/ppermute | solution.py:635
  29.2 53.6 %collective-permute-start.13 = (bf16[1,128,2048]{2,1,0:T(8,128)(2,1)S(1)}, bf16[1,128,2048]{2,1,0:T(8,128)(2,1)S(1)}, u32[]{:S(2)}, u32[]{:S(2)}) collective-permute-start(bf16[1,128,2048]{2,1,0:T(8,128)(2,1)S(1)} %collective-permute-done.12.refs_4_), channel_id=1, source_target_pairs={{0,8},{8,0},{1,9},{9,1},{2,10},{10,2},{3,11},{11,3},{4,12},{12,4},... | collective-permute-start | bytes 1572872 | tf_op jit(solution)/shard_map/ppermute | solution.py:647
  30.8 52.0 %collective-permute-start.15 = (bf16[1,1024,256]{2,1,0:T(8,128)(2,1)}, bf16[1,1024,256]{2,1,0:T(8,128)(2,1)S(1)}, u32[]{:S(2)}, u32[]{:S(2)}) collective-permute-start(bf16[1,1024,256]{2,1,0:T(8,128)(2,1)} %collective-permute-done.14.refs_7_), channel_id=1, source_target_pairs={{0,8},{8,0},{1,9},{9,1},{2,10},{10,2},{3,11},{11,3},{4,12},{12,4},... | collective-permute-start | bytes 1572872 | tf_op jit(solution)/shard_map/ppermute | solution.py:647
  31.8 5.9 %collective-permute-start.1 = (bf16[96,512]{1,0:T(8,128)(2,1)S(1)}, bf16[96,512]{1,0:T(8,128)(2,1)S(1)}, u32[]{:S(2)}, u32[]{:S(2)}) collective-permute-start(bf16[96,512]{1,0:T(8,128)(2,1)S(1)} %get-tuple-element.78), channel_id=1, source_target_pairs={{8,16},{24,32},{40,48},{56,64},{72,80},{88,96},{104,112},{16,8},{3... | collective-permute-start | bytes 294920 | tf_op jit(solution)/shard_map/ppermute | solution.py:636
  38.6 3.6 %collective-permute-start.2 = (bf16[336,128]{1,0:T(8,128)(2,1)S(1)}, bf16[336,128]{1,0:T(8,128)(2,1)S(1)}, u32[]{:S(2)}, u32[]{:S(2)}) collective-permute-start(bf16[336,128]{1,0:T(8,128)(2,1)S(1)} %get-tuple-element.80), channel_id=1, source_target_pairs={{0,2},{4,6},{2,0},{6,4},{1,3},{5,7},{3,1},{7,5},{8,10},{12,14},{10... | collective-permute-start | bytes 258056 | tf_op jit(solution)/shard_map/ppermute | solution.py:641
  42.2 0.7 collective-permute-start.3
  59.2 23.7 %copy-start.8 = (bf16[2,2048,256]{2,1,0:T(8,128)(2,1)S(1)}, bf16[2,2048,256]{2,1,0:T(8,128)(2,1)}, u32[]{:S(2)}) copy-start(bf16[2,2048,256]{2,1,0:T(8,128)(2,1)} %refs_6_.3) | copy-start | bytes 6291460
  59.2 4.9 %collective-permute-start.8 = (bf16[96,512]{1,0:T(8,128)(2,1)S(1)}, bf16[96,512]{1,0:T(8,128)(2,1)S(1)}, u32[]{:S(2)}, u32[]{:S(2)}) collective-permute-start(bf16[96,512]{1,0:T(8,128)(2,1)S(1)} %get-tuple-element.84), channel_id=1, source_target_pairs={{0,8},{16,24},{32,40},{48,56},{64,72},{80,88},{96,104},{112,120},{... | collective-permute-start | bytes 294920 | tf_op jit(solution)/shard_map/ppermute | solution.py:635
  59.3 7.1 %collective-permute-start.9 = (bf16[96,512]{1,0:T(8,128)(2,1)S(1)}, bf16[96,512]{1,0:T(8,128)(2,1)S(1)}, u32[]{:S(2)}, u32[]{:S(2)}) collective-permute-start(bf16[96,512]{1,0:T(8,128)(2,1)S(1)} %get-tuple-element.85), channel_id=1, source_target_pairs={{8,16},{24,32},{40,48},{56,64},{72,80},{88,96},{104,112},{16,8},{3... | collective-permute-start | bytes 294920 | tf_op jit(solution)/shard_map/ppermute | solution.py:636
  67.2 9.3 %collective-permute-start.10 = (bf16[336,128]{1,0:T(8,128)(2,1)S(1)}, bf16[336,128]{1,0:T(8,128)(2,1)S(1)}, u32[]{:S(2)}, u32[]{:S(2)}) collective-permute-start(bf16[336,128]{1,0:T(8,128)(2,1)S(1)} %get-tuple-element.87), channel_id=1, source_target_pairs={{0,2},{4,6},{2,0},{6,4},{1,3},{5,7},{3,1},{7,5},{8,10},{12,14},{10... | collective-permute-start | bytes 258056 | tf_op jit(solution)/shard_map/ppermute | solution.py:641
  74.7 1.9 collective-permute-start.11
  82.8 6.8 %copy-start.19 = (bf16[1,16,32,512]{3,2,1,0:T(8,128)(2,1)S(1)}, bf16[1,16,32,512]{3,2,1,0:T(8,128)(2,1)}, u32[]{:S(2)}) copy-start(bf16[1,16,32,512]{3,2,1,0:T(8,128)(2,1)} %param.12) | copy-start | bytes 1572868
  93.1 10.8 %copy-start = (f32[4480,128]{1,0:T(8,128)}, f32[4480,128]{1,0:T(8,128)S(1)}, u32[]{:S(2)}) copy-start(f32[4480,128]{1,0:T(8,128)S(1)} %get-tuple-element.97.slab.old.grads) | copy-start | bytes 6881284
  96.2 14.5 %copy-start.12 = (f32[2,7,7,512]{3,0,2,1:T(2,128)S(1)}, f32[2,7,7,512]{3,0,2,1:T(2,128)}, u32[]{:S(2)}) copy-start(f32[2,7,7,512]{3,0,2,1:T(2,128)} %param.13) | copy-start | bytes 602116
  96.2 30.7 %collective-permute-start.24 = (bf16[512,2048]{1,0:T(8,128)(2,1)S(1)}, bf16[512,2048]{1,0:T(8,128)(2,1)S(1)}, u32[]{:S(2)}, u32[]{:S(2)}) collective-permute-start(bf16[512,2048]{1,0:T(8,128)(2,1)S(1)} %get-tuple-element.124), channel_id=1, source_target_pairs={{0,8},{8,0},{1,9},{9,1},{2,10},{10,2},{3,11},{11,3},{4,12},{12,4},... | collective-permute-start | bytes 6291464 | tf_op jit(solution)/shard_map/ppermute | solution.py:647
  96.3 5.3 %collective-permute-start.16 = (bf16[96,512]{1,0:T(8,128)(2,1)S(1)}, bf16[96,512]{1,0:T(8,128)(2,1)S(1)}, u32[]{:S(2)}, u32[]{:S(2)}) collective-permute-start(bf16[96,512]{1,0:T(8,128)(2,1)S(1)} %get-tuple-element.98), channel_id=1, source_target_pairs={{0,8},{16,24},{32,40},{48,56},{64,72},{80,88},{96,104},{112,120},{... | collective-permute-start | bytes 294920 | tf_op jit(solution)/shard_map/ppermute | solution.py:635
  96.8 7.1 %collective-permute-start.17 = (bf16[96,512]{1,0:T(8,128)(2,1)S(1)}, bf16[96,512]{1,0:T(8,128)(2,1)S(1)}, u32[]{:S(2)}, u32[]{:S(2)}) collective-permute-start(bf16[96,512]{1,0:T(8,128)(2,1)S(1)} %get-tuple-element.99), channel_id=1, source_target_pairs={{8,16},{24,32},{40,48},{56,64},{72,80},{88,96},{104,112},{16,8},{3... | collective-permute-start | bytes 294920 | tf_op jit(solution)/shard_map/ppermute | solution.py:636
  101.6 8.4 %copy-start.20 = (bf16[96,512]{1,0:T(8,128)(2,1)}, bf16[96,512]{1,0:T(8,128)(2,1)S(1)}, u32[]{:S(2)}) copy-start(bf16[96,512]{1,0:T(8,128)(2,1)S(1)} %collective-permute-done.16.edge_near) | copy-start | bytes 294916
  103.9 6.1 %copy-start.21 = (bf16[96,512]{1,0:T(8,128)(2,1)}, bf16[96,512]{1,0:T(8,128)(2,1)S(1)}, u32[]{:S(2)}) copy-start(bf16[96,512]{1,0:T(8,128)(2,1)S(1)} %collective-permute-done.17.edge_far) | copy-start | bytes 294916
  104.5 5.5 %collective-permute-start.18 = (bf16[336,128]{1,0:T(8,128)(2,1)S(1)}, bf16[336,128]{1,0:T(8,128)(2,1)S(1)}, u32[]{:S(2)}, u32[]{:S(2)}) collective-permute-start(bf16[336,128]{1,0:T(8,128)(2,1)S(1)} %get-tuple-element.100), channel_id=1, source_target_pairs={{0,2},{4,6},{2,0},{6,4},{1,3},{5,7},{3,1},{7,5},{8,10},{12,14},{10... | collective-permute-start | bytes 258056 | tf_op jit(solution)/shard_map/ppermute | solution.py:641
  108.1 1.9 collective-permute-start.19
  126.9 32.6 %collective-permute-start.25 = (bf16[512,2048]{1,0:T(8,128)(2,1)}, bf16[512,2048]{1,0:T(8,128)(2,1)}, u32[]{:S(2)}, u32[]{:S(2)}) collective-permute-start(bf16[512,2048]{1,0:T(8,128)(2,1)} %get-tuple-element.129), channel_id=1, source_target_pairs={{0,8},{8,0},{1,9},{9,1},{2,10},{10,2},{3,11},{11,3},{4,12},{12,4},... | collective-permute-start | bytes 6291464 | tf_op jit(solution)/shard_map/ppermute | solution.py:647
  128.5 22.0 %copy-start.1 = (f32[4480,128]{1,0:T(8,128)S(1)}, f32[4480,128]{1,0:T(8,128)}, u32[]{:S(2)}) copy-start(f32[4480,128]{1,0:T(8,128)} %copy-done) | copy-start | bytes 6881284
  128.5 49.4 %all-to-all-start = ((bf16[64,8,2048]{2,1,0:T(8,128)(2,1)}), bf16[64,8,2048]{2,1,0:T(8,128)(2,1)}, u32[]{:S(2)}, u32[]{:S(2)}) async-start(bf16[64,8,2048]{2,1,0:T(8,128)(2,1)} %shard_map.176), calls=%async_computation | async-start | bytes 4194304 | tf_op jit(solution)/shard_map/all_to_all | solution.py:674
  177.9 37.9 %all-to-all-start.1 = ((bf16[64,8,2304]{2,1,0:T(8,128)(2,1)}), bf16[64,8,2304]{2,1,0:T(8,128)(2,1)S(1)}, u32[]{:S(2)}, u32[]{:S(2)}) async-start(bf16[64,8,2304]{2,1,0:T(8,128)(2,1)} %shard_map.181), calls=%async_computation.1 | async-start | bytes 4718592 | tf_op jit(solution)/shard_map/all_to_all | solution.py:674
  217.6 39.9 %copy-start.31 = (bf16[96,512]{1,0:T(8,128)(2,1)S(1)}, bf16[96,512]{1,0:T(8,128)(2,1)}, u32[]{:S(2)}) copy-start(bf16[96,512]{1,0:T(8,128)(2,1)} %copy-done.30) | copy-start | bytes 294916
  217.6 45.9 %copy-start.4 = (f32[4480,128]{1,0:T(8,128)S(1)}, f32[4480,128]{1,0:T(8,128)}, u32[]{:S(2)}) copy-start(f32[4480,128]{1,0:T(8,128)} %copy-done.2) | copy-start | bytes 6881284
  254.8 14.1 %copy-start.13 = (f32[2,7,7,512]{3,0,2,1:T(2,128)S(1)}, f32[2,7,7,512]{3,0,2,1:T(2,128)}, u32[]{:S(2)}) copy-start(f32[2,7,7,512]{3,0,2,1:T(2,128)} %param.13) | copy-start | bytes 602116
  254.8 25.7 %collective-permute-start.26 = (bf16[32,8,4352]{2,1,0:T(8,128)(2,1)S(1)}, bf16[32,8,4352]{2,1,0:T(8,128)(2,1)S(1)}, u32[]{:S(2)}, u32[]{:S(2)}) collective-permute-start(bf16[32,8,4352]{2,1,0:T(8,128)(2,1)S(1)} %all_to_all.15.ref.whole0.whole1), channel_id=1, source_target_pairs={{0,8},{8,0},{1,9},{9,1},{2,10},{10,2},{3,11},{11,3},{4,12},{12,4},... | collective-permute-start | bytes 6684680 | tf_op jit(solution)/shard_map/ppermute | solution.py:647
  257.5 4.1 %collective-permute-start.20 = (bf16[96,512]{1,0:T(8,128)(2,1)S(1)}, bf16[96,512]{1,0:T(8,128)(2,1)S(1)}, u32[]{:S(2)}, u32[]{:S(2)}) collective-permute-start(bf16[96,512]{1,0:T(8,128)(2,1)S(1)} %copy-done.31), channel_id=1, source_target_pairs={{0,8},{16,24},{32,40},{48,56},{64,72},{80,88},{96,104},{112,120},{... | collective-permute-start | bytes 294920 | tf_op jit(solution)/shard_map/ppermute | solution.py:635
  257.6 5.9 %collective-permute-start.21 = (bf16[96,512]{1,0:T(8,128)(2,1)S(1)}, bf16[96,512]{1,0:T(8,128)(2,1)S(1)}, u32[]{:S(2)}, u32[]{:S(2)}) collective-permute-start(bf16[96,512]{1,0:T(8,128)(2,1)S(1)} %get-tuple-element.117), channel_id=1, source_target_pairs={{8,16},{24,32},{40,48},{56,64},{72,80},{88,96},{104,112},{16,8},{3... | collective-permute-start | bytes 294920 | tf_op jit(solution)/shard_map/ppermute | solution.py:636
  264.1 3.4 %collective-permute-start.22 = (bf16[336,128]{1,0:T(8,128)(2,1)S(1)}, bf16[336,128]{1,0:T(8,128)(2,1)S(1)}, u32[]{:S(2)}, u32[]{:S(2)}) collective-permute-start(bf16[336,128]{1,0:T(8,128)(2,1)S(1)} %get-tuple-element.118), channel_id=1, source_target_pairs={{0,2},{4,6},{2,0},{6,4},{1,3},{5,7},{3,1},{7,5},{8,10},{12,14},{10... | collective-permute-start | bytes 258056 | tf_op jit(solution)/shard_map/ppermute | solution.py:641
  264.4 3.2 %collective-permute-start.23 = (bf16[336,128]{1,0:T(8,128)(2,1)S(1)}, bf16[336,128]{1,0:T(8,128)(2,1)S(1)}, u32[]{:S(2)}, u32[]{:S(2)}) collective-permute-start(bf16[336,128]{1,0:T(8,128)(2,1)S(1)} %get-tuple-element.119), channel_id=1, source_target_pairs={{2,4},{4,2},{3,5},{5,3},{10,12},{12,10},{11,13},{13,11},{18,20},{2... | collective-permute-start | bytes 258056 | tf_op jit(solution)/shard_map/ppermute | solution.py:642
  (17 other events, 47.3 us)
